TPU v7x, 32 devices: a whole 2x2x4 slice. The times are simulated.
32 devices in a mesh: head: 2 (over x), blk: 16 (over z, y, core).
Axes of the slice: x: 2, y: 2, z: 4, core: 2. Of those that a mesh axis runs over, the one named last changes fastest.
Arguments:
- hidden: bfloat16 [2, 2048, 1024], P(None, ('head', 'blk')), may hold values from -3 to 3
- pos_ids: int32 [2, 2048], P(None, ('head', 'blk')), may hold values from 0 to 8191
- type_ids: int32 [2, 2048], P(None, ('head', 'blk')), may hold values from 0 to 1, as said below
- cotangent: bfloat16 [2, 2048, 1024], P(None, ('head', 'blk')), may hold values from -6 to 6
- pos_table: bfloat16 [8192, 1024], P('blk'), may hold values from -4 to 4
- type_table: bfloat16 [2, 1024], P(None, 'blk'), may hold values from -4 to 4
- query_key_value_weight: bfloat16 [1024, 3072], P('blk'), may hold values from -0.1875 to 0.1875
- attention_output_weight: bfloat16 [1024, 1024], P('blk'), may hold values from -6 to 6
- up_projection_weight: bfloat16 [1024, 4096], P('blk'), may hold values from -0.1875 to 0.1875
- down_projection_weight: bfloat16 [4096, 1024], P('blk'), may hold values from -0.09375 to 0.09375
- up_projection_bias: bfloat16 [4096], P('blk'), may hold values from -4 to 4
- norm_gains: bfloat16 [2, 1024], P(None, 'blk'), may hold values from 0.5 to 1.5
- biases: bfloat16 [6, 1024], P(None, 'blk'), may hold values from -4 to 4
Outputs:
- layer_out: bfloat16 [2, 2048, 1024], P(None, ('head', 'blk'))
- grad_hidden: float32 [2, 2048, 1024], P(None, ('head', 'blk'))
- grad_pos_table: float32 [8192, 1024], P('blk')
- grad_type_table: float32 [2, 1024], P(None, 'blk')
- grad_qkv_weight: float32 [1024, 3072], P('blk')
- grad_out_weight: float32 [1024, 1024], P('blk')
- grad_up_weight: float32 [1024, 4096], P('blk')
- grad_down_weight: float32 [4096, 1024], P('blk')
- grad_up_bias: float32 [4096], P('blk')
- grad_norm_gains: float32 [2, 1024], P(None, 'blk')
- grad_biases: float32 [6, 1024], P(None, 'blk')
Inputs may be any that keep to these rules, and one draw needn't show every extreme that they name: `type_ids`: in each sequence the ids are 0 up to some token and 1 from it on, both present.
All inputs are finite; a program needn't handle non-finite values.
Results may differ from a plain program's by a relative error of at most 0.03.
Values may be sent and summed in bfloat16 or wider, within the bound.
A program may use at most 256 MiB of HBM per device.

v0:
```python
import math

import jax
import jax.numpy as jnp
from jax import lax
from jax.sharding import PartitionSpec as P

HEADS = 16


def norm_layer(values_in, gain_row, offset_row):
    average = jnp.mean(values_in, axis=-1, keepdims=True)
    centred = values_in - average
    variance = jnp.mean(centred * centred, axis=-1, keepdims=True)
    return centred * lax.rsqrt(variance + 1e-12) * gain_row + offset_row


def gelu_exact(inner_product_sum):
    return jax.nn.gelu(inner_product_sum, approximate=False)


def widest_block(length, limit):
    return max(
        (candidate for candidate in range(1, min(length, limit) + 1) if length % candidate == 0)
    )


def block_scores(query_heads, key_block, score_scale):
    return (
        jnp.einsum("sqhe,skhe->shqk", query_heads, key_block, preferred_element_type=jnp.float32)
        * score_scale
    )


def key_side(query_block, grad_block, lse_block, delta_block, key_heads, value_heads, score_scale):
    scores = block_scores(query_block, key_heads, score_scale)
    weights = jnp.exp(scores - lse_block[..., None])
    more_values = jnp.einsum(
        "shqk,sqhe->shke",
        weights.astype(jnp.bfloat16),
        grad_block,
        preferred_element_type=jnp.float32,
    )
    grad_weights = jnp.einsum(
        "sqhe,skhe->shqk", grad_block, value_heads, preferred_element_type=jnp.float32
    )
    grad_scores = weights * (grad_weights - delta_block[..., None])
    more_keys = jnp.einsum(
        "shqk,sqhe->shke",
        grad_scores.astype(jnp.bfloat16),
        query_block,
        preferred_element_type=jnp.float32,
    )
    return (more_keys, more_values)


def forward_fold(query_heads, score_scale, head_count, head_size):

    def fold_keys(running, portion, offset):
        key_piece, value_piece = portion
        seq_count, length = (key_piece.shape[0], key_piece.shape[1])
        block_size = widest_block(length, 512)

        def one_step(block_index, carried):
            row_peak, row_total, weighted = carried
            row_start = block_index * block_size
            key_block = lax.dynamic_slice_in_dim(key_piece, row_start, block_size, 1).reshape(
                seq_count, block_size, head_count, head_size
            )
            value_block = lax.dynamic_slice_in_dim(value_piece, row_start, block_size, 1).reshape(
                seq_count, block_size, head_count, head_size
            )
            scores = block_scores(query_heads, key_block, score_scale)
            new_peak = jnp.maximum(row_peak, jnp.max(scores, axis=-1))
            shrink = jnp.exp(row_peak - new_peak)
            weights = jnp.exp(scores - new_peak[..., None])
            row_total = row_total * shrink + jnp.sum(weights, axis=-1)
            weighted = weighted * shrink[..., None] + jnp.einsum(
                "shqk,skhe->shqe",
                weights.astype(jnp.bfloat16),
                value_block,
                preferred_element_type=jnp.float32,
            )
            return (new_peak, row_total, weighted)

        return lax.fori_loop(0, length // block_size, one_step, running)

    return fold_keys


def query_fold(query_heads, grad_heads, log_totals, delta_rows, score_scale, head_count, head_size):

    def fold_keys(running, portion, offset):
        key_piece, value_piece = portion
        seq_count, length = (key_piece.shape[0], key_piece.shape[1])
        block_size = widest_block(length, 512)

        def one_step(block_index, weighted):
            row_start = block_index * block_size
            key_block = lax.dynamic_slice_in_dim(key_piece, row_start, block_size, 1).reshape(
                seq_count, block_size, head_count, head_size
            )
            value_block = lax.dynamic_slice_in_dim(value_piece, row_start, block_size, 1).reshape(
                seq_count, block_size, head_count, head_size
            )
            scores = block_scores(query_heads, key_block, score_scale)
            weights = jnp.exp(scores - log_totals[..., None])
            grad_weights = jnp.einsum(
                "sqhe,skhe->shqk", grad_heads, value_block, preferred_element_type=jnp.float32
            )
            grad_scores = weights * (grad_weights - delta_rows[..., None])
            return weighted + jnp.einsum(
                "shqk,skhe->shqe",
                grad_scores.astype(jnp.bfloat16),
                key_block,
                preferred_element_type=jnp.float32,
            )

        return lax.fori_loop(0, length // block_size, one_step, running)

    return fold_keys


def key_fold(key_heads, value_heads, score_scale, head_count, head_size):

    def fold_queries(running, portion, offset):
        query_piece, grad_piece, lse_piece, delta_piece = portion
        seq_count, length = (query_piece.shape[0], query_piece.shape[1])
        block_size = widest_block(length, 512)

        def one_step(block_index, carried):
            grad_keys, grad_values = carried
            row_start = block_index * block_size
            query_block = lax.dynamic_slice_in_dim(query_piece, row_start, block_size, 1).reshape(
                seq_count, block_size, head_count, head_size
            )
            grad_block = lax.dynamic_slice_in_dim(grad_piece, row_start, block_size, 1).reshape(
                seq_count, block_size, head_count, head_size
            )
            lse_block = lax.dynamic_slice_in_dim(lse_piece, row_start, block_size, 1).transpose(
                0, 2, 1
            )
            delta_block = lax.dynamic_slice_in_dim(delta_piece, row_start, block_size, 1).transpose(
                0, 2, 1
            )
            more_keys, more_values = key_side(
                query_block, grad_block, lse_block, delta_block, key_heads, value_heads, score_scale
            )
            return (grad_keys + more_keys, grad_values + more_values)

        return lax.fori_loop(0, length // block_size, one_step, running)

    return fold_queries


def on_device(
    hidden,
    pos_ids,
    type_ids,
    cotangent,
    pos_table,
    type_table,
    query_key_value_weight,
    attention_output_weight,
    up_projection_weight,
    down_projection_weight,
    up_projection_bias,
    norm_gains,
    biases,
):
    seq_count, seg_tokens, model_width = hidden.shape
    row_count = seq_count * seg_tokens
    head_count = HEADS // lax.axis_size("head")
    head_size = model_width // HEADS
    local_width = head_count * head_size
    query_rows = lax.axis_size("head") * seg_tokens
    score_scale = 1.0 / math.sqrt(head_size)

    def fetch_weights():
        return (
            lax.all_gather(query_key_value_weight, "blk", axis=0, tiled=True),
            lax.all_gather(attention_output_weight, "blk", axis=0, tiled=True),
            lax.all_gather(up_projection_weight, "blk", axis=0, tiled=True),
            lax.all_gather(down_projection_weight, "blk", axis=0, tiled=True),
            lax.all_gather(up_projection_bias, "blk", axis=0, tiled=True),
            lax.all_gather(norm_gains, "blk", axis=1, tiled=True),
            lax.all_gather(biases, "blk", axis=1, tiled=True),
            lax.all_gather(type_table, "blk", axis=1, tiled=True),
        )

    qkv_full, out_full, up_full, down_full, up_bias_full, gain_full, bias_full, type_full = (
        fetch_weights()
    )
    bias_float = bias_full.astype(jnp.float32)
    gain_float = gain_full.astype(jnp.float32)
    flat_pos = pos_ids.reshape(row_count)
    portion = lax.all_gather(pos_table, "blk", axis=0, tiled=True)
    local_slots = flat_pos
    onehot = (
        local_slots[:, None] == jnp.arange(portion.shape[0], dtype=jnp.int32)[None, :]
    ).astype(jnp.bfloat16)
    positions = jnp.dot(onehot, portion, preferred_element_type=jnp.float32)
    is_second = type_ids.reshape(row_count, 1) == 1
    typed_rows = jnp.where(
        is_second, type_full[1].astype(jnp.float32), type_full[0].astype(jnp.float32)
    )
    embedded_tokens = (
        hidden.reshape(row_count, model_width).astype(jnp.float32) + positions + typed_rows
    )
    embedded_low = embedded_tokens.astype(jnp.bfloat16)
    projected_rows = jnp.dot(embedded_low, qkv_full, preferred_element_type=jnp.float32)
    token_shape = (seq_count, seg_tokens, model_width)
    queries = (
        (projected_rows[:, :model_width] + bias_float[0]).astype(jnp.bfloat16).reshape(token_shape)
    )
    keys_token = (
        projected_rows[:, model_width : 2 * model_width].astype(jnp.bfloat16).reshape(token_shape)
    )
    values_token = (
        (projected_rows[:, 2 * model_width :] + bias_float[1])
        .astype(jnp.bfloat16)
        .reshape(token_shape)
    )
    query_local, key_local, value_local = (
        lax.all_to_all(queries, "head", split_axis=2, concat_axis=1, tiled=True),
        lax.all_to_all(keys_token, "head", split_axis=2, concat_axis=1, tiled=True),
        lax.all_to_all(values_token, "head", split_axis=2, concat_axis=1, tiled=True),
    )
    head_shape = (seq_count, query_rows, head_count, head_size)
    query_heads = query_local.reshape(head_shape)
    key_heads = key_local.reshape(head_shape)
    value_heads = value_local.reshape(head_shape)
    start_peak = jnp.full((seq_count, head_count, query_rows), -jnp.inf, jnp.float32)
    start_total = jnp.zeros((seq_count, head_count, query_rows), jnp.float32)
    zero_heads = jnp.zeros((seq_count, head_count, query_rows, head_size), jnp.float32)
    fold_keys = forward_fold(query_heads, score_scale, head_count, head_size)
    row_peak, row_total, weighted = fold_keys(
        (start_peak, start_total, zero_heads),
        (
            lax.all_gather(key_local, "blk", axis=1, tiled=True),
            lax.all_gather(value_local, "blk", axis=1, tiled=True),
        ),
        jnp.int32(0),
    )
    log_totals = row_peak + jnp.log(row_total)
    attention_result = weighted / row_total[..., None]
    attended_low = (
        attention_result.transpose(0, 2, 1, 3)
        .reshape(seq_count, query_rows, local_width)
        .astype(jnp.bfloat16)
    )
    attended_token = lax.all_to_all(
        attended_low, "head", split_axis=1, concat_axis=2, tiled=True
    ).reshape(row_count, model_width)
    residual_branch = (
        jnp.dot(attended_token, out_full, preferred_element_type=jnp.float32) + bias_float[2]
    )
    first_layer_norm, first_pull = jax.vjp(
        norm_layer, embedded_tokens + residual_branch, gain_float[0], bias_float[3]
    )
    first_low = first_layer_norm.astype(jnp.bfloat16)
    inner_product_sum = jnp.dot(
        first_low, up_full, preferred_element_type=jnp.float32
    ) + up_bias_full.astype(jnp.float32)
    gelu_activations, gelu_pull = jax.vjp(gelu_exact, inner_product_sum)
    activated_low = gelu_activations.astype(jnp.bfloat16)
    second_layer_norm = (
        jnp.dot(activated_low, down_full, preferred_element_type=jnp.float32) + bias_float[4]
    )
    final_norm, final_pull = jax.vjp(
        norm_layer, first_layer_norm + second_layer_norm, gain_float[1], bias_float[5]
    )
    layer_out = final_norm.astype(jnp.bfloat16).reshape(token_shape)
    qkv_full, out_full, up_full, down_full, up_bias_full, gain_full, bias_full, type_full = (
        fetch_weights()
    )
    grad_final, grad_gain_two, grad_shift_two = final_pull(
        cotangent.reshape(row_count, model_width).astype(jnp.float32)
    )
    grad_second = grad_final.astype(jnp.bfloat16)
    grad_down = jnp.einsum(
        "rf,rd->fd", activated_low, grad_second, preferred_element_type=jnp.float32
    )
    grad_bias_second = jnp.sum(grad_second.astype(jnp.float32), axis=0)
    (grad_inner,) = gelu_pull(
        jnp.einsum("rd,fd->rf", grad_second, down_full, preferred_element_type=jnp.float32)
    )
    grad_inner_low = grad_inner.astype(jnp.bfloat16)
    grad_up = jnp.einsum("rd,rf->df", first_low, grad_inner_low, preferred_element_type=jnp.float32)
    grad_up_bias = jnp.sum(grad_inner_low.astype(jnp.float32), axis=0)
    grad_first = grad_final + jnp.einsum(
        "rf,df->rd", grad_inner_low, up_full, preferred_element_type=jnp.float32
    )
    grad_resid, grad_gain_one, grad_shift_one = first_pull(grad_first)
    grad_branch = grad_resid.astype(jnp.bfloat16)
    grad_out = jnp.einsum(
        "re,rd->ed", attended_token, grad_branch, preferred_element_type=jnp.float32
    )
    grad_bias_branch = jnp.sum(grad_branch.astype(jnp.float32), axis=0)
    grad_attended = (
        jnp.einsum("rd,ed->re", grad_branch, out_full, preferred_element_type=jnp.float32)
        .astype(jnp.bfloat16)
        .reshape(token_shape)
    )
    grad_local = lax.all_to_all(grad_attended, "head", split_axis=2, concat_axis=1, tiled=True)
    grad_heads = grad_local.reshape(head_shape)
    delta_rows = jnp.sum(
        grad_heads.astype(jnp.float32).transpose(0, 2, 1, 3) * attention_result, axis=-1
    )
    fold_queries = query_fold(
        query_heads, grad_heads, log_totals, delta_rows, score_scale, head_count, head_size
    )
    grad_query_sum = fold_queries(
        zero_heads,
        (
            lax.all_gather(key_local, "blk", axis=1, tiled=True),
            lax.all_gather(value_local, "blk", axis=1, tiled=True),
        ),
        jnp.int32(0),
    )
    fold_side = key_fold(key_heads, value_heads, score_scale, head_count, head_size)
    grad_key_sum, grad_value_sum = fold_side(
        (zero_heads, zero_heads),
        (
            lax.all_gather(query_local.astype(jnp.float32), "blk", axis=1, tiled=True).astype(
                jnp.bfloat16
            ),
            lax.all_gather(grad_local.astype(jnp.float32), "blk", axis=1, tiled=True).astype(
                jnp.bfloat16
            ),
            lax.all_gather(log_totals.transpose(0, 2, 1), "blk", axis=1, tiled=True),
            lax.all_gather(delta_rows.transpose(0, 2, 1), "blk", axis=1, tiled=True),
        ),
        jnp.int32(0),
    )
    grad_keys_local = (
        (grad_key_sum * score_scale)
        .transpose(0, 2, 1, 3)
        .reshape(seq_count, query_rows, local_width)
        .astype(jnp.bfloat16)
    )
    grad_values_local = (
        grad_value_sum.transpose(0, 2, 1, 3)
        .reshape(seq_count, query_rows, local_width)
        .astype(jnp.bfloat16)
    )
    grad_query_local = (
        (grad_query_sum * score_scale)
        .transpose(0, 2, 1, 3)
        .reshape(seq_count, query_rows, local_width)
        .astype(jnp.bfloat16)
    )
    grad_query_token, grad_key_token, grad_value_token = (
        lax.all_to_all(grad_query_local, "head", split_axis=1, concat_axis=2, tiled=True),
        lax.all_to_all(grad_keys_local, "head", split_axis=1, concat_axis=2, tiled=True),
        lax.all_to_all(grad_values_local, "head", split_axis=1, concat_axis=2, tiled=True),
    )
    grad_qkv = jnp.concatenate(
        [grad_query_token, grad_key_token, grad_value_token], axis=-1
    ).reshape(row_count, 3 * model_width)
    grad_qkv_full = jnp.einsum(
        "rd,rf->df", embedded_low, grad_qkv, preferred_element_type=jnp.float32
    )
    grad_bias_query = jnp.sum(
        grad_query_token.astype(jnp.float32).reshape(row_count, model_width), axis=0
    )
    grad_bias_value = jnp.sum(
        grad_value_token.astype(jnp.float32).reshape(row_count, model_width), axis=0
    )
    grad_embedded = grad_resid + jnp.einsum(
        "rf,df->rd", grad_qkv, qkv_full, preferred_element_type=jnp.float32
    )
    second_mask = is_second.astype(jnp.float32)
    grad_type_one = jnp.sum(grad_embedded * second_mask, axis=0)
    grad_type_zero = jnp.sum(grad_embedded * (1.0 - second_mask), axis=0)
    length = lax.axis_size("blk") * pos_table.shape[0]
    local_slots = flat_pos
    inside = (local_slots >= 0) & (local_slots < length)
    slot_index = jnp.where(inside, local_slots, length)
    buffer = jnp.zeros((length + 1, model_width), jnp.float32).at[slot_index].add(grad_embedded)
    grad_positions = lax.psum_scatter(buffer[:length], "blk", scatter_dimension=0, tiled=True)
    gain_stack = jnp.stack([grad_gain_one, grad_gain_two])
    bias_stack = jnp.stack(
        [
            grad_bias_query,
            grad_bias_value,
            grad_bias_branch,
            grad_shift_one,
            grad_bias_second,
            grad_shift_two,
        ]
    )
    type_stack = jnp.stack([grad_type_zero, grad_type_one])
    (
        shard_qkv,
        shard_out,
        shard_up,
        shard_down,
        shard_up_bias,
        shard_gains,
        shard_biases,
        shard_types,
    ) = (
        lax.psum_scatter(grad_qkv_full, "blk", scatter_dimension=0, tiled=True),
        lax.psum_scatter(grad_out, "blk", scatter_dimension=0, tiled=True),
        lax.psum_scatter(grad_up, "blk", scatter_dimension=0, tiled=True),
        lax.psum_scatter(grad_down, "blk", scatter_dimension=0, tiled=True),
        lax.psum_scatter(grad_up_bias, "blk", scatter_dimension=0, tiled=True),
        lax.psum_scatter(gain_stack, "blk", scatter_dimension=1, tiled=True),
        lax.psum_scatter(bias_stack, "blk", scatter_dimension=1, tiled=True),
        lax.psum_scatter(type_stack, "blk", scatter_dimension=1, tiled=True),
    )
    (
        total_qkv,
        total_out,
        total_up,
        total_down,
        total_up_bias,
        total_gains,
        total_biases,
        total_types,
        total_positions,
    ) = lax.psum(
        (
            shard_qkv,
            shard_out,
            shard_up,
            shard_down,
            shard_up_bias,
            shard_gains,
            shard_biases,
            shard_types,
            grad_positions,
        ),
        "head",
    )
    grad_hidden = grad_embedded.reshape(token_shape)
    return (
        layer_out,
        grad_hidden,
        total_positions,
        total_types,
        total_qkv,
        total_out,
        total_up,
        total_down,
        total_up_bias,
        total_gains,
        total_biases,
    )


def solution(mesh):
    in_specs = (
        P(None, ("head", "blk"), None),
        P(None, ("head", "blk")),
        P(None, ("head", "blk")),
        P(None, ("head", "blk"), None),
        P("blk", None),
        P(None, "blk"),
        P("blk", None),
        P("blk", None),
        P("blk", None),
        P("blk", None),
        P("blk"),
        P(None, "blk"),
        P(None, "blk"),
    )
    out_specs = (
        P(None, ("head", "blk"), None),
        P(None, ("head", "blk"), None),
        P("blk", None),
        P(None, "blk"),
        P("blk", None),
        P("blk", None),
        P("blk", None),
        P("blk", None),
        P("blk"),
        P(None, "blk"),
        P(None, "blk"),
    )
    return jax.shard_map(
        on_device, mesh=mesh, in_specs=in_specs, out_specs=out_specs, check_vma=False
    )
```

profile of v0, /device:TPU:0, one launch (start us, length us, event | category | flops | bytes accessed | tf_op | source)
XLA Modules:
  0.0 1844.0 jit_solution(11304274504573571308)
XLA Ops:
  10.2 23.7 %all-gather = bf16[16,64,2]{1,2,0:T(2,128)(2,1)S(1)} all-gather(bf16[1,64,2]{1,2,0:T(2,128)(2,1)} %bitcast.359), channel_id=1, replica_groups=mesh['head'=2,'blk'=16] {'blk'}, dimensions={0}, use_global_device_ids=true | all-gather | bytes 4352 | tf_op jit(solution)/shard_map/all_gather | solution.py:188
  34.0 105.3 %all-gather.14.cloned.1.call-done = bf16[8192,1024]{1,0:T(8,128)(2,1)} async-done(((bf16[512,1024]{1,0:T(8,128)(2,1)}), bf16[8192,1024]{1,0:T(8,128)(2,1)}) %all-gather.14.cloned.1.call-update) | async-done | bytes 16777232 | tf_op jit(solution)/shard_map/all_gather | solution.py:197
  139.3 8.2 fusion.40
  147.6 53.6 %all-gather.16.cloned.1.call-done = bf16[1024,3072]{1,0:T(8,128)(2,1)} async-done(((bf16[64,3072]{1,0:T(8,128)(2,1)}), bf16[1024,3072]{1,0:T(8,128)(2,1)}) %all-gather.16.cloned.1.call-update) | async-done | bytes 6291472 | tf_op jit(solution)/shard_map/all_gather | solution.py:181
  205.9 8.2 all_to_all.126
  215.6 19.3 %all-gather.1 = bf16[16,64,6]{1,2,0:T(8,128)(2,1)S(1)} all-gather(bf16[1,64,6]{1,2,0:T(8,128)(2,1)S(1)} %bitcast.358), channel_id=1, replica_groups=mesh['head'=2,'blk'=16] {'blk'}, dimensions={0}, use_global_device_ids=true | all-gather | bytes 13056 | tf_op jit(solution)/shard_map/all_gather | solution.py:187
  236.7 8.3 all_to_all.127
  248.4 17.3 all-gather.2
  271.1 5.5 all-to-all-done.1
  278.1 6.3 copy.142
  284.4 31.1 %all-gather.20.cloned.1.call-done = bf16[2,2048,512]{2,1,0:T(8,128)(2,1)} async-done(((bf16[2,128,512]{2,1,0:T(8,128)(2,1)}), bf16[2,2048,512]{2,1,0:T(8,128)(2,1)}) %all-gather.20.cloned.1.call-update) | async-done | bytes 4194320 | tf_op jit(solution)/shard_map/all_gather | solution.py:241
  315.5 6.3 copy.144
  321.8 17.7 while.48
  344.0 19.0 %all-gather.3 = bf16[16,1,256]{2,1,0:T(2,128)(2,1)S(1)} all-gather(bf16[1,1,256]{2,1,0:T(2,128)(2,1)S(1)} %reshape.315), channel_id=1, replica_groups=mesh['head'=2,'blk'=16] {'blk'}, dimensions={0}, use_global_device_ids=true | all-gather | bytes 8704 | tf_op jit(solution)/shard_map/all_gather | solution.py:185
  365.8 66.9 %all-gather.24.cloned.1.call-done = bf16[1024,4096]{1,0:T(8,128)(2,1)} async-done(((bf16[64,4096]{1,0:T(8,128)(2,1)}), bf16[1024,4096]{1,0:T(8,128)(2,1)}) %all-gather.24.cloned.1.call-update) | async-done | bytes 8388624 | tf_op jit(solution)/shard_map/all_gather | solution.py:183
  432.6 9.9 multiply_convert_fusion.2
  442.6 65.1 %all-gather.26.cloned.1.call-done = bf16[4096,1024]{1,0:T(8,128)(2,1)} async-done(((bf16[256,1024]{1,0:T(8,128)(2,1)}), bf16[4096,1024]{1,0:T(8,128)(2,1)}) %all-gather.26.cloned.1.call-update) | async-done | bytes 8388624 | tf_op jit(solution)/shard_map/all_gather | solution.py:184
  507.7 4.9 fusion.66
  515.4 6.0 convert_reduce_fusion
  532.0 10.1 all_to_all.128
  549.1 9.6 fusion.57
  559.6 8.2 fusion.70
  571.2 20.6 %all_gather.63 = f32[2,2048,8]{1,2,0:T(8,128)} all-gather(f32[2,128,8]{1,2,0:T(8,128)S(1)} %bitcast.333), channel_id=1, replica_groups=mesh['head'=2,'blk'=16] {'blk'}, dimensions={1}, use_global_device_ids=true | all-gather | bytes 139264 | tf_op jit(solution)/shard_map/all_gather | solution.py:331
  592.5 37.4 %while.49 = (s32[]{:T(128)}, f32[2,8,128,64]{2,3,1,0:T(8,128)}, bf16[2,2048,512]{1,2,0:T(8,128)(2,1)}, bf16[2,128,8,64]{1,3,2,0:T(8,128)(2,1)S(1)}, f32[2,8,128]...) while((s32[]{:T(128)}, f32[2,8,128,64]{2,3,1,0:T(8,128)}, ...), condition=%wide.region_14.15_spmd.clone, body=%wide.region_13.14_spmd.clone.sunk | while | flops 408158208 | bytes 21512432 | solution.py:119
  606.3 4.0 fusion.143
  624.9 4.1 fusion.143
  631.9 4.1 all-to-all-start.5
  636.0 20.0 %all_gather.65 = f32[2,2048,8]{1,2,0:T(8,128)} all-gather(f32[2,128,8]{1,2,0:T(8,128)S(1)} %bitcast.332), channel_id=1, replica_groups=mesh['head'=2,'blk'=16] {'blk'}, dimensions={1}, use_global_device_ids=true | all-gather | bytes 139264 | tf_op jit(solution)/shard_map/all_gather | solution.py:332
  656.0 66.9 %while.50 = (s32[]{:T(128)}, f32[2,8,128,64]{2,3,1,0:T(8,128)}, f32[2,8,128,64]{2,3,1,0:T(8,128)}, bf16[2,2048,512]{2,1,0:T(8,128)(2,1)}, bf16[2,128,8,64]{1,3,2...) while((s32[]{:T(128)}, f32[2,8,128,64]{2,3,1,0:T(8,128)}, ...), condition=%wide.region_16.17_spmd.clone, body=%wide.region_15.16_spmd.clone.sunk | while | flops 545783808 | bytes 36405556 | solution.py:151
  662.4 5.5 fusion.152
  678.5 5.5 fusion.152
  694.7 5.9 fusion.152
  700.6 4.0 fusion.153
  712.4 6.3 fusion.152
  729.4 5.0 all-to-all-done.7
  743.4 6.3 fusion.50
  750.8 5.1 multiply_reduce_fusion.2
  755.9 15.5 scatter_custom_fusion
  771.3 23.6 %slice.70 = f32[8192,1024]{1,0:T(8,128)} slice(f32[8193,1024]{1,0:T(8,128)} %scatter_custom_fusion), slice={[0:8192], [0:1024]} | slice | bytes 67108864 | tf_op jit(solution)/shard_map/slice | solution.py:381
  799.5 67.7 %reduce-scatter.21.cloned.1.call-done = f32[64,4096]{1,0:T(8,128)} async-done(((f32[1024,4096]{1,0:T(8,128)}), f32[64,4096]{1,0:T(8,128)}) %reduce-scatter.21.cloned.1.call-update) | async-done | bytes 1048592 | tf_op jit(solution)/shard_map/reduce_scatter | solution.py:406
  867.2 180.4 %reduce-scatter.23.cloned.1.call-done = f32[256,1024]{1,0:T(8,128)} async-done(((f32[4096,1024]{1,0:T(8,128)}), f32[256,1024]{1,0:T(8,128)}) %reduce-scatter.23.cloned.1.call-update) | async-done | bytes 1048592 | tf_op jit(solution)/shard_map/reduce_scatter | solution.py:407
  1047.6 138.1 %reduce-scatter.17.cloned.1.call-done = f32[64,3072]{1,0:T(8,128)} async-done(((f32[1024,3072]{1,0:T(8,128)}), f32[64,3072]{1,0:T(8,128)}) %reduce-scatter.17.cloned.1.call-update) | async-done | bytes 786448 | tf_op jit(solution)/shard_map/reduce_scatter | solution.py:404
  1185.7 334.0 %reduce-scatter.15.cloned.1.call-done = f32[512,1024]{1,0:T(8,128)} async-done(((f32[8192,1024]{1,0:T(8,128)}), f32[512,1024]{1,0:T(8,128)}) %reduce-scatter.15.cloned.1.call-update) | async-done | bytes 2097168 | tf_op jit(solution)/shard_map/reduce_scatter | solution.py:381
  1521.6 59.7 %all-reduce = f32[4096]{0:T(1024)S(1)} all-reduce(f32[4096]{0:T(1024)S(1)} %get-tuple-element.691), channel_id=8, replica_groups=mesh['head'=2,'blk'=16] {'blk'}, use_global_device_ids=true, to_apply=%region_33.34.clone | all-reduce | flops 4096 | bytes 32768
  1582.2 56.1 %reduce-scatter.25.cloned.1.call-done = f32[64,2]{1,0:T(8,128)} async-done(((f32[1024,2]{1,0:T(8,128)}), f32[64,2]{1,0:T(8,128)}) %reduce-scatter.25.cloned.1.call-update) | async-done | bytes 528
  1639.1 58.4 %reduce-scatter.29.cloned.1.call-done = f32[64,6]{1,0:T(8,128)} async-done(((f32[1024,6]{1,0:T(8,128)}), f32[64,6]{1,0:T(8,128)}) %reduce-scatter.29.cloned.1.call-update) | async-done | bytes 1552
  1698.3 5.6 all-reduce.1
  1703.8 126.0 %all-reduce.5.cloned.1.call-done = (f32[512,1024]{1,0:T(8,128)}, f32[64,3072]{1,0:T(8,128)}, f32[64,1024]{1,0:T(8,128)}, f32[64,4096]{1,0:T(8,128)}, f32[256,1024]{1,0:T(8,128)}) async-done(((f32[512,1024]{1,0:T(8,128)}, f32[64,3072]{1,0:T(8,128)}, f32[64,1024]{1,0:T(8,128)}, f32[64,4096]{1,0:T(8,128)}, f32[256,1024]{1,0:T(8,128)}), (f32[512,1024]{1,0:T(8,128)}, f32[64,3072]{1,0:T(8,128)}, ...) | async-done | bytes 5242896 | tf_op jit(solution)/shard_map/psum | solution.py:423
  (344 shorter events, 173.0 us)
Async XLA Ops:
  7.2 132.2 %all-gather.14.cloned.1.call-start = ((), (), s32[]{:S(2)}) async-start(), calls=%async_computation.16 | async-start | bytes 17825792 | tf_op jit(solution)/shard_map/all_gather | solution.py:197
  7.9 193.3 %all-gather.16.cloned.1.call-start = ((), (), s32[]{:S(2)}) async-start(), calls=%async_computation.17 | async-start | bytes 6684672 | tf_op jit(solution)/shard_map/all_gather | solution.py:181
  8.7 269.4 %all-gather.18.cloned.1.call-start = ((), (), s32[]{:S(2)}) async-start(), calls=%async_computation.18 | async-start | bytes 4456448 | tf_op jit(solution)/shard_map/all_gather | solution.py:240
  9.5 138.1 %copy-start.34 = (pred[128]{0:T(512)(128)(4,1)}, pred[128]{0:T(512)(128)(4,1)S(1)}, u32[]{:S(2)}) copy-start(pred[128]{0:T(512)(128)(4,1)S(1)} %eq.41) | copy-start | bytes 388
  147.6 215.8 %copy-start.2 = (f32[128,1024]{1,0:T(8,128)}, f32[128,1024]{1,0:T(8,128)S(1)}, u32[]{:S(2)}) copy-start(f32[128,1024]{1,0:T(8,128)S(1)} %fusion.40) | copy-start | bytes 1572868
  205.0 10.5 copy-start.29
  214.5 22.2 %copy-start.5 = (bf16[1024,2,64]{2,1,0:T(2,128)(2,1)}, bf16[1024,2,64]{2,1,0:T(2,128)(2,1)S(1)}, u32[]{:S(2)}) copy-start(bf16[1024,2,64]{2,1,0:T(2,128)(2,1)S(1)} %reshape.338) | copy-start | bytes 786436
  215.5 100.0 %all-gather.20.cloned.1.call-start = ((), (), s32[]{:S(2)}) async-start(), calls=%async_computation.19 | async-start | bytes 4456448 | tf_op jit(solution)/shard_map/all_gather | solution.py:241
  236.2 12.1 copy-start.30
  236.2 29.5 %copy-start.18 = (bf16[128,1024]{1,0:T(8,128)(2,1)S(1)}, bf16[128,1024]{1,0:T(8,128)(2,1)}, u32[]{:S(2)}) copy-start(bf16[128,1024]{1,0:T(8,128)(2,1)} %get-tuple-element.710) | copy-start | bytes 786436
  246.4 117.0 %all-gather.22.cloned.1.call-start = ((), (), s32[]{:S(2)}) async-start(), calls=%async_computation.20 | async-start | bytes 2228224 | tf_op jit(solution)/shard_map/all_gather | solution.py:182
  247.0 185.6 %all-gather.24.cloned.1.call-start = ((), (), s32[]{:S(2)}) async-start(), calls=%async_computation.21 | async-start | bytes 8912896 | tf_op jit(solution)/shard_map/all_gather | solution.py:183
  247.6 260.1 %all-gather.26.cloned.1.call-start = ((), (), s32[]{:S(2)}) async-start(), calls=%async_computation.22 | async-start | bytes 8912896 | tf_op jit(solution)/shard_map/all_gather | solution.py:184
  267.2 9.4 all-to-all-start.1
  270.6 385.3 %all-gather.28.cloned.1.call-start = ((), (), s32[]{:S(2)}) async-start(), calls=%async_computation.23 | async-start | bytes 4456448 | tf_op jit(solution)/shard_map/all_gather | solution.py:325
  321.8 22.2 %copy-start.32 = (bf16[256]{0:T(256)(128)(2,1)S(1)}, bf16[256]{0:T(256)(128)(2,1)}, u32[]{:S(2)}) copy-start(bf16[256]{0:T(256)(128)(2,1)} %param.29) | copy-start | bytes 1540
  340.5 22.6 %all-to-all-start.3 = ((bf16[2,128,512]{2,0,1:T(2,128)(2,1)}), bf16[2,128,512]{2,0,1:T(2,128)(2,1)S(1)}, u32[]{:S(2)}, u32[]{:S(2)}) async-start(bf16[2,128,512]{2,0,1:T(2,128)(2,1)} %copy.145), calls=%async_computation.3 | async-start | bytes 524288 | tf_op jit(solution)/shard_map/all_to_all | solution.py:252
  343.9 312.0 %all-gather.30.cloned.1.call-start = ((), (), s32[]{:S(2)}) async-start(), calls=%async_computation.24 | async-start | bytes 4456448 | tf_op jit(solution)/shard_map/all_gather | solution.py:328
  507.7 7.7 slice-start
  507.7 5.2 copy-start.12
  507.7 7.7 slice-start.1
  513.7 7.7 slice-start.2
  515.4 6.0 copy-start.14
  515.4 6.0 slice-start.3
  546.1 253.4 %reduce-scatter.19.cloned.1.call-start = ((), (), s32[]{:S(2)}) async-start(), calls=%async_computation.27 | async-start | bytes 4456448 | tf_op jit(solution)/shard_map/reduce_scatter | solution.py:405
  549.0 318.2 %reduce-scatter.21.cloned.1.call-start = ((), (), s32[]{:S(2)}) async-start(), calls=%async_computation.28 | async-start | bytes 17825792 | tf_op jit(solution)/shard_map/reduce_scatter | solution.py:406
  558.7 488.9 %reduce-scatter.23.cloned.1.call-start = ((), (), s32[]{:S(2)}) async-start(), calls=%async_computation.29 | async-start | bytes 17825792 | tf_op jit(solution)/shard_map/reduce_scatter | solution.py:407
  567.9 23.9 %copy-start.11 = (bf16[2,64,2,512]{3,1,2,0:T(8,128)(2,1)S(1)}, bf16[2,64,2,512]{3,1,2,0:T(8,128)(2,1)}, u32[]{:S(2)}) copy-start(bf16[2,64,2,512]{3,1,2,0:T(8,128)(2,1)} %copy.151) | copy-start | bytes 786436
  631.9 93.0 %all-to-all-start.5 = ((bf16[2,128,512]{2,0,1:T(2,128)(2,1)}), bf16[2,128,512]{2,0,1:T(2,128)(2,1)}, u32[]{:S(2)}, u32[]{:S(2)}) async-start(bf16[2,128,512]{2,0,1:T(2,128)(2,1)} %copy.157), calls=%async_computation.5 | async-start | bytes 524288 | tf_op jit(solution)/shard_map/all_to_all | solution.py:354
  662.4 5.5 copy-start
  678.5 5.5 copy-start
  684.0 3.4 copy-start.22
  694.7 5.9 copy-start
  700.5 4.0 copy-start.22
  712.4 6.3 copy-start
  722.9 5.5 copy-start.23
  724.9 9.4 all-to-all-start.7
  734.3 8.6 all-to-all-start.6
  737.8 448.0 %reduce-scatter.17.cloned.1.call-start = ((), (), s32[]{:S(2)}) async-start(), calls=%async_computation.26 | async-start | bytes 13369344 | tf_op jit(solution)/shard_map/reduce_scatter | solution.py:404
  739.2 4.2 copy-start.3
  749.7 770.0 %reduce-scatter.15.cloned.1.call-start = ((), (), s32[]{:S(2)}) async-start(), calls=%async_computation.25 | async-start | bytes 35651584 | tf_op jit(solution)/shard_map/reduce_scatter | solution.py:381
  755.9 15.5 copy-start.20
  794.9 786.4 %reduce-scatter.27.cloned.1.call-start = ((), (), s32[]{:S(2)}) async-start(), calls=%async_computation.31 | async-start | bytes 557056
  797.0 841.3 %reduce-scatter.25.cloned.1.call-start = ((), (), s32[]{:S(2)}) async-start(), calls=%async_computation.30 | async-start | bytes 557056
  798.2 899.3 %reduce-scatter.29.cloned.1.call-start = ((), (), s32[]{:S(2)}) async-start(), calls=%async_computation.32 | async-start | bytes 557056
  799.4 1030.5 %all-reduce.5.cloned.1.call-start = ((), (), s32[]{:S(2)}) async-start(), calls=%async_computation.33 | async-start | bytes 10485760 | tf_op jit(solution)/shard_map/psum | solution.py:423
  1829.9 4.2 copy-start.26
  1829.9 4.9 copy-start.17
  (33 other events, 58.8 us)
Sparse Core Ops, SparseCore 0:
  10.1 129.1 all-gather.13
  141.6 59.5 all-gather.15
  215.7 48.2 all-gather.17
  266.6 48.9 all-gather.19
  317.6 39.9 all-gather.21
  359.6 73.0 all-gather.23
  434.8 72.8 all-gather.25
  509.9 48.9 all-gather.27
  561.7 49.4 all-gather.29
  614.9 71.9 reduce-scatter.18
  690.9 176.2 reduce-scatter.20
  871.2 176.4 reduce-scatter.22
  1051.7 134.0 reduce-scatter.16
  1189.9 329.8 reduce-scatter.14
  1523.7 55.2 reduce-scatter.26
  1583.0 55.1 reduce-scatter.24
  1642.2 55.1 reduce-scatter.28
  1700.2 129.6 all-reduce.4
where the time goes:
time: 1850 us; the launch traced here: 1840 us
  waiting for transfers between devices  1300 us (70%)
  blocking collectives  212 us (11%)
  matrix products  155 us (8%)
  local copies, waits for them, and re-layouts  115 us (6%)
  other arithmetic  26 us (1%)
  starting transfers between devices  19.4 us (1%)
    reduce_scatter x1, waiting for transfers between devices, on_device(): lax.psum_scatter(buffer[:length], 'blk', scatter_dimension=0, tiled=True)  334 us
    reduce_scatter x1, waiting for transfers between devices, on_device(): lax.psum_scatter(grad_down, 'blk', scatter_dimension=0, tiled=True)  180 us
    reduce_scatter x1, waiting for transfers between devices, on_device(): lax.psum_scatter(grad_qkv_full, 'blk', scatter_dimension=0, tiled=True)  138 us
    psum x1, waiting for transfers between devices, on_device(): lax.psum((shard_qkv, shard_out, shard_up, shard_down, shard_up_bias, shar...  126 us
    unnamed x21, waiting for transfers between devices  118 us
    all_gather x1, waiting for transfers between devices, on_device(): portion = lax.all_gather(pos_table, 'blk', axis=0, tiled=True)  105 us
    reduce_scatter x1, waiting for transfers between devices, on_device(): lax.psum_scatter(grad_up, 'blk', scatter_dimension=0, tiled=True)  67.7 us
    all_gather x1, waiting for transfers between devices, fetch_weights(): lax.all_gather(up_projection_weight, 'blk', axis=0, tiled=True)  66.9 us
  transfers between devices with their start and end apart: 23, of which 15 were waited for; matrix products, arithmetic and copies ran while one was open for 15% of the time, Pallas kernels for 0%

commit v1 on v0

--- a/solution.py
+++ b/solution.py
@@ -1,11 +1,704 @@
+import functools
 import math
 
 import jax
 import jax.numpy as jnp
 from jax import lax
+from jax.experimental import pallas as pl
+from jax.experimental.pallas import tpu as pltpu
 from jax.sharding import PartitionSpec as P
 
 HEADS = 16
+MESH = pl.DeviceIdType.MESH
+F32 = jnp.float32
+BF16 = jnp.bfloat16
+VSPEC = pl.BlockSpec(memory_space=pltpu.VMEM)
+
+
+def place():
+    h = lax.axis_index("head")
+    b = lax.axis_index("blk")
+    return h, b // 4, (b // 2) % 2, b % 2
+
+
+def blk(o, y, c):
+    return (o * 2 + y) * 2 + c
+
+
+def remote(src, dst, sems, index, device):
+    return pltpu.make_async_remote_copy(
+        src_ref=src,
+        dst_ref=dst,
+        send_sem=sems.at[0, index],
+        recv_sem=sems.at[1, index],
+        device_id=device,
+        device_id_type=MESH,
+    )
+
+
+def greet(devices):
+    barrier = pltpu.get_barrier_semaphore()
+    for device in devices:
+        pl.semaphore_signal(barrier, inc=1, device_id=device, device_id_type=MESH)
+    pl.semaphore_wait(barrier, len(devices))
+
+
+def comm_call(kernel, name, outs, ins, scratch, copies, cid, limit=None):
+    return pl.pallas_call(
+        kernel,
+        name=name,
+        out_shape=[jax.ShapeDtypeStruct(s, d) for s, d in outs],
+        in_specs=[VSPEC] * len(ins),
+        out_specs=[VSPEC] * len(outs),
+        scratch_shapes=[pltpu.VMEM(s, d) for s, d in scratch]
+        + [pltpu.SemaphoreType.DMA((2, copies))],
+        compiler_params=pltpu.CompilerParams(
+            collective_id=cid, has_side_effects=True, vmem_limit_bytes=limit
+        ),
+    )(*ins)
+
+
+def plane_gather_kernel(x_ref, out_ref, sems):
+    h, o, y, c = place()
+    dev_x, dev_y, dev_c = (1 - h, blk(o, y, c)), (h, blk(o, 1 - y, c)), (h, blk(o, y, 1 - c))
+    mine = h * 4 + y * 2 + c
+    of_x = (1 - h) * 4 + y * 2 + c
+    of_y = h * 4 + (1 - y) * 2 + c
+    of_d = (1 - h) * 4 + (1 - y) * 2 + c
+    greet((dev_x, dev_y, dev_c))
+    sent = []
+
+    def go(src, slot, index, device, half=None):
+        if half is None:
+            copy = remote(src, out_ref.at[:, slot], sems, index, device)
+        else:
+            copy = remote(src, out_ref.at[half, slot], sems, index, device)
+        copy.start()
+        sent.append(copy)
+
+    def arrived(slot, index, device, half=None):
+        ref = out_ref.at[:, slot] if half is None else out_ref.at[half, slot]
+        remote(ref, ref, sems, index, device).wait_recv()
+
+    go(x_ref, mine, 0, dev_x)
+    go(x_ref, mine, 1, dev_y)
+    go(x_ref, mine, 2, dev_c)
+    out_ref[:, pl.ds(mine, 1)] = x_ref[...][:, None]
+    arrived(of_x, 0, dev_x)
+    go(out_ref.at[0, of_x], of_x, 3, dev_y, 0)
+    go(out_ref.at[:, of_x], of_x, 4, dev_c)
+    arrived(of_y, 1, dev_y)
+    go(out_ref.at[1, of_y], of_y, 5, dev_x, 1)
+    go(out_ref.at[:, of_y], of_y, 6, dev_c)
+    arrived(of_d, 3, dev_y, 0)
+    go(out_ref.at[0, of_d], of_d, 7, dev_c, 0)
+    arrived(of_d, 5, dev_x, 1)
+    go(out_ref.at[1, of_d], of_d, 8, dev_c, 1)
+    flip = 1 - 2 * c
+    arrived(mine + flip, 2, dev_c)
+    arrived(of_x + flip, 4, dev_c)
+    arrived(of_y + flip, 6, dev_c)
+    arrived(of_d + flip, 7, dev_c, 0)
+    arrived(of_d + flip, 8, dev_c, 1)
+    for copy in sent:
+        copy.wait_send()
+
+
+def plane_gather(x, cid):
+    two, rows, width = x.shape
+    (out,) = comm_call(
+        plane_gather_kernel, "plane_gather", [((2, 8, rows, width), x.dtype)], [x], [], 9, cid
+    )
+    return out
+
+
+def plane_scatter_kernel(x_ref, out_ref, near, part, from_x, from_y, diag, sems):
+    h, o, y, c = place()
+    dev_x, dev_y, dev_c = (1 - h, blk(o, y, c)), (h, blk(o, 1 - y, c)), (h, blk(o, y, 1 - c))
+    mine = h * 4 + y * 2 + c
+    of_x = (1 - h) * 4 + y * 2 + c
+    of_y = h * 4 + (1 - y) * 2 + c
+    of_d = (1 - h) * 4 + (1 - y) * 2 + c
+    flip = 1 - 2 * c
+    greet((dev_x, dev_y, dev_c))
+    sent = []
+
+    def go(src, dst, index, device):
+        copy = remote(src, dst, sems, index, device)
+        copy.start()
+        sent.append(copy)
+
+    def arrived(dst, index, device):
+        remote(dst, dst, sems, index, device).wait_recv()
+
+    for k, slot in enumerate((of_d, of_x, of_y, mine)):
+        go(x_ref.at[:, slot + flip], near.at[k], k, dev_c)
+
+    def add(k, slot, half):
+        return x_ref[half, slot].astype(F32) + near[k, half].astype(F32)
+
+    arrived(near.at[0], 0, dev_c)
+    part[0, 0] = add(0, of_d, 0).astype(BF16)
+    go(part.at[0, 0], diag.at[0], 4, dev_x)
+    part[0, 1] = add(0, of_d, 1).astype(BF16)
+    go(part.at[0, 1], diag.at[1], 5, dev_y)
+    arrived(near.at[1], 1, dev_c)
+    part[1, 0] = add(1, of_x, 0).astype(BF16)
+    go(part.at[1, 0], from_x.at[0], 6, dev_x)
+    arrived(near.at[2], 2, dev_c)
+    part[2, 1] = add(2, of_y, 1).astype(BF16)
+    go(part.at[2, 1], from_y.at[1], 7, dev_y)
+    arrived(diag.at[1], 5, dev_y)
+    part[1, 1] = (add(1, of_x, 1) + diag[1].astype(F32)).astype(BF16)
+    go(part.at[1, 1], from_x.at[1], 8, dev_x)
+    arrived(diag.at[0], 4, dev_x)
+    part[2, 0] = (add(2, of_y, 0) + diag[0].astype(F32)).astype(BF16)
+    go(part.at[2, 0], from_y.at[0], 9, dev_y)
+    arrived(near.at[3], 3, dev_c)
+    arrived(from_x.at[0], 6, dev_x)
+    arrived(from_y.at[1], 7, dev_y)
+    arrived(from_x.at[1], 8, dev_x)
+    arrived(from_y.at[0], 9, dev_y)
+    for half in range(2):
+        out_ref[half] = (
+            add(3, mine, half) + from_x[half].astype(F32) + from_y[half].astype(F32)
+        )
+    for copy in sent:
+        copy.wait_send()
+
+
+def plane_scatter(x, cid):
+    two, eight, rows, width = x.shape
+    (out,) = comm_call(
+        plane_scatter_kernel,
+        "plane_scatter",
+        [((2, rows, width), F32)],
+        [x],
+        [
+            ((4, 2, rows, width), BF16),
+            ((3, 2, rows, width), BF16),
+            ((2, rows, width), BF16),
+            ((2, rows, width), BF16),
+            ((2, rows, width), BF16),
+        ],
+        10,
+        cid,
+    )
+    return out
+
+
+def small_gather_kernel(n, x_ref, out_ref, sems):
+    h = lax.axis_index("head")
+    b = lax.axis_index("blk")
+    greet([(h, (b + k) % n) for k in range(1, n)])
+    copies = []
+    for k in range(1, n):
+        copy = remote(x_ref, out_ref.at[b], sems, k, (h, (b + k) % n))
+        copy.start()
+        copies.append(copy)
+    out_ref[pl.ds(b, 1)] = x_ref[...][None]
+    for copy in copies:
+        copy.wait()
+
+
+def small_gather(x, n, cid):
+    (out,) = comm_call(
+        functools.partial(small_gather_kernel, n),
+        "small_gather",
+        [((n,) + x.shape, x.dtype)],
+        [x],
+        [],
+        n,
+        cid,
+    )
+    return out
+
+
+def small_scatter_kernel(n, x_ref, out_ref, held, sems):
+    h = lax.axis_index("head")
+    b = lax.axis_index("blk")
+    others = [(h, (b + k) % n) for k in range(1, n)] + [(1 - h, (b + k) % n) for k in range(n)]
+    greet(others)
+    copies = []
+    for k, (to_h, to_b) in enumerate(others):
+        copy = remote(x_ref.at[to_b], held.at[k], sems, k, (to_h, to_b))
+        copy.start()
+        copies.append(copy)
+    for copy in copies:
+        copy.wait()
+    out_ref[...] = x_ref[b] + jnp.sum(held[...], axis=0)
+
+
+def small_scatter(x, n, cid):
+    (out,) = comm_call(
+        functools.partial(small_scatter_kernel, n),
+        "small_scatter",
+        [(x.shape[1:], F32)],
+        [x],
+        [((2 * n - 1,) + x.shape[1:], F32)],
+        2 * n - 1,
+        cid,
+    )
+    return out
+
+
+def weight_kernel(wu_ref, wd_ref, wo_ref, ou_ref, od_ref, oo_ref, usem, dsem, osem):
+    h = lax.axis_index("head")
+    b = lax.axis_index("blk")
+    o, g = b // 4, b % 4
+    greet([(h, (b + k) % 16) for k in range(1, 16)])
+    sent = []
+    for k in range(1, 16):
+        to = (b + k) % 16
+        copy = remote(wu_ref.at[to % 4], ou_ref.at[b], usem, k, (h, to))
+        copy.start()
+        sent.append(copy)
+    has = o // 2 == h
+    for k in range(1, 4):
+        to = (h, ((o + k) % 4) * 4 + g)
+
+        @pl.when(has)
+        def _():
+            remote(wo_ref, oo_ref.at[o % 2], osem, k, to).start()
+
+        copy = remote(wd_ref, od_ref.at[o], dsem, k, to)
+        copy.start()
+        sent.append(copy)
+    ou_ref[pl.ds(b, 1)] = wu_ref[pl.ds(g, 1)]
+    od_ref[pl.ds(o, 1)] = wd_ref[...][None]
+
+    @pl.when(has)
+    def _():
+        oo_ref[pl.ds(o % 2, 1)] = wo_ref[...][None]
+
+    for copy in sent:
+        copy.wait()
+    for k in range(1, 4):
+        source = (o + 4 - k) % 4
+
+        @pl.when(has)
+        def _():
+            remote(wo_ref, oo_ref.at[o % 2], osem, k, (h, b)).wait_send()
+
+        @pl.when(source // 2 == h)
+        def _():
+            remote(wo_ref, oo_ref.at[source % 2], osem, k, (h, b)).wait_recv()
+
+
+def weight_exchange(wu, wd, wo, cid):
+    return pl.pallas_call(
+        weight_kernel,
+        name="weight_exchange",
+        out_shape=[
+            jax.ShapeDtypeStruct((16,) + wu.shape[1:], BF16),
+            jax.ShapeDtypeStruct((4,) + wd.shape, BF16),
+            jax.ShapeDtypeStruct((2,) + wo.shape, BF16),
+        ],
+        in_specs=[VSPEC] * 3,
+        out_specs=[VSPEC] * 3,
+        scratch_shapes=[
+            pltpu.SemaphoreType.DMA((2, 16)),
+            pltpu.SemaphoreType.DMA((2, 4)),
+            pltpu.SemaphoreType.DMA((2, 4)),
+        ],
+        compiler_params=pltpu.CompilerParams(collective_id=cid, has_side_effects=True),
+    )(wu, wd, wo)
+
+
+def rows_kernel(x_ref, out_ref, near, part, from_y, part_z, from_z, csem, ysem, zsem):
+    h, o, y, c = place()
+    dev_y, dev_c = (h, blk(o, 1 - y, c)), (h, blk(o, y, 1 - c))
+    others = [(o + k) % 4 for k in range(1, 4)]
+    greet([dev_y, dev_c] + [(h, blk(z, y, c)) for z in others])
+    order = others + [o]
+    sent = []
+    for j, z in enumerate(order):
+        for i, yy in enumerate((1 - y, y)):
+            copy = remote(x_ref.at[z, yy, 1 - c], near.at[i, j], csem, i * 4 + j, dev_c)
+            copy.start()
+            sent.append(copy)
+    for j, z in enumerate(order):
+        remote(near.at[0, j], near.at[0, j], csem, j, dev_c).wait_recv()
+        part[j] = (x_ref[z, 1 - y, c].astype(F32) + near[0, j].astype(F32)).astype(BF16)
+        copy = remote(part.at[j], from_y.at[j], ysem, j, dev_y)
+        copy.start()
+        sent.append(copy)
+    for j, z in enumerate(order):
+        remote(near.at[1, j], near.at[1, j], csem, 4 + j, dev_c).wait_recv()
+        remote(from_y.at[j], from_y.at[j], ysem, j, dev_y).wait_recv()
+        total = x_ref[z, y, c].astype(F32) + near[1, j].astype(F32) + from_y[j].astype(F32)
+        part_z[j] = total.astype(BF16)
+        if j < 3:
+            copy = remote(part_z.at[j], from_z.at[j], zsem, j, (h, blk(z, y, c)))
+            copy.start()
+            sent.append(copy)
+    for j in range(3):
+        remote(from_z.at[j], from_z.at[j], zsem, j, (h, blk(o, y, c))).wait_recv()
+    out_ref[...] = part_z[3].astype(F32) + jnp.sum(from_z[...].astype(F32), axis=0)
+    for copy in sent:
+        copy.wait_send()
+
+
+def rows_scatter(x, cid):
+    rows, width = x.shape[3:]
+    block = (rows, width)
+    return pl.pallas_call(
+        rows_kernel,
+        name="rows_scatter",
+        out_shape=jax.ShapeDtypeStruct(block, F32),
+        in_specs=[VSPEC],
+        out_specs=VSPEC,
+        scratch_shapes=[
+            pltpu.VMEM((2, 4) + block, BF16),
+            pltpu.VMEM((4,) + block, BF16),
+            pltpu.VMEM((4,) + block, BF16),
+            pltpu.VMEM((4,) + block, BF16),
+            pltpu.VMEM((3,) + block, BF16),
+            pltpu.SemaphoreType.DMA((2, 8)),
+            pltpu.SemaphoreType.DMA((2, 4)),
+            pltpu.SemaphoreType.DMA((2, 3)),
+        ],
+        compiler_params=pltpu.CompilerParams(
+            collective_id=cid, has_side_effects=True, vmem_limit_bytes=48 << 20
+        ),
+    )(x)
+
+
+def blk_gather_kernel(x_ref, out_ref, zsem, ysem, csem):
+    h, o, y, c = place()
+    dev_y, dev_c = (h, blk(o, 1 - y, c)), (h, blk(o, y, 1 - c))
+    others = [(o + k) % 4 for k in range(1, 4)]
+    greet([dev_y, dev_c] + [(h, blk(z, y, c)) for z in others])
+    sent = []
+
+    def go(src, z, yy, sem, index, device):
+        copy = remote(src, out_ref.at[z, yy, c], sem, index, device)
+        copy.start()
+        sent.append(copy)
+
+    def arrived(z, yy, cc, sem, index):
+        ref = out_ref.at[z, yy, cc]
+        remote(ref, ref, sem, index, dev_c).wait_recv()
+
+    for j, z in enumerate(others):
+        go(x_ref, o, y, zsem, j, (h, blk(z, y, c)))
+    go(x_ref, o, y, ysem, 0, dev_y)
+    go(x_ref, o, y, csem, 0, dev_c)
+    out_ref[o, y, c] = x_ref[...]
+    froms = [(o + 4 - k) % 4 for k in range(1, 4)]
+    for j, z in enumerate(froms):
+        arrived(z, y, c, zsem, j)
+        go(out_ref.at[z, y, c], z, y, ysem, 1 + j, dev_y)
+        go(out_ref.at[z, y, c], z, y, csem, 1 + j, dev_c)
+    for j, z in enumerate([o] + froms):
+        arrived(z, 1 - y, c, ysem, j)
+        go(out_ref.at[z, 1 - y, c], z, 1 - y, csem, 4 + j, dev_c)
+    for j, z in enumerate([o] + froms):
+        arrived(z, y, 1 - c, csem, j)
+        arrived(z, 1 - y, 1 - c, csem, 4 + j)
+    for copy in sent:
+        copy.wait_send()
+
+
+def blk_gather(x, cid):
+    return pl.pallas_call(
+        blk_gather_kernel,
+        name="blk_gather",
+        out_shape=jax.ShapeDtypeStruct((4, 2, 2) + x.shape, x.dtype),
+        in_specs=[VSPEC],
+        out_specs=VSPEC,
+        scratch_shapes=[
+            pltpu.SemaphoreType.DMA((2, 3)),
+            pltpu.SemaphoreType.DMA((2, 4)),
+            pltpu.SemaphoreType.DMA((2, 8)),
+        ],
+        compiler_params=pltpu.CompilerParams(collective_id=cid, has_side_effects=True),
+    )(x)
+
+
+def to_pairs_kernel(rows, cols, x_ref, out_ref, sems):
+    h = lax.axis_index("head")
+    b = lax.axis_index("blk")
+    o, g = b // 4, b % 4
+    greet([(h, ((o + k) % 4) * 4 + g) for k in range(1, 4)])
+
+    def block(z):
+        s, j = z // 2, z % 2
+        return x_ref.at[pl.ds(j * rows, rows), pl.ds(s * cols, cols)]
+
+    copies = []
+    for k in range(1, 4):
+        to = (o + k) % 4
+        copy = remote(block(to), out_ref.at[:, pl.ds(o * cols, cols)], sems, k, (h, to * 4 + g))
+        copy.start()
+        copies.append(copy)
+    out_ref[:, pl.ds(o * cols, cols)] = block(o)[...]
+    for copy in copies:
+        copy.wait()
+
+
+def to_pairs(x, cid):
+    rows, cols = x.shape[0] // 2, x.shape[1] // 2
+    (out,) = comm_call(
+        functools.partial(to_pairs_kernel, rows, cols),
+        "to_pairs",
+        [((rows, 4 * cols), x.dtype)],
+        [x],
+        [],
+        4,
+        cid,
+    )
+    return out
+
+
+def from_pairs_kernel(rows, cols, x_ref, out_ref, sems):
+    h = lax.axis_index("head")
+    b = lax.axis_index("blk")
+    o, g = b // 4, b % 4
+    greet([(h, ((o + k) % 4) * 4 + g) for k in range(1, 4)])
+    s, j = o // 2, o % 2
+
+    def spot():
+        return out_ref.at[pl.ds(j * rows, rows), pl.ds(s * cols, cols)]
+
+    copies = []
+    for k in range(1, 4):
+        to = (o + k) % 4
+        copy = remote(x_ref.at[:, pl.ds(to * cols, cols)], spot(), sems, k, (h, to * 4 + g))
+        copy.start()
+        copies.append(copy)
+    out_ref[pl.ds(j * rows, rows), pl.ds(s * cols, cols)] = x_ref[:, pl.ds(o * cols, cols)]
+    for copy in copies:
+        copy.wait()
+
+
+def from_pairs(x, cid):
+    rows, cols = x.shape[0], x.shape[1] // 4
+    (out,) = comm_call(
+        functools.partial(from_pairs_kernel, rows, cols),
+        "from_pairs",
+        [((2 * rows, 2 * cols), x.dtype)],
+        [x],
+        [],
+        4,
+        cid,
+    )
+    return out
+
+
+def grad_kernel(
+    gu_ref, gd_ref, go_ref, ou_ref, od_ref, oo_ref, ru, rd, ro, su, zsem, dsem, osem, usem, xsem
+):
+    h, o, y, c = place()
+    g = y * 2 + c
+    t = h * 4 + g
+    plane = [((t + k) % 8 // 4, o * 4 + (t + k) % 4) for k in range(1, 8)]
+    others = [(o + k) % 4 for k in range(1, 4)]
+    greet(plane + [(h, z * 4 + g) for z in others])
+    dev_x = (1 - h, o * 4 + g)
+    has = o // 2 == h
+    sent = []
+    for k, z in enumerate(others):
+        for src, dst, sem in ((gu_ref, ru, zsem), (gd_ref, rd, dsem)):
+            copy = remote(src.at[z], dst.at[k], sem, k, (h, z * 4 + g))
+            copy.start()
+            sent.append(copy)
+
+        @pl.when(z // 2 == h)
+        def _():
+            remote(go_ref.at[z % 2], ro.at[k], osem, k, (h, z * 4 + g)).start()
+
+    for k in range(3):
+        remote(ru.at[k], ru.at[k], zsem, k, dev_x).wait_recv()
+    su[...] = (gu_ref[o].astype(F32) + jnp.sum(ru[...].astype(F32), axis=0)).astype(BF16)
+    for k, (to_h, to_b) in enumerate(plane):
+        copy = remote(su.at[to_b % 4], ou_ref.at[t], usem, k, (to_h, to_b))
+        copy.start()
+        sent.append(copy)
+    ou_ref[pl.ds(t, 1)] = su[pl.ds(g, 1)]
+    for k in range(3):
+        remote(rd.at[k], rd.at[k], dsem, k, dev_x).wait_recv()
+    od_ref[h] = (gd_ref[o].astype(F32) + jnp.sum(rd[...].astype(F32), axis=0)).astype(BF16)
+    copy = remote(od_ref.at[h], od_ref.at[h], xsem, 0, dev_x)
+    copy.start()
+    sent.append(copy)
+
+    @pl.when(has)
+    def _():
+        for k in range(3):
+            remote(ro.at[k], ro.at[k], osem, k, dev_x).wait_recv()
+        oo_ref[...] = (go_ref[o % 2].astype(F32) + jnp.sum(ro[...].astype(F32), axis=0)).astype(
+            BF16
+        )
+        remote(oo_ref, oo_ref, xsem, 1, dev_x).start()
+        remote(oo_ref, oo_ref, xsem, 1, dev_x).wait_send()
+
+    @pl.when(jnp.logical_not(has))
+    def _():
+        remote(oo_ref, oo_ref, xsem, 1, dev_x).wait_recv()
+
+    for k, z in enumerate(others):
+
+        @pl.when(z // 2 == h)
+        def _():
+            remote(go_ref.at[z % 2], ro.at[k], osem, k, dev_x).wait_send()
+
+    for k in range(7):
+        source = (t + 7 - k) % 8
+        remote(su.at[0], ou_ref.at[source], usem, k, dev_x).wait_recv()
+    remote(od_ref.at[1 - h], od_ref.at[1 - h], xsem, 0, dev_x).wait_recv()
+    for copy in sent:
+        copy.wait_send()
+
+
+def grad_exchange(gu, gd, go, cid):
+    ublock, dblock, oblock = gu.shape[1:], gd.shape[1:], go.shape[1:]
+    return pl.pallas_call(
+        grad_kernel,
+        name="grad_exchange",
+        out_shape=[
+            jax.ShapeDtypeStruct((8,) + ublock[1:], BF16),
+            jax.ShapeDtypeStruct((2,) + dblock, BF16),
+            jax.ShapeDtypeStruct(oblock, BF16),
+        ],
+        in_specs=[VSPEC] * 3,
+        out_specs=[VSPEC] * 3,
+        scratch_shapes=[
+            pltpu.VMEM((3,) + ublock, BF16),
+            pltpu.VMEM((3,) + dblock, BF16),
+            pltpu.VMEM((3,) + oblock, BF16),
+            pltpu.VMEM(ublock, BF16),
+            pltpu.SemaphoreType.DMA((2, 3)),
+            pltpu.SemaphoreType.DMA((2, 3)),
+            pltpu.SemaphoreType.DMA((2, 3)),
+            pltpu.SemaphoreType.DMA((2, 7)),
+            pltpu.SemaphoreType.DMA((2, 2)),
+        ],
+        compiler_params=pltpu.CompilerParams(collective_id=cid, has_side_effects=True),
+    )(gu, gd, go)
+
+
+def pair_sum_kernel(x_ref, out_ref, held, sems):
+    h = lax.axis_index("head")
+    b = lax.axis_index("blk")
+    dev_x = (1 - h, b)
+    greet([dev_x])
+    pieces = x_ref.shape[0]
+    copies = [remote(x_ref.at[k], held.at[k], sems, k, dev_x) for k in range(pieces)]
+    for copy in copies:
+        copy.start()
+    for k, copy in enumerate(copies):
+        copy.wait()
+        out_ref[k] = x_ref[k].astype(F32) + held[k].astype(F32)
+
+
+def pair_sum(x, cid):
+    (out,) = comm_call(
+        pair_sum_kernel, "pair_sum", [(x.shape, F32)], [x], [(x.shape, BF16)], x.shape[0], cid
+    )
+    return out
+
+
+def attend_kernel(scale, x_ref, o_ref, low_ref, lse_ref, keys):
+    e = o_ref.shape[0]
+    step = pl.program_id(0)
+    cols = o_ref.shape[1]
+
+    @pl.when(step == 0)
+    def _():
+        keys[...] = x_ref[e : 2 * e].astype(F32).T.astype(BF16)
+
+    q = (x_ref[0:e, pl.ds(pl.multiple_of(step * cols, cols), cols)].astype(F32) * scale).astype(
+        BF16
+    )
+    s = jnp.dot(keys[...], q, preferred_element_type=F32)
+    peak = jnp.max(s, axis=0, keepdims=True)
+    p = jnp.exp(s - peak)
+    total = jnp.sum(p, axis=0, keepdims=True)
+    o = jnp.dot(x_ref[2 * e : 3 * e], p.astype(BF16), preferred_element_type=F32) / total
+    o_ref[...] = o
+    low_ref[...] = o.astype(BF16)
+    lse_ref[...] = peak + jnp.log(total)
+
+
+def attend(x, scale, cols=256):
+    rows, length = x.shape
+    e = rows // 3
+    return pl.pallas_call(
+        functools.partial(attend_kernel, scale),
+        name="attend",
+        grid=(length // cols,),
+        out_shape=[
+            jax.ShapeDtypeStruct((e, length), F32),
+            jax.ShapeDtypeStruct((e, length), BF16),
+            jax.ShapeDtypeStruct((1, length), F32),
+        ],
+        in_specs=[pl.BlockSpec((rows, length), lambda i: (0, 0))],
+        out_specs=[
+            pl.BlockSpec((e, cols), lambda i: (0, i)),
+            pl.BlockSpec((e, cols), lambda i: (0, i)),
+            pl.BlockSpec((1, cols), lambda i: (0, i)),
+        ],
+        scratch_shapes=[pltpu.VMEM((length, e), BF16)],
+        compiler_params=pltpu.CompilerParams(vmem_limit_bytes=48 << 20),
+    )(x)
+
+
+def attend_back_kernel(scale, x_ref, g_ref, o_ref, lse_ref, out_ref, keys, values, dk, dv):
+    e = o_ref.shape[0]
+    step = pl.program_id(0)
+    cols = o_ref.shape[1]
+
+    @pl.when(step == 0)
+    def _():
+        keys[...] = x_ref[e : 2 * e].astype(F32).T.astype(BF16)
+        values[...] = x_ref[2 * e : 3 * e].astype(F32).T.astype(BF16)
+        dk[...] = jnp.zeros_like(dk)
+        dv[...] = jnp.zeros_like(dv)
+
+    here = pl.ds(pl.multiple_of(step * cols, cols), cols)
+    q32 = x_ref[0:e, here].astype(F32) * scale
+    q = q32.astype(BF16)
+    g32 = g_ref[...].astype(F32)
+    delta = jnp.sum(g32 * o_ref[...], axis=0, keepdims=True)
+    s = jnp.dot(keys[...], q, preferred_element_type=F32)
+    p = jnp.exp(s - lse_ref[...])
+    dv[...] += jnp.dot(p.astype(BF16), g32.T.astype(BF16), preferred_element_type=F32)
+    dp = jnp.dot(values[...], g_ref[...], preferred_element_type=F32)
+    ds = (p * (dp - delta)).astype(BF16)
+    dk[...] += jnp.dot(ds, q32.T.astype(BF16), preferred_element_type=F32)
+    dq = jnp.dot(x_ref[e : 2 * e], ds, preferred_element_type=F32) * scale
+    out_ref[0:e, here] = dq.astype(BF16)
+
+    @pl.when(step == pl.num_programs(0) - 1)
+    def _():
+        out_ref[e : 2 * e] = dk[...].T.astype(BF16)
+        out_ref[2 * e : 3 * e] = dv[...].T.astype(BF16)
+
+
+def attend_back(x, g, o, lse, scale, cols=256):
+    rows, length = x.shape
+    e = rows // 3
+    return pl.pallas_call(
+        functools.partial(attend_back_kernel, scale),
+        name="attend_back",
+        grid=(length // cols,),
+        out_shape=jax.ShapeDtypeStruct((rows, length), BF16),
+        in_specs=[
+            pl.BlockSpec((rows, length), lambda i: (0, 0)),
+            pl.BlockSpec((e, cols), lambda i: (0, i)),
+            pl.BlockSpec((e, cols), lambda i: (0, i)),
+            pl.BlockSpec((1, cols), lambda i: (0, i)),
+        ],
+        out_specs=pl.BlockSpec((rows, length), lambda i: (0, 0)),
+        scratch_shapes=[
+            pltpu.VMEM((length, e), BF16),
+            pltpu.VMEM((length, e), BF16),
+            pltpu.VMEM((length, e), F32),
+            pltpu.VMEM((length, e), F32),
+        ],
+        compiler_params=pltpu.CompilerParams(vmem_limit_bytes=48 << 20),
+    )(x, g, o, lse)
 
 
 def norm_layer(values_in, gain_row, offset_row):
@@ -153,7 +846,7 @@
     return fold_queries
 
 
-def on_device(
+def layer_in_blocks(
     hidden,
     pos_ids,
     type_ids,
@@ -450,6 +1143,240 @@
     )
 
 
+def layer_in_planes(
+    hidden,
+    pos_ids,
+    type_ids,
+    cotangent,
+    pos_table,
+    type_table,
+    query_key_value_weight,
+    attention_output_weight,
+    up_projection_weight,
+    down_projection_weight,
+    up_projection_bias,
+    norm_gains,
+    biases,
+):
+    seqs, seg, width = hidden.shape
+    blks = lax.axis_size("blk")
+    h = lax.axis_index("head")
+    b = lax.axis_index("blk")
+    o, g = b // 4, b % 4
+    rows = seqs * seg
+    e = width // HEADS
+    ff = up_projection_weight.shape[1]
+    scale = 1.0 / math.sqrt(e)
+    slots = pos_table.shape[0]
+    fcols = ff // blks // 2
+    plane_rows = 8 * rows
+
+    small = jnp.concatenate(
+        [
+            biases.astype(F32),
+            norm_gains.astype(F32),
+            type_table.astype(F32),
+            up_projection_bias.astype(F32).reshape(4, e),
+        ]
+    ).reshape(7, 2 * e)
+    packed = jnp.concatenate([small, pos_ids.astype(F32).reshape(1, rows)])
+    everyone = small_gather(packed, blks, 0)
+    params = everyone[:, :7].reshape(blks, 14, e).transpose(1, 0, 2)
+    vectors = params[:10].reshape(10, width)
+    bias_float, gain_float, type_float = vectors[:6], vectors[6:8], vectors[8:10]
+    up_bias = lax.dynamic_slice_in_dim(
+        params[10:].transpose(1, 0, 2).reshape(4, 4, 2, fcols), h, 1, 2
+    )
+    up_bias = lax.dynamic_slice_in_dim(up_bias, g, 1, 1).reshape(1, 4 * fcols)
+    all_ids = everyone[:, 7].astype(jnp.int32)
+
+    qkv_cut = query_key_value_weight.reshape(e, 3, 2, 2, 4, e)
+    qkv_cut = lax.dynamic_slice_in_dim(qkv_cut, h, 1, 2).reshape(e, 3, 2, 4, e)
+    qkv_cut = qkv_cut.transpose(3, 0, 2, 1, 4).reshape(4, e, 6 * e)
+    up_cut = up_projection_weight.reshape(e, 4, 4, 2, fcols)
+    up_cut = lax.dynamic_slice_in_dim(up_cut, h, 1, 3).reshape(e, 4, 4, fcols)
+    up_cut = up_cut.transpose(2, 0, 1, 3).reshape(4, e, 4 * fcols)
+    down_cut = lax.dynamic_slice_in_dim(down_projection_weight, h * fcols, fcols, 0)
+    wide, down_all, out_all = weight_exchange(
+        jnp.concatenate([qkv_cut, up_cut], axis=2), down_cut, attention_output_weight, 1
+    )
+    qkv_own = wide[:, :, : 6 * e].reshape(width, 6 * e)
+    up_own = wide[:, :, 6 * e :].reshape(width, 4 * fcols)
+    down_own = down_all.reshape(4 * fcols, width)
+    out_own = out_all.reshape(2 * e, width)
+
+    local_ids = all_ids.reshape(blks * rows, 1) - b * slots
+    onehot = (local_ids == lax.broadcasted_iota(jnp.int32, (1, slots), 1)).astype(BF16)
+    found = jnp.dot(onehot, pos_table, preferred_element_type=F32).astype(BF16)
+    positions = rows_scatter(found.reshape(4, 2, 2, rows, width), 2)
+    is_second = type_ids.reshape(rows, 1) == 1
+    typed = jnp.where(is_second, type_float[1], type_float[0])
+    embedded = hidden.reshape(rows, width).astype(F32) + positions + typed
+    token_shape = (seqs, seg, width)
+
+    plane_low = plane_gather(embedded.astype(BF16).reshape(token_shape), 3).reshape(
+        plane_rows, width
+    )
+    bias_heads = bias_float.reshape(6, 2, 2, 4, e)
+    bias_heads = lax.dynamic_slice_in_dim(bias_heads, h, 1, 1)
+    bias_heads = lax.dynamic_slice_in_dim(bias_heads, g, 1, 3).reshape(6, 2, e)
+    qkv_bias = jnp.stack(
+        [bias_heads[0], jnp.zeros_like(bias_heads[0]), bias_heads[1]], axis=1
+    ).reshape(6 * e, 1)
+    projected = (
+        jnp.einsum("kf,rk->fr", qkv_own, plane_low, preferred_element_type=F32) + qkv_bias
+    ).astype(BF16)
+    pair_qkv = to_pairs(projected, 4)
+    pair_out, pair_low, lse = attend(pair_qkv, scale)
+    attended = from_pairs(pair_low, 5)
+    branch = jnp.einsum("fr,fd->rd", attended, out_own, preferred_element_type=F32).astype(BF16)
+    branch = plane_scatter(branch.reshape(seqs, 8, seg, width), 6).reshape(rows, width)
+    first, first_pull = jax.vjp(
+        norm_layer, embedded + (branch + bias_float[2]), gain_float[0], bias_float[3]
+    )
+
+    first_low = plane_gather(first.astype(BF16).reshape(token_shape), 3).reshape(plane_rows, width)
+    inner = jnp.dot(first_low, up_own, preferred_element_type=F32) + up_bias
+    activated, gelu_pull = jax.vjp(gelu_exact, inner)
+    activated_low = activated.astype(BF16)
+    second = jnp.dot(activated_low, down_own, preferred_element_type=F32).astype(BF16)
+    second = plane_scatter(second.reshape(seqs, 8, seg, width), 6).reshape(rows, width)
+    final, final_pull = jax.vjp(
+        norm_layer, first + (second + bias_float[4]), gain_float[1], bias_float[5]
+    )
+    layer_out = final.astype(BF16).reshape(token_shape)
+
+    grad_final, grad_gain_two, grad_shift_two = final_pull(
+        cotangent.reshape(rows, width).astype(F32)
+    )
+    grad_low = grad_final.astype(BF16)
+    grad_bias_second = jnp.sum(grad_low.astype(F32), axis=0)
+    plane_grad = plane_gather(grad_low.reshape(token_shape), 3).reshape(plane_rows, width)
+    grad_down = jnp.einsum(
+        "rf,rd->fd", activated_low, plane_grad, preferred_element_type=F32
+    ).astype(BF16)
+    (grad_inner,) = gelu_pull(
+        jnp.einsum("rd,fd->rf", plane_grad, down_own, preferred_element_type=F32)
+    )
+    grad_inner_low = grad_inner.astype(BF16)
+    grad_up = jnp.einsum(
+        "rd,rf->df", first_low, grad_inner_low, preferred_element_type=F32
+    ).astype(BF16)
+    grad_up_bias = jnp.sum(grad_inner_low.astype(F32), axis=0)
+    grad_first = jnp.einsum(
+        "rf,df->rd", grad_inner_low, up_own, preferred_element_type=F32
+    ).astype(BF16)
+    grad_first = plane_scatter(grad_first.reshape(seqs, 8, seg, width), 6).reshape(rows, width)
+    grad_resid, grad_gain_one, grad_shift_one = first_pull(grad_final + grad_first)
+    branch_low = grad_resid.astype(BF16)
+    grad_bias_branch = jnp.sum(branch_low.astype(F32), axis=0)
+    plane_branch = plane_gather(branch_low.reshape(token_shape), 3).reshape(plane_rows, width)
+    grad_out = jnp.einsum(
+        "fr,rd->fd", attended, plane_branch, preferred_element_type=F32
+    ).astype(BF16)
+    grad_attended = jnp.einsum(
+        "fd,rd->fr", out_own, plane_branch, preferred_element_type=F32
+    ).astype(BF16)
+    pair_grad = to_pairs(grad_attended, 7)
+    pair_dqkv = attend_back(pair_qkv, pair_grad, pair_out, lse, scale)
+    grad_qkv = from_pairs(pair_dqkv, 8)
+    grad_qkv_weight = jnp.einsum(
+        "rk,fr->kf", plane_low, grad_qkv, preferred_element_type=F32
+    ).astype(BF16)
+    head_sums = jnp.sum(grad_qkv.astype(F32), axis=1).reshape(2, 3, e)
+    back = jnp.einsum("fr,kf->rk", grad_qkv, qkv_own, preferred_element_type=F32).astype(BF16)
+    back = plane_scatter(back.reshape(seqs, 8, seg, width), 6).reshape(rows, width)
+    grad_embedded = grad_resid + back
+    grad_hidden = grad_embedded.reshape(token_shape)
+
+    all_grads = blk_gather(grad_embedded.astype(BF16), 9).reshape(blks * rows, width)
+    flat_ids = all_ids.reshape(1, blks * rows) - b * slots
+    pick = (flat_ids == lax.broadcasted_iota(jnp.int32, (slots, 1), 0)).astype(BF16)
+    pos_part = jnp.dot(pick, all_grads, preferred_element_type=F32).astype(BF16)
+    total_pos = pair_sum(pos_part.reshape(8, slots // 8, width), 10).reshape(slots, width)
+
+    got_wide, got_down, got_out = grad_exchange(
+        jnp.concatenate([grad_qkv_weight, grad_up], axis=1).reshape(4, 4, e, 6 * e + 4 * fcols),
+        grad_down.reshape(4, fcols, width),
+        grad_out.reshape(2, e, width),
+        11,
+    )
+    total_qkv = (
+        got_wide[:, :, : 6 * e]
+        .reshape(2, 4, e, 2, 3, e)
+        .transpose(2, 4, 0, 3, 1, 5)
+        .reshape(e, 3 * width)
+        .astype(F32)
+    )
+    total_up = (
+        got_wide[:, :, 6 * e :]
+        .reshape(2, 4, e, 4, fcols)
+        .transpose(2, 3, 1, 0, 4)
+        .reshape(e, ff)
+        .astype(F32)
+    )
+    total_down = got_down.reshape(2 * fcols, width).astype(F32)
+    total_out = got_out.astype(F32)
+
+    second_mask = is_second.astype(F32)
+    type_one = jnp.sum(grad_embedded * second_mask, axis=0)
+    type_zero = jnp.sum(grad_embedded * (1.0 - second_mask), axis=0)
+
+    def spread(part):
+        whole = jnp.zeros((1, 2, 4, e), F32)
+        whole = lax.dynamic_update_slice(
+            jnp.zeros((2, 2, 4, e), F32), part.reshape(1, 2, 1, e), (h, 0, g, 0)
+        )
+        return whole.reshape(width)
+
+    stacked = jnp.stack(
+        [
+            spread(head_sums[:, 0]),
+            spread(head_sums[:, 2]),
+            grad_bias_branch,
+            grad_shift_one,
+            grad_bias_second,
+            grad_shift_two,
+            grad_gain_one,
+            grad_gain_two,
+            type_zero,
+            type_one,
+        ]
+    )
+    up_spread = lax.dynamic_update_slice(
+        jnp.zeros((4, 4, 2, fcols), F32), grad_up_bias.reshape(4, 1, 1, fcols), (0, g, h, 0)
+    ).reshape(blks, 4, e)
+    vector_pack = jnp.concatenate(
+        [stacked.reshape(10, blks, e).transpose(1, 0, 2), up_spread], axis=1
+    ).reshape(blks, 7, 2 * e)
+    vector_pack = jnp.pad(vector_pack, ((0, 0), (0, 1), (0, 0)))
+    totals = small_scatter(vector_pack, blks, 12)[:7].reshape(14, e)
+    return (
+        layer_out,
+        grad_hidden,
+        total_pos,
+        totals[8:10],
+        total_qkv,
+        total_out,
+        total_up,
+        total_down,
+        totals[10:14].reshape(4 * e),
+        totals[6:8],
+        totals[:6],
+    )
+
+
+def planes_fit(hidden, head_axis, blk_axis):
+    seqs, seg, width = hidden.shape
+    return head_axis == 2 and blk_axis == HEADS and seqs == 2 and seqs * seg == 2 * width // HEADS
+
+
+def on_device(hidden, *rest):
+    if planes_fit(hidden, lax.axis_size("head"), lax.axis_size("blk")):
+        return layer_in_planes(hidden, *rest)
+    return layer_in_blocks(hidden, *rest)
+
+
 def solution(mesh):
     in_specs = (
         P(None, ("head", "blk"), None),

time: 1850 us -> 623 us (0.34)
  waiting for transfers between devices: 1300 us -> 0 us
  Pallas kernels: 0 us -> 507 us
  blocking collectives: 212 us -> 0 us
  matrix products: 155 us -> 48.2 us
  local copies, waits for them, and re-layouts: 115 us -> 38.6 us
  starting transfers between devices: 19.4 us -> 0 us
    reduce_scatter x5 -> x0, waiting for transfers between devices: 720 us -> none  [the longest x1 334 us: on_device(): lax.psum_scatter(buffer[:length], 'blk', scatter_dimension=0, tiled=True)]
    pallas_call x0 -> x21, Pallas kernels: none -> 507 us  [the longest x15 258 us: comm_call(): pl.pallas_call(kernel, name=name, out_shape=[jax.ShapeDtypeStruct(s, d) f...]
    all_gather x9 -> x0, waiting for transfers between devices: 322 us -> none  [the longest x1 105 us: on_device(): portion = lax.all_gather(pos_table, 'blk', axis=0, tiled=True)]
    psum x1 -> x0, waiting for transfers between devices: 126 us -> none  [on_device(): lax.psum((shard_qkv, shard_out, shard_up, shard_down, shard_up_bias, shar...]
    all_gather x6 -> x0, blocking collectives: 120 us -> none  [the longest x1 23.7 us: fetch_weights(): lax.all_gather(type_table, 'blk', axis=1, tiled=True)]
    unnamed x21 -> x0, waiting for transfers between devices: 118 us -> none
    dot_general x41 -> x14, matrix products: 155 us -> 48.2 us  [the longest x1 7.13 us: layer_in_planes(): inner = jnp.dot(first_low, up_own, preferred_element_type=F32) + up_bias]
    unnamed x1 -> x0, blocking collectives: 59.7 us -> none
  transfers between devices with their start and end apart: 23 -> 0, of which waited for: 15 -> 0; matrix products, arithmetic and copies ran while one was open for 15% -> 0% of each run, Pallas kernels for 0% -> 0%
where the time goes in v1:
time: 623 us; the launch traced here: 616 us
  Pallas kernels  507 us (81%)
  matrix products  48.2 us (8%)
  local copies, waits for them, and re-layouts  38.6 us (6%)
  other arithmetic  20.8 us (3%)
    pallas_call x15, Pallas kernels, comm_call(): pl.pallas_call(kernel, name=name, out_shape=[jax.ShapeDtypeStruct(s, d) f...  258 us
    pallas_call x1, Pallas kernels, grad_exchange(): pl.pallas_call(grad_kernel, name='grad_exchange', out_shape=[jax.ShapeDty...  72 us
    pallas_call x1, Pallas kernels, weight_exchange(): pl.pallas_call(weight_kernel, name='weight_exchange', out_shape=[jax.Shap...  65.5 us
    pallas_call x1, Pallas kernels, rows_scatter(): pl.pallas_call(rows_kernel, name='rows_scatter', out_shape=jax.ShapeDtype...  50.9 us
    pallas_call x1, Pallas kernels, blk_gather(): pl.pallas_call(blk_gather_kernel, name='blk_gather', out_shape=jax.ShapeD...  37.8 us

profile of v1, /device:TPU:0, one launch (start us, length us, event | category | flops | bytes accessed | tf_op | source)
XLA Modules:
  0.0 616.0 jit_solution(7983616284228131412)
XLA Ops:
  3.7 10.2 %small_gather.1 = f32[16,8,128]{2,1,0:T(8,128)} custom-call(f32[8,128]{1,0:T(8,128)} %pad_maximum_fusion.3.x_ref), custom_call_target="tpu_custom_call" | custom-call | tf_op jit(solution)/shard_map/small_gather/pallas_call | solution.py:47
  15.1 1.5 reshape.351
  20.2 65.5 %weight_exchange.1 = (bf16[16,64,896]{2,1,0:T(8,128)(2,1)}, bf16[4,128,1024]{2,1,0:T(8,128)(2,1)}, bf16[2,64,1024]{2,1,0:T(8,128)(2,1)}) custom-call(bf16[4,64,896]{2,1,0:T(8,128)(2,1)} %pad_maximum_fusion.1.wu_ref, bf16[128,1024]{1,0:T(8,128)(2,1)} %constant_dynamic-slice_fusion.3.wd_ref, bf16[64,1024]{1,0:T(8,128)(2,1)} %wo_ref.1), custom_call_target="tpu_custom_call" | custom-call | tf_op jit(solution)/shard_map/weight_exchange/pallas_call | solution.py:289
  88.8 2.6 fusion.2
  91.4 50.9 %rows_scatter.1 = f32[128,1024]{1,0:T(8,128)S(1)} custom-call(bf16[4,2,2,128,1024]{4,3,2,1,0:T(8,128)(2,1)S(1)} %bitcast.125), custom_call_target="tpu_custom_call" | custom-call | tf_op jit(solution)/shard_map/rows_scatter/pallas_call | solution.py:345
  143.3 16.6 %plane_gather.4 = bf16[2,8,64,1024]{3,2,1,0:T(8,128)(2,1)} custom-call(bf16[2,64,1024]{2,1,0:T(8,128)(2,1)} %bitcast.156), custom_call_target="tpu_custom_call" | custom-call | tf_op jit(solution)/shard_map/plane_gather/pallas_call | solution.py:47
  159.9 3.5 add_convert_fusion.1.x_ref
  163.4 19.6 %to_pairs.2.x_ref = bf16[192,2048]{1,0:T(8,128)(2,1)} custom-call(bf16[384,1024]{1,0:T(8,128)(2,1)} %add_convert_fusion.1.x_ref), custom_call_target="tpu_custom_call" | custom-call | tf_op jit(solution)/shard_map/to_pairs/pallas_call | solution.py:47
  184.2 10.3 %attend.1 = (f32[64,2048]{1,0:T(8,128)S(1)}, bf16[64,2048]{1,0:T(8,128)(2,1)S(1)}, f32[1,2048]{1,0:T(1,128)S(1)}) custom-call(bf16[192,2048]{1,0:T(8,128)(2,1)S(1)} %copy-done.2), custom_call_target="tpu_custom_call" | custom-call | tf_op jit(solution)/shard_map/attend/pallas_call | solution.py:627
  195.2 12.7 %from_pairs.2 = bf16[128,1024]{1,0:T(8,128)(2,1)} custom-call(bf16[64,2048]{1,0:T(8,128)(2,1)} %copy-done.6), custom_call_target="tpu_custom_call" | custom-call | tf_op jit(solution)/shard_map/from_pairs/pallas_call | solution.py:47
  207.9 3.0 convolution_convert_fusion.3
  210.9 15.1 %plane_scatter.4 = f32[2,64,1024]{2,1,0:T(8,128)} custom-call(bf16[2,8,64,1024]{3,2,1,0:T(8,128)(2,1)} %bitcast.128), custom_call_target="tpu_custom_call" | custom-call | tf_op jit(solution)/shard_map/plane_scatter/pallas_call | solution.py:47
  226.1 1.3 fusion.28
  228.7 15.7 %plane_gather.5 = bf16[2,8,64,1024]{3,2,1,0:T(8,128)(2,1)} custom-call(bf16[2,64,1024]{2,1,0:T(8,128)(2,1)} %bitcast.151), custom_call_target="tpu_custom_call" | custom-call | tf_op jit(solution)/shard_map/plane_gather/pallas_call | solution.py:47
  244.7 1.8 copy-done.15
  246.5 7.1 %multiply_convert_fusion = (bf16[1024,512]{1,0:T(8,128)(2,1)S(1)}, f32[1024,512]{1,0:T(8,128)}, f32[1024,512]{1,0:T(8,128)}) fusion(f32[512]{0:T(512)S(1)} %bitcast.173, bf16[1024,1024]{1,0:T(8,128)(2,1)S(1)} %bitcast.143, bf16[1024,512]{1,0:T(8,128)(2,1)S(1)} %bitcast.152), kind=kOutput, calls=%fused_computation.10 | convolution fusion | flops 1108344832 | bytes 8390656 | tf_op jit(solution)/shard_map/dot_general | solution.py:1239
  253.6 2.6 convolution_convert_fusion.2
  256.3 15.7 %plane_scatter.5 = f32[2,64,1024]{2,1,0:T(8,128)} custom-call(bf16[2,8,64,1024]{3,2,1,0:T(8,128)(2,1)} %bitcast.139), custom_call_target="tpu_custom_call" | custom-call | tf_op jit(solution)/shard_map/plane_scatter/pallas_call | solution.py:47
  272.0 1.3 fusion.25
  275.8 15.7 %plane_gather.6 = bf16[2,8,64,1024]{3,2,1,0:T(8,128)(2,1)} custom-call(bf16[2,64,1024]{2,1,0:T(8,128)(2,1)} %bitcast.154), custom_call_target="tpu_custom_call" | custom-call | tf_op jit(solution)/shard_map/plane_gather/pallas_call | solution.py:47
  291.6 4.1 convolution_convert_fusion.4
  295.7 5.0 convert_reduce_fusion
  300.6 2.3 convolution_convert_fusion.5
  302.9 2.6 convolution_convert_fusion.1
  305.6 15.6 %plane_scatter.6 = f32[2,64,1024]{2,1,0:T(8,128)} custom-call(bf16[2,8,64,1024]{3,2,1,0:T(8,128)(2,1)} %bitcast.137), custom_call_target="tpu_custom_call" | custom-call | tf_op jit(solution)/shard_map/plane_scatter/pallas_call | solution.py:47
  321.2 1.4 multiply_reduce_fusion.2
  323.6 1.4 convert_reduce_fusion.4
  325.0 15.5 %plane_gather.7 = bf16[2,8,64,1024]{3,2,1,0:T(8,128)(2,1)} custom-call(bf16[2,64,1024]{2,1,0:T(8,128)(2,1)} %bitcast.155), custom_call_target="tpu_custom_call" | custom-call | tf_op jit(solution)/shard_map/plane_gather/pallas_call | solution.py:47
  340.6 3.2 convolution_convert_fusion.8.x_ref
  343.8 11.0 %to_pairs.3.g_ref = bf16[64,2048]{1,0:T(8,128)(2,1)} custom-call(bf16[128,1024]{1,0:T(8,128)(2,1)} %convolution_convert_fusion.8.x_ref), custom_call_target="tpu_custom_call" | custom-call | tf_op jit(solution)/shard_map/to_pairs/pallas_call | solution.py:47
  355.7 12.4 %attend_back.1.x_ref = bf16[192,2048]{1,0:T(8,128)(2,1)S(1)} custom-call(bf16[192,2048]{1,0:T(8,128)(2,1)S(1)} %copy-done.3, bf16[64,2048]{1,0:T(8,128)(2,1)S(1)} %copy-done.5, f32[64,2048]{1,0:T(8,128)S(1)} %get-tuple-element.24.o_ref, f32[1,2048]{1,0:T(1,128)S(1)} %get-tuple-element.25.lse_ref), custom_call_target="tpu_custom_call" | custom-call | tf_op jit(solution)/shard_map/attend_back/pallas_call | solution.py:682
  369.1 19.6 %from_pairs.3 = bf16[384,1024]{1,0:T(8,128)(2,1)} custom-call(bf16[192,2048]{1,0:T(8,128)(2,1)} %copy-done.4), custom_call_target="tpu_custom_call" | custom-call | tf_op jit(solution)/shard_map/from_pairs/pallas_call | solution.py:47
  388.7 2.9 convolution_convert_fusion.6
  391.6 1.4 pad_maximum_fusion
  393.0 4.0 copy.45
  398.1 72.0 %grad_exchange.1 = (bf16[8,64,896]{2,1,0:T(8,128)(2,1)}, bf16[2,128,1024]{2,1,0:T(8,128)(2,1)}, bf16[64,1024]{1,0:T(8,128)(2,1)}) custom-call(bf16[4,4,64,896]{3,2,1,0:T(8,128)(2,1)} %bitcast.133, bf16[4,128,1024]{2,1,0:T(8,128)(2,1)} %bitcast.135, bf16[2,64,1024]{2,1,0:T(8,128)(2,1)} %bitcast.149), custom_call_target="tpu_custom_call" | custom-call | tf_op jit(solution)/shard_map/grad_exchange/pallas_call | solution.py:556
  472.3 2.2 copy.46
  474.4 3.5 reshape.396
  479.3 1.8 reshape.397
  482.9 2.6 convolution_convert_fusion
  485.6 16.5 %plane_scatter.7 = f32[2,64,1024]{2,1,0:T(8,128)} custom-call(bf16[2,8,64,1024]{3,2,1,0:T(8,128)(2,1)} %bitcast.138), custom_call_target="tpu_custom_call" | custom-call | tf_op jit(solution)/shard_map/plane_scatter/pallas_call | solution.py:47
  502.1 1.2 multiply_reduce_fusion
  505.7 29.8 %small_scatter.1 = f32[8,128]{1,0:T(8,128)} custom-call(f32[16,8,128]{2,1,0:T(8,128)} %pad.4.x_ref), custom_call_target="tpu_custom_call" | custom-call | tf_op jit(solution)/shard_map/small_scatter/pallas_call | solution.py:47
  539.0 1.2 slice_bitcast_fusion.3
  541.0 37.8 %blk_gather.1 = bf16[4,2,2,128,1024]{4,3,2,1,0:T(8,128)(2,1)} custom-call(bf16[128,1024]{1,0:T(8,128)(2,1)} %convert_element_type.176.x_ref), custom_call_target="tpu_custom_call" | custom-call | tf_op jit(solution)/shard_map/blk_gather/pallas_call | solution.py:404
  578.8 5.5 fusion.11
  584.3 28.2 %pair_sum.1 = f32[8,64,1024]{2,1,0:T(8,128)} custom-call(bf16[8,64,1024]{2,1,0:T(8,128)(2,1)} %bitcast.146), custom_call_target="tpu_custom_call" | custom-call | tf_op jit(solution)/shard_map/pair_sum/pallas_call | solution.py:47
  612.5 3.2 copy.58
  (189 shorter events, 33.4 us)
Async XLA Ops:
  0.6 88.1 %copy-start = (bf16[512,1024]{1,0:T(8,128)(2,1)S(1)}, bf16[512,1024]{1,0:T(8,128)(2,1)}, u32[]{:S(2)}) copy-start(bf16[512,1024]{1,0:T(8,128)(2,1)} %param.17) | copy-start | bytes 3145732
  2.2 15.2 %copy-start.30 = (bf16[64,4096]{1,0:T(8,128)(2,1)S(1)}, bf16[64,4096]{1,0:T(8,128)(2,1)}, u32[]{:S(2)}) copy-start(bf16[64,4096]{1,0:T(8,128)(2,1)} %param.21) | copy-start | bytes 1572868
  17.4 2.0 copy-start.32
  86.9 73.0 %copy-start.27 = (bf16[16,64,384]{2,1,0:T(8,128)(2,1)}, bf16[16,64,384]{2,1,0:T(8,128)(2,1)S(1)}, u32[]{:S(2)}) copy-start(bf16[16,64,384]{2,1,0:T(8,128)(2,1)S(1)} %slice.118) | copy-start | bytes 2359300
  88.8 2.7 copy-start.37
  91.4 51.0 %copy-start.47 = (s32[2,64]{1,0:T(2,128)S(1)}, s32[2,64]{1,0:T(2,128)}, u32[]{:S(2)}) copy-start(s32[2,64]{1,0:T(2,128)} %param.15) | copy-start | bytes 1540
  91.4 51.1 %copy-start.23 = (bf16[2,64,1024]{2,1,0:T(8,128)(2,1)S(1)}, bf16[2,64,1024]{2,1,0:T(8,128)(2,1)}, u32[]{:S(2)}) copy-start(bf16[2,64,1024]{2,1,0:T(8,128)(2,1)} %param.13) | copy-start | bytes 786436
  142.5 180.3 %copy-start.41 = (pred[128]{0:T(512)(128)(4,1)}, pred[128]{0:T(512)(128)(4,1)S(1)}, u32[]{:S(2)}) copy-start(pred[128]{0:T(512)(128)(4,1)S(1)} %eq.53) | copy-start | bytes 388
  163.4 44.5 %copy-start.19 = (bf16[2,64,1024]{2,1,0:T(8,128)(2,1)S(1)}, bf16[2,64,1024]{2,1,0:T(8,128)(2,1)}, u32[]{:S(2)}) copy-start(bf16[2,64,1024]{2,1,0:T(8,128)(2,1)} %get-tuple-element.22) | copy-start | bytes 786436
  183.0 1.1 copy-start.2
  194.5 0.7 copy-start.6
  210.9 16.7 %copy-start.35 = (f32[16,64]{1,0:T(8,128)S(1)}, f32[16,64]{1,0:T(8,128)}, u32[]{:S(2)}) copy-start(f32[16,64]{1,0:T(8,128)} %get-tuple-element.40) | copy-start | bytes 12292
  210.9 16.8 %copy-start.34 = (f32[16,64]{1,0:T(8,128)S(1)}, f32[16,64]{1,0:T(8,128)}, u32[]{:S(2)}) copy-start(f32[16,64]{1,0:T(8,128)} %get-tuple-element.39) | copy-start | bytes 12292
  227.4 17.1 %copy-start.17 = (bf16[16,64,896]{2,1,0:T(8,128)(2,1)S(1)}, bf16[16,64,896]{2,1,0:T(8,128)(2,1)}, u32[]{:S(2)}) copy-start(bf16[16,64,896]{2,1,0:T(8,128)(2,1)} %get-tuple-element.20) | copy-start | bytes 5505028
  244.5 2.0 copy-start.15
  244.7 8.9 %copy-start.21 = (bf16[16,64,512]{2,1,0:T(8,128)(2,1)}, bf16[16,64,512]{2,1,0:T(8,128)(2,1)S(1)}, u32[]{:S(2)}) copy-start(bf16[16,64,512]{2,1,0:T(8,128)(2,1)S(1)} %slice.125) | copy-start | bytes 3145732
  246.5 7.2 %copy-start.45 = (bf16[4,128,1024]{2,1,0:T(8,128)(2,1)S(1)}, bf16[4,128,1024]{2,1,0:T(8,128)(2,1)}, u32[]{:S(2)}) copy-start(bf16[4,128,1024]{2,1,0:T(8,128)(2,1)} %get-tuple-element.23) | copy-start | bytes 3145732
  253.6 2.6 copy-start.24
  256.3 15.7 %copy-start.33 = (f32[16,64]{1,0:T(8,128)S(1)}, f32[16,64]{1,0:T(8,128)}, u32[]{:S(2)}) copy-start(f32[16,64]{1,0:T(8,128)} %get-tuple-element.38) | copy-start | bytes 12292
  256.3 17.4 %copy-start.13 = (bf16[2,64,1024]{2,1,0:T(8,128)(2,1)S(1)}, bf16[2,64,1024]{2,1,0:T(8,128)(2,1)}, u32[]{:S(2)}) copy-start(bf16[2,64,1024]{2,1,0:T(8,128)(2,1)} %param.16) | copy-start | bytes 786436
  275.0 16.6 %copy-start.25 = (bf16[1024,512]{1,0:T(8,128)(2,1)S(1)}, bf16[1024,512]{1,0:T(8,128)(2,1)}, u32[]{:S(2)}) copy-start(bf16[1024,512]{1,0:T(8,128)(2,1)} %copy-done.24) | copy-start | bytes 3145732
  291.6 4.1 copy-start.8
  291.6 4.1 copy-start.46
  295.7 5.0 copy-start.16
  300.6 2.3 copy-start.22
  322.5 18.0 %copy-start.20 = (bf16[2,64,1024]{2,1,0:T(8,128)(2,1)S(1)}, bf16[2,64,1024]{2,1,0:T(8,128)(2,1)}, u32[]{:S(2)}) copy-start(bf16[2,64,1024]{2,1,0:T(8,128)(2,1)} %get-tuple-element.22) | copy-start | bytes 786436
  322.8 0.8 copy-start.9
  323.4 20.4 %copy-start.39 = (f32[128]{0:T(128)}, f32[128]{0:T(128)S(1)}, u32[]{:S(2)}) copy-start(f32[128]{0:T(128)S(1)} %get-tuple-element.70) | copy-start | bytes 1540
  340.5 14.3 %copy-start.3 = (bf16[192,2048]{1,0:T(8,128)(2,1)S(1)}, bf16[192,2048]{1,0:T(8,128)(2,1)}, u32[]{:S(2)}) copy-start(bf16[192,2048]{1,0:T(8,128)(2,1)} %to_pairs.2.x_ref) | copy-start | bytes 2359300
  354.8 1.0 copy-start.5
  368.2 0.9 copy-start.4
  388.7 2.9 copy-start.18
  393.0 4.0 copy-start.7
  393.0 4.0 copy-start.12
  474.4 3.5 copy-start.26
  478.4 2.7 copy-start.29
  479.2 3.0 copy-start.31
  479.2 3.7 copy-start.11
  479.2 3.7 copy-start.28
  485.5 16.6 %copy-start.42 = (pred[128]{0:T(512)(128)(4,1)S(1)}, pred[128]{0:T(512)(128)(4,1)}, u32[]{:S(2)}) copy-start(pred[128]{0:T(512)(128)(4,1)} %copy-done.41) | copy-start | bytes 388
  485.5 16.6 %copy-start.10 = (f32[128,1024]{1,0:T(8,128)S(1)}, f32[128,1024]{1,0:T(8,128)}, u32[]{:S(2)}) copy-start(f32[128,1024]{1,0:T(8,128)} %copy-done.9) | copy-start | bytes 1572868
  485.5 16.6 %copy-start.40 = (f32[128]{0:T(128)S(1)}, f32[128]{0:T(128)}, u32[]{:S(2)}) copy-start(f32[128]{0:T(128)} %copy-done.39) | copy-start | bytes 1540
  485.5 16.6 %copy-start.43 = (f32[128]{0:T(128)S(1)}, f32[128]{0:T(128)}, u32[]{:S(2)}) copy-start(f32[128]{0:T(128)} %get-tuple-element.71) | copy-start | bytes 1540
  485.6 18.4 %copy-start.36 = (f32[1024]{0:T(1024)S(1)}, f32[1024]{0:T(1024)}, u32[]{:S(2)}) copy-start(f32[1024]{0:T(1024)} %get-tuple-element.49) | copy-start | bytes 12292
  502.1 2.5 copy-start.44
  503.4 75.4 %copy-start.14 = (f32[128,1024]{1,0:T(8,128)}, f32[128,1024]{1,0:T(8,128)S(1)}, u32[]{:S(2)}) copy-start(f32[128,1024]{1,0:T(8,128)S(1)} %get-tuple-element.46) | copy-start | bytes 1572868
  541.0 37.8 %copy-start.38 = (s32[16,1,128]{2,1,0:T(1,128)S(1)}, s32[16,1,128]{2,1,0:T(1,128)}, u32[]{:S(2)}) copy-start(s32[16,1,128]{2,1,0:T(1,128)} %copy-done.37) | copy-start | bytes 24580
  612.5 3.3 copy-start.1

commit v2 on v0

--- a/solution.py
+++ b/solution.py
@@ -1,11 +1,864 @@
+import functools
 import math
 
 import jax
 import jax.numpy as jnp
 from jax import lax
+from jax.experimental import pallas as pl
+from jax.experimental.pallas import tpu as pltpu
 from jax.sharding import PartitionSpec as P
 
 HEADS = 16
+MESH = pl.DeviceIdType.MESH
+F32 = jnp.float32
+BF16 = jnp.bfloat16
+VSPEC = pl.BlockSpec(memory_space=pltpu.VMEM)
+
+
+def place():
+    h = lax.axis_index("head")
+    b = lax.axis_index("blk")
+    return h, b // 4, (b // 2) % 2, b % 2
+
+
+def blk(o, y, c):
+    return (o * 2 + y) * 2 + c
+
+
+def peer(dx, dz, dy, dc):
+    h, o, y, c = place()
+    flip = lambda v, d: 1 - v if d else v
+    return flip(h, dx), blk((o + dz) % 4 if dz else o, flip(y, dy), flip(c, dc))
+
+
+def remote(src, dst, sems, index, device):
+    return pltpu.make_async_remote_copy(
+        src_ref=src,
+        dst_ref=dst,
+        send_sem=sems.at[0, index],
+        recv_sem=sems.at[1, index],
+        device_id=device,
+        device_id_type=MESH,
+    )
+
+
+def landed(ref, sems, index):
+    remote(ref, ref, sems, index, peer(1, 0, 0, 0)).wait_recv()
+
+
+def sems(count):
+    return pltpu.SemaphoreType.DMA((2, count))
+
+
+NEAR_X, NEAR_Y, NEAR_C = (1, 0, 0, 0), (0, 0, 1, 0), (0, 0, 0, 1)
+COLUMN = ((0, 1, 0, 0), (0, 2, 0, 0), (0, 3, 0, 0))
+PLANE = tuple(
+    (dx, 0, dy, dc) for dx in range(2) for dy in range(2) for dc in range(2) if dx or dy or dc
+)
+
+
+class Part:
+    def __init__(self, run, ins, outs, scratch, peers):
+        self.run, self.ins, self.outs, self.scratch, self.peers = run, ins, outs, scratch, peers
+
+
+def fused(name, cid, parts, limit=None):
+    peers = sorted({p for part in parts for p in part.peers})
+    ins = [x for part in parts for x in part.ins]
+    outs = [s for part in parts for s in part.outs]
+    scratch = [s for part in parts for s in part.scratch]
+
+    def kernel(*refs):
+        in_refs, out_refs = refs[: len(ins)], refs[len(ins) : len(ins) + len(outs)]
+        own = refs[len(ins) + len(outs) :]
+        gens = []
+        i = j = k = 0
+        for part in parts:
+            gens.append(
+                part.run(
+                    in_refs[i : i + len(part.ins)],
+                    out_refs[j : j + len(part.outs)],
+                    own[k : k + len(part.scratch)],
+                )
+            )
+            i, j, k = i + len(part.ins), j + len(part.outs), k + len(part.scratch)
+        barrier = pltpu.get_barrier_semaphore()
+        for p in peers:
+            pl.semaphore_signal(barrier, inc=1, device_id=peer(*p), device_id_type=MESH)
+        pl.semaphore_wait(barrier, len(peers))
+        for gen in gens:
+            next(gen)
+        for gen in gens:
+            for _ in gen:
+                pass
+
+    got = pl.pallas_call(
+        kernel,
+        name=name,
+        out_shape=[jax.ShapeDtypeStruct(s, d) for s, d in outs],
+        in_specs=[VSPEC] * len(ins),
+        out_specs=[VSPEC] * len(outs),
+        scratch_shapes=scratch,
+        compiler_params=pltpu.CompilerParams(
+            collective_id=cid, has_side_effects=True, vmem_limit_bytes=limit
+        ),
+    )(*ins)
+    result = []
+    for part in parts:
+        result.append(got[: len(part.outs)])
+        got = got[len(part.outs) :]
+    return result
+
+
+def plane_gather(x):
+    two, r, n = x.shape
+
+    def run(ins, outs, own):
+        (x_ref,), (out_ref,), (sem,) = ins, outs, own
+        h, o, y, c = place()
+        dev_x, dev_y, dev_c = peer(*NEAR_X), peer(*NEAR_Y), peer(*NEAR_C)
+        mine = h * 4 + y * 2 + c
+        of_x = (1 - h) * 4 + y * 2 + c
+        of_y = h * 4 + (1 - y) * 2 + c
+        of_d = (1 - h) * 4 + (1 - y) * 2 + c
+        sent = []
+
+        def go(src, slot, index, device, half):
+            copy = remote(src.at[half], out_ref.at[half, slot], sem, index, device)
+            copy.start()
+            sent.append(copy)
+
+        go(x_ref, mine, 0, dev_x, 0)
+        go(x_ref, mine, 1, dev_y, 1)
+        go(x_ref, mine, 2, dev_x, 1)
+        go(x_ref, mine, 3, dev_y, 0)
+        go(x_ref, mine, 4, dev_c, 0)
+        go(x_ref, mine, 5, dev_c, 1)
+        yield
+        out_ref[:, pl.ds(mine, 1)] = x_ref[...][:, None]
+
+        def relay(slot, half, index, device, onward, to_core):
+            landed(out_ref.at[half, slot], sem, index)
+            if onward is not None:
+                go(out_ref.at[:, slot], slot, onward, device, half)
+            go(out_ref.at[:, slot], slot, to_core, dev_c, half)
+
+        relay(of_x, 0, 0, dev_y, 6, 8)
+        relay(of_y, 1, 1, dev_x, 7, 9)
+        relay(of_x, 1, 2, None, None, 10)
+        relay(of_y, 0, 3, None, None, 11)
+        relay(of_d, 0, 6, None, None, 12)
+        relay(of_d, 1, 7, None, None, 13)
+        flip = 1 - 2 * c
+        for slot, half, index in (
+            (mine, 0, 4),
+            (mine, 1, 5),
+            (of_x, 0, 8),
+            (of_y, 1, 9),
+            (of_x, 1, 10),
+            (of_y, 0, 11),
+            (of_d, 0, 12),
+            (of_d, 1, 13),
+        ):
+            landed(out_ref.at[half, slot + flip], sem, index)
+        for copy in sent:
+            copy.wait_send()
+
+    return Part(run, [x], [((2, 8, r, n), x.dtype)], [sems(14)], [NEAR_X, NEAR_Y, NEAR_C])
+
+
+def plane_scatter(x):
+    two, eight, r, n = x.shape
+
+    def run(ins, outs, own):
+        (x_ref,), (out_ref,), (near, part, from_x, from_y, diag, sem) = ins, outs, own
+        h, o, y, c = place()
+        dev_x, dev_y, dev_c = peer(*NEAR_X), peer(*NEAR_Y), peer(*NEAR_C)
+        mine = h * 4 + y * 2 + c
+        of_x = (1 - h) * 4 + y * 2 + c
+        of_y = h * 4 + (1 - y) * 2 + c
+        of_d = (1 - h) * 4 + (1 - y) * 2 + c
+        flip = 1 - 2 * c
+        sent = []
+
+        def go(src, dst, index, device):
+            copy = remote(src, dst, sem, index, device)
+            copy.start()
+            sent.append(copy)
+
+        order = (of_d, of_x, of_y, mine)
+        for half in range(2):
+            go(x_ref.at[half, of_d + flip], near.at[0, half], half, dev_c)
+        go(x_ref.at[0, of_x + flip], near.at[1, 0], 2, dev_c)
+        go(x_ref.at[1, of_y + flip], near.at[2, 1], 5, dev_c)
+        go(x_ref.at[1, of_x + flip], near.at[1, 1], 3, dev_c)
+        go(x_ref.at[0, of_y + flip], near.at[2, 0], 4, dev_c)
+        for half in range(2):
+            go(x_ref.at[half, mine + flip], near.at[3, half], 6 + half, dev_c)
+        yield
+
+        def add(k, half):
+            landed(near.at[k, half], sem, 2 * k + half)
+            return x_ref[half, order[k]].astype(F32) + near[k, half].astype(F32)
+
+        part[0, 0] = add(0, 0).astype(BF16)
+        go(part.at[0, 0], diag.at[0], 8, dev_x)
+        part[0, 1] = add(0, 1).astype(BF16)
+        go(part.at[0, 1], diag.at[1], 9, dev_y)
+        part[1, 0] = add(1, 0).astype(BF16)
+        go(part.at[1, 0], from_x.at[0], 10, dev_x)
+        part[2, 1] = add(2, 1).astype(BF16)
+        go(part.at[2, 1], from_y.at[1], 11, dev_y)
+        kept_x = add(1, 1)
+        landed(diag.at[1], sem, 9)
+        part[1, 1] = (kept_x + diag[1].astype(F32)).astype(BF16)
+        go(part.at[1, 1], from_x.at[1], 12, dev_x)
+        kept_y = add(2, 0)
+        landed(diag.at[0], sem, 8)
+        part[2, 0] = (kept_y + diag[0].astype(F32)).astype(BF16)
+        go(part.at[2, 0], from_y.at[0], 13, dev_y)
+        for half in range(2):
+            out_ref[half] = add(3, half)
+        for half, ix, iy in ((0, 10, 13), (1, 12, 11)):
+            landed(from_x.at[half], sem, ix)
+            landed(from_y.at[half], sem, iy)
+            out_ref[half] += from_x[half].astype(F32) + from_y[half].astype(F32)
+        for copy in sent:
+            copy.wait_send()
+
+    return Part(
+        run,
+        [x],
+        [((2, r, n), F32)],
+        [
+            pltpu.VMEM((4, 2, r, n), BF16),
+            pltpu.VMEM((3, 2, r, n), BF16),
+            pltpu.VMEM((2, r, n), BF16),
+            pltpu.VMEM((2, r, n), BF16),
+            pltpu.VMEM((2, r, n), BF16),
+            sems(14),
+        ],
+        [NEAR_X, NEAR_Y, NEAR_C],
+    )
+
+
+def exchange(x, peers, out_lead, source, target):
+    peers = list(peers)
+
+    def coords(p):
+        h, o, y, c = place()
+        flip = lambda v, d: 1 - v if d else v
+        return flip(h, p[0]), (o + p[1]) % 4 if p[1] else o, flip(y, p[2]), flip(c, p[3])
+
+    def run(ins, outs, own):
+        (x_ref,), (out_ref,), (sem,) = ins, outs, own
+        me = place()
+        copies = []
+        for k, p in enumerate(peers):
+            copy = remote(
+                source(x_ref, coords(p)), target(out_ref, me), sem, k, peer(*p)
+            )
+            copy.start()
+            copies.append(copy)
+        yield
+        target(out_ref, me)[...] = source(x_ref, me)[...]
+        for copy in copies:
+            copy.wait()
+
+    return Part(run, [x], [(out_lead, x.dtype)], [sems(len(peers))], peers)
+
+
+def line_gather(x):
+    return exchange(x, COLUMN, (4,) + x.shape, lambda r, d: r, lambda r, s: r.at[s[1]])
+
+
+def blk_exchange(x):
+    return exchange(
+        x,
+        [(0, 0, 1, 0), (0, 0, 0, 1), (0, 0, 1, 1)],
+        x.shape,
+        lambda r, d: r.at[d[2] * 2 + d[3]],
+        lambda r, s: r.at[s[2] * 2 + s[3]],
+    )
+
+
+def small_gather(x):
+    peers = [
+        (0, dz, dy, dc) for dz in range(4) for dy in range(2) for dc in range(2) if dz or dy or dc
+    ]
+    return exchange(x, peers, (16,) + x.shape, lambda r, d: r, lambda r, s: r.at[blk(*s[1:])])
+
+
+def pair_copy(x):
+    return exchange(x, [NEAR_X], (2,) + x.shape, lambda r, d: r, lambda r, s: r.at[s[0]])
+
+
+def line_sum(x):
+    block = x.shape[1:]
+
+    def run(ins, outs, own):
+        (x_ref,), (out_ref,), (held, sem) = ins, outs, own
+        o = place()[1]
+        copies = []
+        for k, p in enumerate(COLUMN):
+            copy = remote(x_ref.at[(o + k + 1) % 4], held.at[k], sem, k, peer(*p))
+            copy.start()
+            copies.append(copy)
+        yield
+        for copy in copies:
+            copy.wait()
+        total = x_ref[o].astype(F32)
+        for k in range(3):
+            total += held[k].astype(F32)
+        out_ref[...] = total.astype(BF16)
+
+    return Part(
+        run, [x], [(block, BF16)], [pltpu.VMEM((3,) + block, BF16), sems(3)], COLUMN
+    )
+
+
+def plane_spread(x, width, spots):
+    four, r, n = x.shape
+    lanes = 128
+    pieces = n // lanes
+
+    def run(ins, outs, own):
+        (x_ref,), (out_ref,), (sem,) = ins, outs, own
+        h, o, y, c = place()
+        t = h * 4 + y * 2 + c
+        columns = [
+            out_ref.at[:, pl.ds(pl.multiple_of(lane * lanes, lanes), lanes)] for lane in spots(t)
+        ]
+        copies = []
+        for k, p in enumerate(PLANE):
+            to = (1 - y if p[2] else y) * 2 + (1 - c if p[3] else c)
+            for i in range(pieces):
+                src = x_ref.at[to, :, pl.ds(i * lanes, lanes)]
+                copy = remote(src, columns[i], sem, k * pieces + i, peer(*p))
+                copy.start()
+                copies.append(copy)
+        yield
+        for i in range(pieces):
+            columns[i][...] = x_ref[y * 2 + c, :, i * lanes : (i + 1) * lanes]
+        for copy in copies:
+            copy.wait()
+
+    return Part(run, [x], [((r, width), x.dtype)], [sems(7 * pieces)], PLANE)
+
+
+def place_copy(src, dst, send_sem, recv_sem, device):
+    return pltpu.make_async_remote_copy(
+        src_ref=src,
+        dst_ref=dst,
+        send_sem=send_sem,
+        recv_sem=recv_sem,
+        device_id=device,
+        device_id_type=MESH,
+    )
+
+
+BLK = tuple(
+    (0, dz, dy, dc) for dz in range(4) for dy in range(2) for dc in range(2) if dz or dy or dc
+)
+
+
+def out_weights(w):
+    r, n = w.shape
+
+    def run(ins, outs, own):
+        (w_ref,), (out_ref,), (send, recv) = ins, outs, own
+        h, o, y, c = place()
+        has = o // 2 == h
+        serves = (o % 2 == y) & (y == c)
+
+        def each(act):
+            for k in range(4):
+                device = (h, blk((o + k) % 4, o % 2, y))
+                copy = place_copy(w_ref, out_ref.at[c], send.at[k], recv.at[c], device)
+
+                @pl.when(has if k else has & jnp.logical_not(serves))
+                def _():
+                    act(copy)
+
+        each(lambda copy: copy.start())
+        yield
+
+        @pl.when(has & serves)
+        def _():
+            out_ref[pl.ds(c, 1)] = w_ref[...][None]
+
+        each(lambda copy: copy.wait_send())
+        for core in range(2):
+            from_self = (o == 2 * h + y) & (y == c) & (c == core)
+            ref = out_ref.at[core]
+
+            @pl.when(jnp.logical_not(from_self))
+            def _():
+                place_copy(ref, ref, send.at[0], recv.at[core], (h, blk(o, y, c))).wait_recv()
+
+    scratch = [pltpu.SemaphoreType.DMA((4,)), pltpu.SemaphoreType.DMA((2,))]
+    return Part(run, [w], [((2, r, n), BF16)], scratch, BLK)
+
+
+def out_grads(x):
+    two, r, n = x.shape
+
+    def run(ins, outs, own):
+        (x_ref,), (out_ref,), (held, send, recv) = ins, outs, own
+        h, o, y, c = place()
+        has = o // 2 == h
+
+        def each(act):
+            for j in range(2):
+                device = (h, blk(2 * h + y, c, j))
+                copy = place_copy(x_ref.at[j], held.at[o], send.at[j], recv.at[o], device)
+
+                @pl.when(jnp.logical_not((o == 2 * h + y) & (y == c) & (c == j)))
+                def _():
+                    act(copy)
+
+        each(lambda copy: copy.start())
+        yield
+        out_ref[...] = jnp.zeros_like(out_ref)
+        for z in range(4):
+            mine = (z == o) & (o % 2 == y) & (y == c)
+
+            @pl.when(has & mine)
+            def _():
+                out_ref[...] += x_ref[c].astype(F32)
+
+            @pl.when(has & jnp.logical_not(mine))
+            def _():
+                ref = held.at[z]
+                place_copy(ref, ref, send.at[0], recv.at[z], (h, blk(o, y, c))).wait_recv()
+                out_ref[...] += held[z].astype(F32)
+
+        each(lambda copy: copy.wait_send())
+
+    scratch = [
+        pltpu.VMEM((4, r, n), BF16),
+        pltpu.SemaphoreType.DMA((2,)),
+        pltpu.SemaphoreType.DMA((4,)),
+    ]
+    return Part(run, [x], [((r, n), F32)], scratch, BLK)
+
+
+def mirrored():
+    o = place()[1]
+    far = o // 2
+    seen = lambda v: v * (1 - 2 * far) + 3 * far
+    return seen(o), seen
+
+
+def rows_scatter(x):
+    r, n = x.shape[3:]
+
+    def run(ins, outs, own):
+        (x_ref,), (out_ref,), (near, part, from_y, term, ends, mids, last, csem, ysem, zsem) = (
+            ins,
+            outs,
+            own,
+        )
+        h, o, y, c = place()
+        at, seen = mirrored()
+        dev_y, dev_c = peer(*NEAR_Y), peer(*NEAR_C)
+        order = [seen(3), seen(2), seen(1 - at), o]
+        end, inner, other = (h, blk(seen(0), y, c)), (h, blk(seen(1), y, c)), (h, blk(seen(2), y, c))
+        sent = []
+        for i, yy in enumerate((1 - y, y)):
+            for j, z in enumerate(order):
+                copy = remote(x_ref.at[z, yy, 1 - c], near.at[i, j], csem, i * 4 + j, dev_c)
+                copy.start()
+                sent.append(copy)
+        yield
+        for j, z in enumerate(order):
+            landed(near.at[0, j], csem, j)
+            part[j] = x_ref[z, 1 - y, c] + near[0, j]
+            copy = remote(part.at[j], from_y.at[j], ysem, j, dev_y)
+            copy.start()
+            sent.append(copy)
+        for j, z in enumerate(order):
+            landed(near.at[1, j], csem, 4 + j)
+            landed(from_y.at[j], ysem, j)
+            term[j] = x_ref[z, y, c] + near[1, j] + from_y[j]
+            if j < 3:
+
+                @pl.when(at == 0)
+                def _():
+                    remote(term.at[j], ends.at[j], zsem, j, inner).start()
+
+            if j < 2:
+
+                @pl.when(at == 1)
+                def _():
+                    landed(ends.at[j], zsem, j)
+                    term[j] += ends[j]
+                    remote(term.at[j], mids.at[j], zsem, 3 + j, other).start()
+
+        @pl.when(at == 1)
+        def _():
+            landed(mids.at[0], zsem, 3)
+            term[2] += mids[0]
+            remote(term.at[2], last, zsem, 5, end).start()
+            landed(ends.at[2], zsem, 2)
+            landed(mids.at[1], zsem, 4)
+            out_ref[...] = (term[3] + ends[2] + mids[1]).astype(F32)
+            for j in range(2):
+                remote(term.at[j], mids.at[j], zsem, 3 + j, other).wait_send()
+            remote(term.at[2], last, zsem, 5, end).wait_send()
+
+        @pl.when(at == 0)
+        def _():
+            landed(last, zsem, 5)
+            out_ref[...] = (term[3] + last[...]).astype(F32)
+            for j in range(3):
+                remote(term.at[j], ends.at[j], zsem, j, inner).wait_send()
+
+        for copy in sent:
+            copy.wait_send()
+
+    block = (r, n)
+    scratch = [
+        pltpu.VMEM((2, 4) + block, BF16),
+        pltpu.VMEM((4,) + block, BF16),
+        pltpu.VMEM((4,) + block, BF16),
+        pltpu.VMEM((4,) + block, BF16),
+        pltpu.VMEM((3,) + block, BF16),
+        pltpu.VMEM((2,) + block, BF16),
+        pltpu.VMEM(block, BF16),
+        sems(8),
+        sems(4),
+        sems(6),
+    ]
+    return Part(run, [x], [(block, F32)], scratch, (NEAR_Y, NEAR_C) + COLUMN)
+
+
+def blk_gather(x):
+    r, n = x.shape
+
+    def run(ins, outs, own):
+        (x_ref,), (out_ref,), (zsem, ysem, csem) = ins, outs, own
+        h, o, y, c = place()
+        at, seen = mirrored()
+        dev_y, dev_c = peer(*NEAR_Y), peer(*NEAR_C)
+        end, inner, other = (h, blk(seen(0), y, c)), (h, blk(seen(1), y, c)), (h, blk(seen(2), y, c))
+        sent = []
+
+        def spot(z, yy=y, cc=c):
+            return out_ref.at[z, yy, cc]
+
+        def go(src, z, yy, sem, index, device):
+            copy = remote(src, spot(z, yy), sem, index, device)
+            copy.start()
+            sent.append(copy)
+
+        def line(src, z, index, device):
+            return remote(src, spot(z), zsem, index, device)
+
+        @pl.when(at == 0)
+        def _():
+            line(x_ref, o, 0, inner).start()
+
+        @pl.when(at == 1)
+        def _():
+            line(x_ref, o, 1, end).start()
+            line(x_ref, o, 2, other).start()
+
+        go(x_ref, o, y, ysem, 0, dev_y)
+        go(x_ref, o, y, csem, 0, dev_c)
+        yield
+        out_ref[o, y, c] = x_ref[...]
+
+        def onward(j, z):
+            go(spot(z), z, y, ysem, j, dev_y)
+            go(spot(z), z, y, csem, j, dev_c)
+
+        first = seen(1 - at)
+
+        @pl.when(at == 0)
+        def _():
+            landed(spot(seen(1)), zsem, 1)
+
+        @pl.when(at == 1)
+        def _():
+            landed(spot(seen(0)), zsem, 0)
+            line(spot(seen(0)), seen(0), 3, other).start()
+
+        onward(1, first)
+
+        @pl.when(at == 0)
+        def _():
+            landed(spot(seen(2)), zsem, 4)
+
+        @pl.when(at == 1)
+        def _():
+            landed(spot(seen(2)), zsem, 2)
+            line(spot(seen(2)), seen(2), 4, end).start()
+
+        onward(2, seen(2))
+
+        @pl.when(at == 0)
+        def _():
+            landed(spot(seen(3)), zsem, 5)
+
+        @pl.when(at == 1)
+        def _():
+            landed(spot(seen(3)), zsem, 3)
+            line(spot(seen(3)), seen(3), 5, end).start()
+
+        onward(3, seen(3))
+        for j, z in enumerate((o, first, seen(2), seen(3))):
+            landed(spot(z, 1 - y), ysem, j)
+            go(spot(z, 1 - y), z, 1 - y, csem, 4 + j, dev_c)
+        for j, z in enumerate((o, first, seen(2), seen(3))):
+            landed(spot(z, y, 1 - c), csem, j)
+            landed(spot(z, 1 - y, 1 - c), csem, 4 + j)
+
+        @pl.when(at == 0)
+        def _():
+            line(x_ref, o, 0, inner).wait_send()
+
+        @pl.when(at == 1)
+        def _():
+            line(x_ref, o, 1, end).wait_send()
+            line(x_ref, o, 2, other).wait_send()
+            line(spot(seen(0)), seen(0), 3, other).wait_send()
+            line(spot(seen(2)), seen(2), 4, end).wait_send()
+            line(spot(seen(3)), seen(3), 5, end).wait_send()
+
+        for copy in sent:
+            copy.wait_send()
+
+    return Part(
+        run,
+        [x],
+        [((4, 2, 2, r, n), x.dtype)],
+        [sems(6), sems(4), sems(8)],
+        (NEAR_Y, NEAR_C) + COLUMN,
+    )
+
+
+def pair_sum(x):
+    n = x.shape[0]
+
+    def run(ins, outs, own):
+        (x_ref,), (out_ref,), (held, sem) = ins, outs, own
+        copies = [remote(x_ref.at[k], held.at[k], sem, k, peer(*NEAR_X)) for k in range(n)]
+        for copy in copies:
+            copy.start()
+        yield
+        for k, copy in enumerate(copies):
+            copy.wait()
+            out_ref[k] = x_ref[k].astype(F32) + held[k].astype(F32)
+
+    return Part(
+        run, [x], [(x.shape, F32)], [pltpu.VMEM(x.shape, x.dtype), sems(n)], [NEAR_X]
+    )
+
+
+def small_scatter(x):
+    peers = [
+        (dx, dz, dy, dc)
+        for dx in range(2)
+        for dz in range(4)
+        for dy in range(2)
+        for dc in range(2)
+        if dx or dz or dy or dc
+    ]
+    block = x.shape[1:]
+
+    def run(ins, outs, own):
+        (x_ref,), (out_ref,), (held, sem) = ins, outs, own
+        h, o, y, c = place()
+        copies = []
+        for k, p in enumerate(peers):
+            to = peer(*p)
+            copy = remote(x_ref.at[to[1]], held.at[k], sem, k, to)
+            copy.start()
+            copies.append(copy)
+        yield
+        for copy in copies:
+            copy.wait()
+        out_ref[...] = x_ref[blk(o, y, c)] + jnp.sum(held[...], axis=0)
+
+    return Part(
+        run, [x], [(block, F32)], [pltpu.VMEM((31,) + block, F32), sems(31)], peers
+    )
+
+
+def attend(x, scale, cols=256):
+    three, two, e, wide = x.shape
+    n = wide // 2
+    length = 4 * n
+
+    def run(ins, outs, own):
+        (x_ref,), (back_ref, held, o_ref, lse_ref), (keys, low, isem, osem) = ins, outs, own
+        o = place()[1]
+        copies = []
+        for k, p in enumerate(COLUMN):
+            z = (o + k + 1) % 4
+            copy = remote(
+                x_ref.at[:, z % 2, :, pl.ds(pl.multiple_of((z // 2) * n, n), n)],
+                held.at[:, :, pl.ds(pl.multiple_of(o * n, n), n)],
+                isem,
+                k,
+                peer(*p),
+            )
+            copy.start()
+            copies.append(copy)
+        yield
+        mine = pl.ds(pl.multiple_of((o // 2) * n, n), n)
+        held[:, :, pl.ds(pl.multiple_of(o * n, n), n)] = x_ref[:, o % 2, :, mine]
+        for copy in copies:
+            copy.wait()
+        keys[...] = held[1].astype(F32).T.astype(BF16)
+
+        def back(i, z):
+            return remote(
+                low.at[:, pl.ds(pl.multiple_of(z * n, n), n)],
+                back_ref.at[o % 2, :, mine],
+                osem,
+                i,
+                (place()[0], z * 4 + lax.axis_index("blk") % 4),
+            )
+
+        @pl.loop(0, 4 * (n // cols))
+        def _(step):
+            i = step // (n // cols)
+            z = (o + 1 + i) % 4
+            at = pl.ds(pl.multiple_of(z * n + step % (n // cols) * cols, cols), cols)
+            q = (held[0, :, at].astype(F32) * scale).astype(BF16)
+            s = jnp.dot(keys[...], q, preferred_element_type=F32)
+            peak = jnp.max(s, axis=0, keepdims=True)
+            p = jnp.exp(s - peak)
+            total = jnp.sum(p, axis=0, keepdims=True)
+            out = jnp.dot(held[2], p.astype(BF16), preferred_element_type=F32) / total
+            o_ref[:, at] = out
+            low[:, at] = out.astype(BF16)
+            lse_ref[:, at] = peak + jnp.log(total)
+
+            @pl.when((step % (n // cols) == n // cols - 1) & (i < 3))
+            def _():
+                back(i, z).start()
+
+        back_ref[o % 2, :, mine] = low[:, pl.ds(pl.multiple_of(o * n, n), n)]
+        for i in range(3):
+            back(i, (o + 1 + i) % 4).wait_send()
+            z = (o + 3 - i) % 4
+            ref = back_ref.at[z % 2, :, pl.ds(pl.multiple_of((z // 2) * n, n), n)]
+            landed(ref, osem, i)
+
+    return Part(
+        run,
+        [x],
+        [
+            ((two, e, wide), BF16),
+            ((three, e, length), BF16),
+            ((e, length), F32),
+            ((1, length), F32),
+        ],
+        [pltpu.VMEM((length, e), BF16), pltpu.VMEM((e, length), BF16), sems(3), sems(3)],
+        COLUMN,
+    )
+
+
+def attend_back(g, held, out, lse, scale, rows=256):
+    three, e, length = held.shape
+    n = length // 4
+
+    def run(ins, outs, own):
+        (g_ref, held_ref, o_ref, lse_ref), (back_ref,) = ins, outs
+        gs, qs, q_rows, g_rows, dq, delta, low, isem, ksem, qsem = own
+        o = place()[1]
+        copies = []
+        for k, p in enumerate(COLUMN):
+            z = (o + k + 1) % 4
+            copy = remote(
+                g_ref.at[z % 2, :, pl.ds(pl.multiple_of((z // 2) * n, n), n)],
+                gs.at[:, pl.ds(pl.multiple_of(o * n, n), n)],
+                isem,
+                k,
+                peer(*p),
+            )
+            copy.start()
+            copies.append(copy)
+        yield
+        mine = pl.ds(pl.multiple_of((o // 2) * n, n), n)
+        gs[:, pl.ds(pl.multiple_of(o * n, n), n)] = g_ref[o % 2, :, mine]
+        q32 = held_ref[0].astype(F32) * scale
+        qs[...] = q32.astype(BF16)
+        q_rows[...] = q32.T.astype(BF16)
+        dq[...] = jnp.zeros_like(dq)
+        for copy in copies:
+            copy.wait()
+        g32 = gs[...].astype(F32)
+        g_rows[...] = g32.T.astype(BF16)
+        delta[...] = jnp.sum(g32 * o_ref[...], axis=0, keepdims=True)
+
+        def back(part, sem, i, z):
+            return remote(
+                low.at[part, :, pl.ds(pl.multiple_of(z * n, n), n)],
+                back_ref.at[part, o % 2, :, mine],
+                sem,
+                i,
+                (place()[0], z * 4 + lax.axis_index("blk") % 4),
+            )
+
+        late = pl.ds(1, 2)
+        steps = n // rows
+
+        @pl.loop(0, 4 * steps)
+        def _(step):
+            i = step // steps
+            z = (o + 1 + i) % 4
+            at = pl.ds(pl.multiple_of(z * n + step % steps * rows, rows), rows)
+            k_cols = held_ref[1, :, at]
+            k_rows = k_cols.astype(F32).T.astype(BF16)
+            v_rows = held_ref[2, :, at].astype(F32).T.astype(BF16)
+            s = jnp.dot(k_rows, qs[...], preferred_element_type=F32)
+            p = jnp.exp(s - lse_ref[...])
+            dv = jnp.dot(p.astype(BF16), g_rows[...], preferred_element_type=F32)
+            dp = jnp.dot(v_rows, gs[...], preferred_element_type=F32)
+            ds = (p * (dp - delta[...])).astype(BF16)
+            dk = jnp.dot(ds, q_rows[...], preferred_element_type=F32)
+            dq[...] += jnp.dot(k_cols, ds, preferred_element_type=F32)
+            low[1, :, at] = dk.T.astype(BF16)
+            low[2, :, at] = dv.T.astype(BF16)
+
+            @pl.when((step % steps == steps - 1) & (i < 3))
+            def _():
+                back(late, ksem, i, z).start()
+
+        low[0] = (dq[...] * scale).astype(BF16)
+        for i in range(3):
+            back(pl.ds(0, 1), qsem, i, (o + 1 + i) % 4).start()
+        back_ref[:, o % 2, :, mine] = low[:, :, pl.ds(pl.multiple_of(o * n, n), n)]
+        for i in range(3):
+            back(late, ksem, i, (o + 1 + i) % 4).wait_send()
+            back(pl.ds(0, 1), qsem, i, (o + 1 + i) % 4).wait_send()
+            z = (o + 3 - i) % 4
+            there = pl.ds(pl.multiple_of((z // 2) * n, n), n)
+            landed(back_ref.at[late, z % 2, :, there], ksem, i)
+            landed(back_ref.at[pl.ds(0, 1), z % 2, :, there], qsem, i)
+
+    return Part(
+        run,
+        [g, held, out, lse],
+        [((three,) + g.shape, BF16)],
+        [
+            pltpu.VMEM((e, length), BF16),
+            pltpu.VMEM((e, length), BF16),
+            pltpu.VMEM((length, e), BF16),
+            pltpu.VMEM((length, e), BF16),
+            pltpu.VMEM((e, length), F32),
+            pltpu.VMEM((1, length), F32),
+            pltpu.VMEM((three, e, length), BF16),
+            sems(3),
+            sems(3),
+            sems(3),
+        ],
+        COLUMN,
+    )
 
 
 def norm_layer(values_in, gain_row, offset_row):
@@ -153,7 +1006,7 @@
     return fold_queries
 
 
-def on_device(
+def layer_in_blocks(
     hidden,
     pos_ids,
     type_ids,
@@ -450,6 +1303,312 @@
     )
 
 
+BIG = 56 << 20
+
+
+def layer_in_planes(
+    hidden,
+    pos_ids,
+    type_ids,
+    cotangent,
+    pos_table,
+    type_table,
+    query_key_value_weight,
+    attention_output_weight,
+    up_projection_weight,
+    down_projection_weight,
+    up_projection_bias,
+    norm_gains,
+    biases,
+):
+    seqs, seg, width = hidden.shape
+    blks = lax.axis_size("blk")
+    h = lax.axis_index("head")
+    b = lax.axis_index("blk")
+    o, g = b // 4, b % 4
+    rows = seqs * seg
+    e = width // HEADS
+    ff = up_projection_weight.shape[1]
+    scale = 1.0 / math.sqrt(e)
+    slots = pos_table.shape[0]
+    fcols = ff // blks // 2
+    plane_rows = 8 * rows
+
+    small = jnp.concatenate(
+        [
+            biases.astype(F32),
+            norm_gains.astype(F32),
+            type_table.astype(F32),
+            up_projection_bias.astype(F32).reshape(4, e),
+        ]
+    ).reshape(7, 2 * e)
+    packed = jnp.concatenate([small, pos_ids.astype(F32).reshape(1, rows)])
+    qkv_cut = query_key_value_weight.reshape(e, 3, 2, 4, 2 * e)
+    qkv_cut = lax.dynamic_slice_in_dim(qkv_cut, h, 1, 2).reshape(e, 3, 4, 2 * e)
+    qkv_cut = qkv_cut.transpose(2, 0, 1, 3).reshape(4, e, 6 * e)
+    up_cut = up_projection_weight.reshape(e, 4, 4, 2, fcols)
+    up_cut = lax.dynamic_slice_in_dim(up_cut, h, 1, 3).reshape(e, 4, 4, fcols)
+    up_cut = up_cut.transpose(2, 0, 1, 3).reshape(4, e, 4 * fcols)
+    down_cut = lax.dynamic_slice_in_dim(down_projection_weight, h * fcols, fcols, 0)
+    half_down, half_up = fcols // 2, 2 * fcols
+    (everyone,), (out_all,), (qkv_cut,), (up_cut,) = fused(
+        "opening",
+        0,
+        [
+            small_gather(packed),
+            out_weights(attention_output_weight),
+            blk_exchange(qkv_cut),
+            blk_exchange(up_cut),
+        ],
+    )
+    out_own = out_all.reshape(2 * e, width)
+    params = everyone[:, :7].reshape(blks, 14, e).transpose(1, 0, 2)
+    vectors = params[:10].reshape(10, width)
+    bias_float, gain_float, type_float = vectors[:6], vectors[6:8], vectors[8:10]
+    up_bias = lax.dynamic_slice_in_dim(
+        params[10:].transpose(1, 0, 2).reshape(4, 4, 2, fcols), h, 1, 2
+    )
+    up_bias = lax.dynamic_slice_in_dim(up_bias, g, 1, 1).reshape(1, 4 * fcols)
+    all_ids = everyone[:, 7].astype(jnp.int32)
+
+    local_ids = all_ids.reshape(blks * rows, 1) - b * slots
+    onehot = (local_ids == lax.broadcasted_iota(jnp.int32, (1, slots), 1)).astype(BF16)
+    found = jnp.dot(onehot, pos_table, preferred_element_type=F32).astype(BF16)
+    (positions,), (qkv_all,) = fused(
+        "rows", 1, [rows_scatter(found.reshape(4, 2, 2, rows, width)), line_gather(qkv_cut)], BIG
+    )
+    qkv_own = qkv_all.reshape(width, 6 * e)
+    is_second = type_ids.reshape(rows, 1) == 1
+    typed = jnp.where(is_second, type_float[1], type_float[0])
+    embedded = hidden.reshape(rows, width).astype(F32) + positions + typed
+    token_shape = (seqs, seg, width)
+
+    (plane_low,), (up_first,) = fused(
+        "gather_tokens",
+        2,
+        [
+            plane_gather(embedded.astype(BF16).reshape(token_shape)),
+            line_gather(up_cut[:, :, :half_up]),
+        ],
+    )
+    plane_low = plane_low.reshape(plane_rows, width)
+    bias_heads = bias_float.reshape(6, 8, 2 * e)
+    bias_heads = lax.dynamic_slice_in_dim(bias_heads, h * 4 + g, 1, 1)[:, 0]
+    qkv_bias = jnp.concatenate(
+        [bias_heads[0], jnp.zeros_like(bias_heads[0]), bias_heads[1]]
+    ).reshape(6 * e, 1)
+    projected = (
+        jnp.einsum("kf,rk->fr", qkv_own, plane_low, preferred_element_type=F32) + qkv_bias
+    ).astype(BF16)
+    (attended, pair_qkv, pair_out, lse), (down_first,) = fused(
+        "attend",
+        3,
+        [
+            attend(projected.reshape(3, 2, e, plane_rows), scale),
+            line_gather(down_cut[:half_down]),
+        ],
+        BIG,
+    )
+    attended = attended.reshape(2 * e, plane_rows)
+    branch = jnp.einsum("fr,fd->rd", attended, out_own, preferred_element_type=F32).astype(BF16)
+    (branch,), (up_second,) = fused(
+        "scatter_branch",
+        4,
+        [
+            plane_scatter(branch.reshape(seqs, 8, seg, width)),
+            line_gather(up_cut[:, :, half_up:]),
+        ],
+    )
+    branch = branch.reshape(rows, width)
+    first, first_pull = jax.vjp(
+        norm_layer, embedded + (branch + bias_float[2]), gain_float[0], bias_float[3]
+    )
+
+    (first_low,), (down_second,) = fused(
+        "gather_first",
+        5,
+        [
+            plane_gather(first.astype(BF16).reshape(token_shape)),
+            line_gather(down_cut[half_down:]),
+        ],
+    )
+    first_low = first_low.reshape(plane_rows, width)
+    up_own = jnp.concatenate([up_first, up_second], axis=3).reshape(width, 4 * fcols)
+    down_own = jnp.concatenate([down_first, down_second], axis=1).reshape(4 * fcols, width)
+    inner = jnp.dot(first_low, up_own, preferred_element_type=F32) + up_bias
+    activated, gelu_pull = jax.vjp(gelu_exact, inner)
+    activated_low = activated.astype(BF16)
+    second = jnp.dot(activated_low, down_own, preferred_element_type=F32).astype(BF16)
+    ((second,),) = fused("scatter_second", 6, [plane_scatter(second.reshape(seqs, 8, seg, width))])
+    second = second.reshape(rows, width)
+    final, final_pull = jax.vjp(
+        norm_layer, first + (second + bias_float[4]), gain_float[1], bias_float[5]
+    )
+    layer_out = final.astype(BF16).reshape(token_shape)
+
+    grad_final, grad_gain_two, grad_shift_two = final_pull(
+        cotangent.reshape(rows, width).astype(F32)
+    )
+    grad_low = grad_final.astype(BF16)
+    grad_bias_second = jnp.sum(grad_low.astype(F32), axis=0)
+    ((plane_grad,),) = fused("gather_grad", 7, [plane_gather(grad_low.reshape(token_shape))])
+    plane_grad = plane_grad.reshape(plane_rows, width)
+    grad_down = jnp.einsum(
+        "rf,rd->fd", activated_low, plane_grad, preferred_element_type=F32
+    ).astype(BF16)
+    (grad_inner,) = gelu_pull(
+        jnp.einsum("rd,fd->rf", plane_grad, down_own, preferred_element_type=F32)
+    )
+    grad_inner_low = grad_inner.astype(BF16)
+    grad_up = jnp.einsum(
+        "rd,rf->df", first_low, grad_inner_low, preferred_element_type=F32
+    ).astype(BF16)
+    grad_up_bias = jnp.sum(grad_inner_low.astype(F32), axis=0)
+    grad_first = jnp.einsum(
+        "rf,df->rd", grad_inner_low, up_own, preferred_element_type=F32
+    ).astype(BF16)
+    grad_up = grad_up.reshape(4, 4, e, 4 * fcols)
+    grad_down = grad_down.reshape(4, fcols, width)
+    (grad_first,), (down_one,), (up_one,) = fused(
+        "scatter_first",
+        8,
+        [
+            plane_scatter(grad_first.reshape(seqs, 8, seg, width)),
+            line_sum(grad_down[:, :half_down]),
+            line_sum(grad_up[:, :, :, :half_up]),
+        ],
+    )
+    grad_first = grad_first.reshape(rows, width)
+    grad_resid, grad_gain_one, grad_shift_one = first_pull(grad_final + grad_first)
+    branch_low = grad_resid.astype(BF16)
+    grad_bias_branch = jnp.sum(branch_low.astype(F32), axis=0)
+    (plane_branch,), (down_two,), (up_two,) = fused(
+        "gather_branch",
+        9,
+        [
+            plane_gather(branch_low.reshape(token_shape)),
+            line_sum(grad_down[:, half_down:]),
+            line_sum(grad_up[:, :, :, half_up:]),
+        ],
+    )
+    plane_branch = plane_branch.reshape(plane_rows, width)
+    grad_out = jnp.einsum(
+        "fr,rd->fd", attended, plane_branch, preferred_element_type=F32
+    ).astype(BF16)
+    grad_attended = jnp.einsum(
+        "fd,rd->fr", out_own, plane_branch, preferred_element_type=F32
+    ).astype(BF16)
+    (grad_qkv,), (out_total,), (got_up,), (got_down,) = fused(
+        "attend_back",
+        10,
+        [
+            attend_back(grad_attended.reshape(2, e, plane_rows), pair_qkv, pair_out, lse, scale),
+            out_grads(grad_out.reshape(2, e, width)),
+            plane_spread(
+                jnp.concatenate([up_one, up_two], axis=2),
+                ff,
+                lambda t: [(i * 4 + t % 4) * 2 + t // 4 for i in range(4)],
+            ),
+            pair_copy(jnp.concatenate([down_one, down_two], axis=0)),
+        ],
+        BIG,
+    )
+    grad_qkv = grad_qkv.reshape(6 * e, plane_rows)
+    grad_qkv_weight = jnp.einsum(
+        "rk,fr->kf", plane_low, grad_qkv, preferred_element_type=F32
+    ).astype(BF16)
+    head_sums = jnp.sum(grad_qkv.astype(F32), axis=1).reshape(3, 2 * e)
+    back = jnp.einsum("fr,kf->rk", grad_qkv, qkv_own, preferred_element_type=F32).astype(BF16)
+    (back,), (qkv_total,), (got_out,) = fused(
+        "scatter_back",
+        11,
+        [
+            plane_scatter(back.reshape(seqs, 8, seg, width)),
+            line_sum(grad_qkv_weight.reshape(4, 4, e, 6 * e)),
+            pair_copy(out_total.astype(BF16)),
+        ],
+    )
+    grad_embedded = grad_resid + back.reshape(rows, width)
+    grad_hidden = grad_embedded.reshape(token_shape)
+
+    second_mask = is_second.astype(F32)
+    type_one = jnp.sum(grad_embedded * second_mask, axis=0)
+    type_zero = jnp.sum(grad_embedded * (1.0 - second_mask), axis=0)
+
+    def spread(part):
+        whole = lax.dynamic_update_slice(
+            jnp.zeros((8, 2 * e), F32), part.reshape(1, 2 * e), (h * 4 + g, 0)
+        )
+        return whole.reshape(width)
+
+    stacked = jnp.stack(
+        [
+            spread(head_sums[0]),
+            spread(head_sums[2]),
+            grad_bias_branch,
+            grad_shift_one,
+            grad_bias_second,
+            grad_shift_two,
+            grad_gain_one,
+            grad_gain_two,
+            type_zero,
+            type_one,
+        ]
+    )
+    up_spread = lax.dynamic_update_slice(
+        jnp.zeros((4, 4, 2, fcols), F32), grad_up_bias.reshape(4, 1, 1, fcols), (0, g, h, 0)
+    ).reshape(blks, 4, e)
+    vector_pack = jnp.concatenate(
+        [stacked.reshape(10, blks, e).transpose(1, 0, 2), up_spread], axis=1
+    ).reshape(blks, 7, 2 * e)
+    vector_pack = jnp.pad(vector_pack, ((0, 0), (0, 1), (0, 0)))
+
+    (all_grads,), (totals,), (got_qkv,) = fused(
+        "closing",
+        12,
+        [
+            blk_gather(grad_embedded.astype(BF16)),
+            small_scatter(vector_pack),
+            plane_spread(qkv_total, 3 * width, lambda t: [i * 8 + t for i in range(3)]),
+        ],
+    )
+    totals = totals[:7].reshape(14, e)
+    all_grads = all_grads.reshape(blks * rows, width)
+    flat_ids = all_ids.reshape(1, blks * rows) - b * slots
+    pick = (flat_ids == lax.broadcasted_iota(jnp.int32, (slots, 1), 0)).astype(BF16)
+    pos_part = jnp.dot(pick, all_grads, preferred_element_type=F32).astype(BF16)
+    ((total_pos,),) = fused("pos_sum", 13, [pair_sum(pos_part.reshape(8, slots // 8, width))])
+    total_pos = total_pos.reshape(slots, width)
+    total_qkv = got_qkv.astype(F32)
+    total_up = got_up.astype(F32)
+    total_down = got_down.reshape(2 * fcols, width).astype(F32)
+    total_out = lax.dynamic_index_in_dim(got_out, o // 2, 0, False).astype(F32)
+    return (
+        layer_out,
+        grad_hidden,
+        total_pos,
+        totals[8:10],
+        total_qkv,
+        total_out,
+        total_up,
+        total_down,
+        totals[10:14].reshape(4 * e),
+        totals[6:8],
+        totals[:6],
+    )
+
+
+def planes_fit(hidden, head_axis, blk_axis):
+    seqs, seg, width = hidden.shape
+    return head_axis == 2 and blk_axis == HEADS and seqs == 2 and seqs * seg == 2 * width // HEADS
+
+
+def on_device(hidden, *rest):
+    if planes_fit(hidden, lax.axis_size("head"), lax.axis_size("blk")):
+        return layer_in_planes(hidden, *rest)
+    return layer_in_blocks(hidden, *rest)
+
+
 def solution(mesh):
     in_specs = (
         P(None, ("head", "blk"), None),

time: 1850 us -> 468 us (0.25)
  waiting for transfers between devices: 1300 us -> 0 us
  Pallas kernels: 0 us -> 376 us
  blocking collectives: 212 us -> 0 us
  matrix products: 155 us -> 47.9 us
  local copies, waits for them, and re-layouts: 115 us -> 17.6 us
  starting transfers between devices: 19.4 us -> 0 us
    reduce_scatter x5 -> x0, waiting for transfers between devices: 720 us -> none  [the longest x1 334 us: on_device(): lax.psum_scatter(buffer[:length], 'blk', scatter_dimension=0, tiled=True)]
    pallas_call x0 -> x14, Pallas kernels: none -> 376 us  [fused(): pl.pallas_call(kernel, name=name, out_shape=[jax.ShapeDtypeStruct(s, d) f...]
    all_gather x9 -> x0, waiting for transfers between devices: 322 us -> none  [the longest x1 105 us: on_device(): portion = lax.all_gather(pos_table, 'blk', axis=0, tiled=True)]
    psum x1 -> x0, waiting for transfers between devices: 126 us -> none  [on_device(): lax.psum((shard_qkv, shard_out, shard_up, shard_down, shard_up_bias, shar...]
    all_gather x6 -> x0, blocking collectives: 120 us -> none  [the longest x1 23.7 us: fetch_weights(): lax.all_gather(type_table, 'blk', axis=1, tiled=True)]
    unnamed x21 -> x0, waiting for transfers between devices: 118 us -> none
    dot_general x41 -> x14, matrix products: 155 us -> 47.9 us  [the longest x1 8.41 us: layer_in_planes(): inner = jnp.dot(first_low, up_own, preferred_element_type=F32) + up_bias]
    unnamed x1 -> x0, blocking collectives: 59.7 us -> none
  transfers between devices with their start and end apart: 23 -> 0, of which waited for: 15 -> 0; matrix products, arithmetic and copies ran while one was open for 15% -> 0% of each run, Pallas kernels for 0% -> 0%
where the time goes in v2:
time: 468 us; the launch traced here: 467 us
  Pallas kernels  376 us (80%)
  matrix products  47.9 us (10%)
  other arithmetic  24.7 us (5%)
  local copies, waits for them, and re-layouts  17.6 us (4%)
    pallas_call x14, Pallas kernels, fused(): pl.pallas_call(kernel, name=name, out_shape=[jax.ShapeDtypeStruct(s, d) f...  376 us

profile of v2, /device:TPU:0, one launch (start us, length us, event | category | flops | bytes accessed | tf_op | source)
XLA Modules:
  0.0 467.0 jit_solution(5679790781622915660)
XLA Ops:
  0.7 1.5 reshape.361
  6.0 18.5 %opening.1 = (f32[16,8,128]{2,1,0:T(8,128)}, bf16[2,64,1024]{2,1,0:T(8,128)(2,1)}, bf16[4,64,384]{2,1,0:T(8,128)(2,1)}, bf16[4,64,512]{2,1,0:T(8,128)(2,1)}) custom-call(f32[8,128]{1,0:T(8,128)} %pad_maximum_fusion.5.refs_0_, bf16[64,1024]{1,0:T(8,128)(2,1)} %refs_1_.1, bf16[4,64,384]{2,1,0:T(8,128)(2,1)} %reshape.360.refs_2_, ...), custom_call_target="tpu_custom_call" | custom-call | tf_op jit(solution)/shard_map/opening/pallas_call | solution.py:95
  24.5 0.9 reshape.365
  25.6 0.9 convert_subtract_fusion
  26.4 3.9 fusion.2
  30.4 43.3 %rows.1 = (f32[128,1024]{1,0:T(8,128)}, bf16[4,4,64,384]{3,2,1,0:T(8,128)(2,1)}) custom-call(bf16[4,2,2,128,1024]{4,3,2,1,0:T(8,128)(2,1)} %bitcast.129, bf16[4,64,384]{2,1,0:T(8,128)(2,1)} %get-tuple-element.45.refs_1_), custom_call_target="tpu_custom_call" | custom-call | tf_op jit(solution)/shard_map/rows/pallas_call | solution.py:95
  74.1 1.9 fusion.20
  76.7 15.4 %gather_tokens.1 = (bf16[2,8,64,1024]{3,2,1,0:T(8,128)(2,1)}, bf16[4,4,64,256]{3,2,1,0:T(8,128)(2,1)}) custom-call(bf16[2,64,1024]{2,1,0:T(8,128)(2,1)} %bitcast.150, bf16[4,64,256]{2,1,0:T(8,128)(2,1)} %get-tuple-element.120.refs_1_), custom_call_target="tpu_custom_call" | custom-call | tf_op jit(solution)/shard_map/gather_tokens/pallas_call | solution.py:95
  92.1 3.6 add_convert_fusion.1
  96.4 40.9 %attend.1 = (bf16[2,64,1024]{2,1,0:T(8,128)(2,1)}, bf16[3,64,2048]{2,1,0:T(8,128)(2,1)}, f32[64,2048]{1,0:T(8,128)}, f32[1,2048]{1,0:T(1,128)}, bf16[4,64,1024]{2,1,0:T(8,128)(2,1)}) custom-call(bf16[3,2,64,1024]{3,2,1,0:T(8,128)(2,1)} %bitcast.153, bf16[64,1024]{1,0:T(8,128)(2,1)} %get-tuple-element.118.refs_1_), custom_call_target="tpu_custom_call" | custom-call | tf_op jit(solution)/shard_map/attend/pallas_call | solution.py:95
  137.4 3.1 bitcast_convert_fusion
  140.4 18.3 %scatter_branch.1 = (f32[2,64,1024]{2,1,0:T(8,128)}, bf16[4,4,64,256]{3,2,1,0:T(8,128)(2,1)}) custom-call(bf16[2,8,64,1024]{3,2,1,0:T(8,128)(2,1)} %bitcast.125, bf16[4,64,256]{2,1,0:T(8,128)(2,1)} %get-tuple-element.119.refs_1_), custom_call_target="tpu_custom_call" | custom-call | tf_op jit(solution)/shard_map/scatter_branch/pallas_call | solution.py:95
  158.8 1.3 fusion.30
  160.5 0.9 fusion.19
  161.3 16.5 %gather_first.1 = (bf16[2,8,64,1024]{3,2,1,0:T(8,128)(2,1)}, bf16[4,64,1024]{2,1,0:T(8,128)(2,1)}) custom-call(bf16[2,64,1024]{2,1,0:T(8,128)(2,1)} %bitcast.148, bf16[64,1024]{1,0:T(8,128)(2,1)} %get-tuple-element.117.refs_1_), custom_call_target="tpu_custom_call" | custom-call | tf_op jit(solution)/shard_map/gather_first/pallas_call | solution.py:95
  177.8 1.1 pad_maximum_fusion.1
  179.0 1.7 pad_maximum_fusion
  180.8 8.4 %multiply_convert_fusion = (bf16[1024,512]{1,0:T(8,128)(2,1)S(1)}, f32[1024,512]{1,0:T(8,128)}, f32[1024,512]{1,0:T(8,128)}) fusion(f32[512]{0:T(512)S(1)} %bitcast.164, bf16[1024,1024]{1,0:T(8,128)(2,1)} %bitcast.169, bf16[1024,512]{1,0:T(8,128)(2,1)S(1)} %bitcast.142), kind=kOutput, calls=%fused_computation.11 | convolution fusion | flops 1108344832 | bytes 8390656 | tf_op jit(solution)/shard_map/dot_general | solution.py:1438
  189.2 2.6 convolution_convert_fusion.2
  191.8 16.0 %scatter_second.1 = f32[2,64,1024]{2,1,0:T(8,128)} custom-call(bf16[2,8,64,1024]{3,2,1,0:T(8,128)(2,1)} %bitcast.131), custom_call_target="tpu_custom_call" | custom-call | tf_op jit(solution)/shard_map/scatter_second/pallas_call | solution.py:95
  207.9 1.3 fusion.27
  209.9 1.0 fusion.26
  211.6 14.8 %gather_grad.1 = bf16[2,8,64,1024]{3,2,1,0:T(8,128)(2,1)} custom-call(bf16[2,64,1024]{2,1,0:T(8,128)(2,1)} %bitcast.149), custom_call_target="tpu_custom_call" | custom-call | tf_op jit(solution)/shard_map/gather_grad/pallas_call | solution.py:95
  226.5 5.3 %convert_reduce_fusion = (f32[512]{0:T(512)S(1)}, bf16[1024,512]{1,0:T(8,128)(2,1)S(1)}) fusion(f32[1024,512]{1,0:T(8,128)} %get-tuple-element.109, f32[1024,512]{1,0:T(8,128)} %get-tuple-element.125, f32[512]{0:T(512)S(1)} %bitcast.165, bf16[1024,1024]{1,0:T(8,128)(2,1)} %bitcast.127, bf16[512,1024]{1,0:T(8,128)(2,1)} %bitcast.145), kind=kOutput, calls=%fused_computation.8 | convolution fusion | flops 1082654208 | bytes 8392704 | tf_op jit(solution)/shard_map/rd,fd->rf/dot_general | solution.py:1460
  231.8 1.3 convolution_convert_fusion.3
  233.1 1.1 fusion.32
  235.1 1.3 convolution_convert_fusion.4
  236.4 1.0 fusion.33
  237.4 2.6 convolution_convert_fusion.1
  240.0 28.1 %scatter_first.1 = (f32[2,64,1024]{2,1,0:T(8,128)}, bf16[64,1024]{1,0:T(8,128)(2,1)}, bf16[4,64,256]{2,1,0:T(8,128)(2,1)}) custom-call(bf16[2,8,64,1024]{3,2,1,0:T(8,128)(2,1)} %bitcast.133, bf16[4,64,1024]{2,1,0:T(8,128)(2,1)} %get-tuple-element.115.refs_1_, bf16[4,4,64,256]{3,2,1,0:T(8,128)(2,1)} %get-tuple-element.113.refs_2_), custom_call_target="tpu_custom_call" | custom-call | tf_op jit(solution)/shard_map/scatter_first/pallas_call | solution.py:95
  268.1 1.4 multiply_reduce_fusion.2
  270.6 28.9 %gather_branch.1 = (bf16[2,8,64,1024]{3,2,1,0:T(8,128)(2,1)}, bf16[64,1024]{1,0:T(8,128)(2,1)}, bf16[4,64,256]{2,1,0:T(8,128)(2,1)}) custom-call(bf16[2,64,1024]{2,1,0:T(8,128)(2,1)} %bitcast.147, bf16[4,64,1024]{2,1,0:T(8,128)(2,1)} %get-tuple-element.114.refs_1_, bf16[4,4,64,256]{3,2,1,0:T(8,128)(2,1)} %get-tuple-element.112.refs_2_), custom_call_target="tpu_custom_call" | custom-call | tf_op jit(solution)/shard_map/gather_branch/pallas_call | solution.py:95
  299.6 1.8 pad_maximum_fusion.3.refs_6_
  301.3 1.6 pad_maximum_fusion.2.refs_5_
  303.0 2.7 convolution_convert_fusion.6
  305.7 1.6 convolution_convert_fusion.7
  307.3 43.8 %attend_back.1 = (bf16[3,2,64,1024]{3,2,1,0:T(8,128)(2,1)}, f32[64,1024]{1,0:T(8,128)}, bf16[64,4096]{1,0:T(8,128)(2,1)}, bf16[2,128,1024]{2,1,0:T(8,128)(2,1)}) custom-call(bf16[2,64,1024]{2,1,0:T(8,128)(2,1)} %bitcast.139, bf16[3,64,2048]{2,1,0:T(8,128)(2,1)} %get-tuple-element.60.refs_1_, f32[64,2048]{1,0:T(8,128)} %get-tuple-element.61.refs_2_, ...), custom_call_target="tpu_custom_call" | custom-call | tf_op jit(solution)/shard_map/attend_back/pallas_call | solution.py:95
  351.1 3.4 convolution_convert_fusion.5
  354.5 2.6 convolution_convert_fusion
  357.8 19.9 %scatter_back.1 = (f32[2,64,1024]{2,1,0:T(8,128)}, bf16[4,64,384]{2,1,0:T(8,128)(2,1)}, bf16[2,64,1024]{2,1,0:T(8,128)(2,1)}) custom-call(bf16[2,8,64,1024]{3,2,1,0:T(8,128)(2,1)} %bitcast.134, bf16[4,4,64,384]{3,2,1,0:T(8,128)(2,1)} %bitcast.154, bf16[64,1024]{1,0:T(8,128)(2,1)} %convert_element_type.169.refs_2_), custom_call_target="tpu_custom_call" | custom-call | tf_op jit(solution)/shard_map/scatter_back/pallas_call | solution.py:95
  377.8 1.2 multiply_reduce_fusion
  382.1 42.8 %closing.1 = (bf16[4,2,2,128,1024]{4,3,2,1,0:T(8,128)(2,1)}, f32[8,128]{1,0:T(8,128)}, bf16[64,3072]{1,0:T(8,128)(2,1)}) custom-call(bf16[128,1024]{1,0:T(8,128)(2,1)} %convert_element_type.170.refs_0_, f32[16,8,128]{2,1,0:T(8,128)} %pad.4.refs_1_, bf16[4,64,384]{2,1,0:T(8,128)(2,1)} %get-tuple-element.70.refs_2_), custom_call_target="tpu_custom_call" | custom-call | tf_op jit(solution)/shard_map/closing/pallas_call | solution.py:95
  424.9 5.5 %fusion.11 = bf16[512,1024]{1,0:T(8,128)(2,1)} fusion(bf16[2048,1024]{1,0:T(8,128)(2,1)} %bitcast.166, s32[2048]{0:T(1024)S(1)} %bitcast.162), kind=kOutput, calls=%fused_computation.31 | convolution fusion | flops 2149056512 | bytes 5251072 | tf_op jit(solution)/shard_map/dot_general | solution.py:1579
  430.4 28.3 %pos_sum.1 = f32[8,64,1024]{2,1,0:T(8,128)} custom-call(bf16[8,64,1024]{2,1,0:T(8,128)(2,1)} %bitcast.135), custom_call_target="tpu_custom_call" | custom-call | tf_op jit(solution)/shard_map/pos_sum/pallas_call | solution.py:95
  458.7 0.9 convert_element_type.178
  462.9 1.1 bitcast_convert_fusion.1
  464.0 1.0 convert_element_type.181
  465.1 1.3 copy.41
  (159 shorter events, 17.4 us)
Async XLA Ops:
  0.6 25.8 %copy-start = (bf16[512,1024]{1,0:T(8,128)(2,1)S(1)}, bf16[512,1024]{1,0:T(8,128)(2,1)}, u32[]{:S(2)}) copy-start(bf16[512,1024]{1,0:T(8,128)(2,1)} %param.17) | copy-start | bytes 3145732
  0.7 3.1 copy-start.18
  2.2 2.9 copy-start.36
  2.2 3.0 copy-start.27
  2.2 3.0 copy-start.29
  2.2 2.9 copy-start.30
  2.3 3.0 copy-start.28
  30.4 43.6 %copy-start.35 = (s32[2,64]{1,0:T(2,128)S(1)}, s32[2,64]{1,0:T(2,128)}, u32[]{:S(2)}) copy-start(s32[2,64]{1,0:T(2,128)} %param.15) | copy-start | bytes 1540
  30.4 43.7 %copy-start.11 = (bf16[2,64,1024]{2,1,0:T(8,128)(2,1)S(1)}, bf16[2,64,1024]{2,1,0:T(8,128)(2,1)}, u32[]{:S(2)}) copy-start(bf16[2,64,1024]{2,1,0:T(8,128)(2,1)} %param.13) | copy-start | bytes 786436
  30.4 45.6 %copy-start.21 = (bf16[4,64,512]{2,1,0:T(8,128)(2,1)S(1)}, bf16[4,64,512]{2,1,0:T(8,128)(2,1)}, u32[]{:S(2)}) copy-start(bf16[4,64,512]{2,1,0:T(8,128)(2,1)} %get-tuple-element.48) | copy-start | bytes 786436
  73.6 18.5 %copy-start.33 = (bf16[4,4,64,384]{3,2,1,0:T(8,128)(2,1)S(1)}, bf16[4,4,64,384]{3,2,1,0:T(8,128)(2,1)}, u32[]{:S(2)}) copy-start(bf16[4,4,64,384]{3,2,1,0:T(8,128)(2,1)} %get-tuple-element.47) | copy-start | bytes 2359300
  92.1 3.6 copy-start.22
  92.1 45.2 %copy-start.8 = (bf16[2,64,1024]{2,1,0:T(8,128)(2,1)S(1)}, bf16[2,64,1024]{2,1,0:T(8,128)(2,1)}, u32[]{:S(2)}) copy-start(bf16[2,64,1024]{2,1,0:T(8,128)(2,1)} %get-tuple-element.51) | copy-start | bytes 786436
  137.3 21.4 %copy-start.7 = (f32[128,1024]{1,0:T(8,128)S(1)}, f32[128,1024]{1,0:T(8,128)}, u32[]{:S(2)}) copy-start(f32[128,1024]{1,0:T(8,128)} %get-tuple-element.46) | copy-start | bytes 1572868
  158.7 19.1 %copy-start.17 = (bf16[4,64,1024]{2,1,0:T(8,128)(2,1)S(1)}, bf16[4,64,1024]{2,1,0:T(8,128)(2,1)}, u32[]{:S(2)}) copy-start(bf16[4,64,1024]{2,1,0:T(8,128)(2,1)} %get-tuple-element.56) | copy-start | bytes 1572868
  179.0 10.2 %copy-start.10 = (bf16[4,128,1024]{2,1,0:T(8,128)(2,1)}, bf16[4,128,1024]{2,1,0:T(8,128)(2,1)S(1)}, u32[]{:S(2)}) copy-start(bf16[4,128,1024]{2,1,0:T(8,128)(2,1)S(1)} %pad_maximum_fusion.1) | copy-start | bytes 3145732
  189.2 2.6 copy-start.12
  191.8 17.6 %copy-start.5 = (bf16[2,64,1024]{2,1,0:T(8,128)(2,1)S(1)}, bf16[2,64,1024]{2,1,0:T(8,128)(2,1)}, u32[]{:S(2)}) copy-start(bf16[2,64,1024]{2,1,0:T(8,128)(2,1)} %param.16) | copy-start | bytes 786436
  226.5 5.3 %copy-start.32 = (bf16[2,8,64,1024]{3,2,1,0:T(8,128)(2,1)S(1)}, bf16[2,8,64,1024]{3,2,1,0:T(8,128)(2,1)}, u32[]{:S(2)}) copy-start(bf16[2,8,64,1024]{3,2,1,0:T(8,128)(2,1)} %get-tuple-element.53) | copy-start | bytes 6291460
  231.8 2.4 copy-start.13
  233.1 2.0 copy-start.4
  269.5 30.1 %copy-start.24 = (bf16[64,1024]{1,0:T(8,128)(2,1)S(1)}, bf16[64,1024]{1,0:T(8,128)(2,1)}, u32[]{:S(2)}) copy-start(bf16[64,1024]{1,0:T(8,128)(2,1)} %get-tuple-element.65) | copy-start | bytes 393220
  269.5 31.8 %copy-start.23 = (bf16[4,64,256]{2,1,0:T(8,128)(2,1)S(1)}, bf16[4,64,256]{2,1,0:T(8,128)(2,1)}, u32[]{:S(2)}) copy-start(bf16[4,64,256]{2,1,0:T(8,128)(2,1)} %get-tuple-element.63) | copy-start | bytes 393220
  269.5 33.4 %copy-start.9 = (bf16[2,64,1024]{2,1,0:T(8,128)(2,1)S(1)}, bf16[2,64,1024]{2,1,0:T(8,128)(2,1)}, u32[]{:S(2)}) copy-start(bf16[2,64,1024]{2,1,0:T(8,128)(2,1)} %get-tuple-element.50) | copy-start | bytes 786436
  299.6 6.2 %copy-start.2 = (bf16[2,8,64,1024]{3,2,1,0:T(8,128)(2,1)S(1)}, bf16[2,8,64,1024]{3,2,1,0:T(8,128)(2,1)}, u32[]{:S(2)}) copy-start(bf16[2,8,64,1024]{3,2,1,0:T(8,128)(2,1)} %get-tuple-element.59) | copy-start | bytes 6291460
  305.7 45.4 %copy-start.31 = (bf16[2,8,64,1024]{3,2,1,0:T(8,128)(2,1)S(1)}, bf16[2,8,64,1024]{3,2,1,0:T(8,128)(2,1)}, u32[]{:S(2)}) copy-start(bf16[2,8,64,1024]{3,2,1,0:T(8,128)(2,1)} %get-tuple-element.49) | copy-start | bytes 6291460
  351.1 3.5 copy-start.14
  351.1 3.4 copy-start.34
  354.5 2.6 copy-start.20
  379.0 51.3 %copy-start.6 = (f32[128,1024]{1,0:T(8,128)}, f32[128,1024]{1,0:T(8,128)S(1)}, u32[]{:S(2)}) copy-start(f32[128,1024]{1,0:T(8,128)S(1)} %get-tuple-element.94) | copy-start | bytes 1572868
  430.3 28.3 %copy-start.19 = (bf16[64,3072]{1,0:T(8,128)(2,1)S(1)}, bf16[64,3072]{1,0:T(8,128)(2,1)}, u32[]{:S(2)}) copy-start(bf16[64,3072]{1,0:T(8,128)(2,1)} %get-tuple-element.73) | copy-start | bytes 1179652
  430.4 29.3 %copy-start.26 = (f32[8,128]{1,0:T(8,128)S(1)}, f32[8,128]{1,0:T(8,128)}, u32[]{:S(2)}) copy-start(f32[8,128]{1,0:T(8,128)} %get-tuple-element.72) | copy-start | bytes 12292
  430.4 31.8 %copy-start.25 = (bf16[2,64,1024]{2,1,0:T(8,128)(2,1)S(1)}, bf16[2,64,1024]{2,1,0:T(8,128)(2,1)}, u32[]{:S(2)}) copy-start(bf16[2,64,1024]{2,1,0:T(8,128)(2,1)} %get-tuple-element.74) | copy-start | bytes 786436
  430.4 32.6 %copy-start.16 = (bf16[2,128,1024]{2,1,0:T(8,128)(2,1)S(1)}, bf16[2,128,1024]{2,1,0:T(8,128)(2,1)}, u32[]{:S(2)}) copy-start(bf16[2,128,1024]{2,1,0:T(8,128)(2,1)} %get-tuple-element.76) | copy-start | bytes 1572868
  458.7 5.3 %copy-start.15 = (bf16[64,4096]{1,0:T(8,128)(2,1)S(1)}, bf16[64,4096]{1,0:T(8,128)(2,1)}, u32[]{:S(2)}) copy-start(bf16[64,4096]{1,0:T(8,128)(2,1)} %get-tuple-element.75) | copy-start | bytes 1572868
  459.6 5.4 %copy-start.3 = (f32[8,64,1024]{2,1,0:T(8,128)S(1)}, f32[8,64,1024]{2,1,0:T(8,128)}, u32[]{:S(2)}) copy-start(f32[8,64,1024]{2,1,0:T(8,128)} %pos_sum.1) | copy-start | bytes 6291460
  465.1 2.0 copy-start.1

commit v3 on v2

--- a/solution.py
+++ b/solution.py
@@ -60,6 +60,11 @@
 class Part:
     def __init__(self, run, ins, outs, scratch, peers):
         self.run, self.ins, self.outs, self.scratch, self.peers = run, ins, outs, scratch, peers
+        self.turns = ()
+
+    def on(self, *turns):
+        self.turns = turns
+        return self
 
 
 def fused(name, cid, parts, limit=None):
@@ -88,7 +93,11 @@
         pl.semaphore_wait(barrier, len(peers))
         for gen in gens:
             next(gen)
-        for gen in gens:
+        for turn, _ in enumerate(gens[0]):
+            for part, gen in zip(parts, gens):
+                if turn in part.turns:
+                    next(gen)
+        for gen in gens[1:]:
             for _ in gen:
                 pass
 
@@ -346,6 +355,25 @@
     return Part(run, [x], [((r, width), x.dtype)], [sems(7 * pieces)], PLANE)
 
 
+def sum_spread(x, width, spots):
+    planes, four, r, n = x.shape
+    first = line_sum(x)
+    second = plane_spread(jax.ShapeDtypeStruct((four, r, n), BF16), width, spots)
+
+    def run(ins, outs, own):
+        count = len(first.scratch)
+        total = own[-1]
+        yield from first.run(ins, (total,), own[:count])
+        yield from second.run((total,), outs, own[count:-1])
+
+    scratch = first.scratch + second.scratch + [pltpu.VMEM((four, r, n), BF16)]
+    return Part(run, [x], second_outs(second, BF16), scratch, tuple(COLUMN) + tuple(PLANE))
+
+
+def second_outs(part, dtype):
+    return [(shape, dtype) for shape, _ in part.outs]
+
+
 def place_copy(src, dst, send_sem, recv_sem, device):
     return pltpu.make_async_remote_copy(
         src_ref=src,
@@ -404,7 +432,7 @@
     two, r, n = x.shape
 
     def run(ins, outs, own):
-        (x_ref,), (out_ref,), (held, send, recv) = ins, outs, own
+        (x_ref,), (out_ref,), (held, total, send, recv, pair) = ins, outs, own
         h, o, y, c = place()
         has = o // 2 == h
 
@@ -419,28 +447,44 @@
 
         each(lambda copy: copy.start())
         yield
-        out_ref[...] = jnp.zeros_like(out_ref)
+        total[...] = jnp.zeros_like(total)
         for z in range(4):
             mine = (z == o) & (o % 2 == y) & (y == c)
 
             @pl.when(has & mine)
             def _():
-                out_ref[...] += x_ref[c].astype(F32)
+                total[...] += x_ref[c].astype(F32)
 
             @pl.when(has & jnp.logical_not(mine))
             def _():
                 ref = held.at[z]
                 place_copy(ref, ref, send.at[0], recv.at[z], (h, blk(o, y, c))).wait_recv()
-                out_ref[...] += held[z].astype(F32)
-
+                total[...] += held[z].astype(F32)
+
+        @pl.when(has)
+        def _():
+            out_ref[...] = total[...].astype(BF16)
+            remote(out_ref, out_ref, pair, 0, peer(*NEAR_X)).start()
+
+        yield
         each(lambda copy: copy.wait_send())
+
+        @pl.when(has)
+        def _():
+            remote(out_ref, out_ref, pair, 0, peer(*NEAR_X)).wait_send()
+
+        @pl.when(jnp.logical_not(has))
+        def _():
+            landed(out_ref, pair, 0)
 
     scratch = [
         pltpu.VMEM((4, r, n), BF16),
+        pltpu.VMEM((r, n), F32),
         pltpu.SemaphoreType.DMA((2,)),
         pltpu.SemaphoreType.DMA((4,)),
+        sems(1),
     ]
-    return Part(run, [x], [((r, n), F32)], scratch, BLK)
+    return Part(run, [x], [((r, n), BF16)], scratch, BLK + (NEAR_X,))
 
 
 def mirrored():
@@ -832,6 +876,7 @@
         low[0] = (dq[...] * scale).astype(BF16)
         for i in range(3):
             back(pl.ds(0, 1), qsem, i, (o + 1 + i) % 4).start()
+        yield
         back_ref[:, o % 2, :, mine] = low[:, :, pl.ds(pl.multiple_of(o * n, n), n)]
         for i in range(3):
             back(late, ksem, i, (o + 1 + i) % 4).wait_send()
@@ -858,6 +903,569 @@
             sems(3),
         ],
         COLUMN,
+    )
+
+
+def gather_steps(src, dst, sem):
+    h, o, y, c = place()
+    dev_x, dev_y, dev_c = peer(*NEAR_X), peer(*NEAR_Y), peer(*NEAR_C)
+    mine = h * 4 + y * 2 + c
+    of_x = (1 - h) * 4 + y * 2 + c
+    of_y = h * 4 + (1 - y) * 2 + c
+    of_d = (1 - h) * 4 + (1 - y) * 2 + c
+    flip = 1 - 2 * c
+    sent = []
+
+    def go(ref, slot, half, index, device):
+        copy = remote(ref, dst(half, slot), sem, index, device)
+        copy.start()
+        sent.append(copy)
+
+    go(src(0), mine, 0, 0, dev_x)
+    go(src(1), mine, 1, 1, dev_y)
+    go(src(1), mine, 1, 2, dev_x)
+    go(src(0), mine, 0, 3, dev_y)
+    go(src(0), mine, 0, 4, dev_c)
+    go(src(1), mine, 1, 5, dev_c)
+    for half in range(2):
+        dst(half, mine)[...] = src(half)[...]
+
+    def relay(slot, half, index, device, onward, to_core):
+        landed(dst(half, slot), sem, index)
+        if onward is not None:
+            go(dst(half, slot), slot, half, onward, device)
+        go(dst(half, slot), slot, half, to_core, dev_c)
+
+    yield
+    relay(of_x, 0, 0, dev_y, 6, 8)
+    relay(of_y, 1, 1, dev_x, 7, 9)
+    yield
+    relay(of_x, 1, 2, None, None, 10)
+    relay(of_y, 0, 3, None, None, 11)
+    yield
+    relay(of_d, 0, 6, None, None, 12)
+    relay(of_d, 1, 7, None, None, 13)
+    yield
+    for slot, half, index in (
+        (mine, 0, 4),
+        (mine, 1, 5),
+        (of_x, 0, 8),
+        (of_y, 1, 9),
+        (of_x, 1, 10),
+        (of_y, 0, 11),
+        (of_d, 0, 12),
+        (of_d, 1, 13),
+    ):
+        landed(dst(half, slot + flip), sem, index)
+    for copy in sent:
+        copy.wait_send()
+
+
+def scatter_steps(src, total, near, part, from_x, from_y, diag, sem):
+    h, o, y, c = place()
+    dev_x, dev_y, dev_c = peer(*NEAR_X), peer(*NEAR_Y), peer(*NEAR_C)
+    mine = h * 4 + y * 2 + c
+    of_x = (1 - h) * 4 + y * 2 + c
+    of_y = h * 4 + (1 - y) * 2 + c
+    of_d = (1 - h) * 4 + (1 - y) * 2 + c
+    flip = 1 - 2 * c
+    order = (of_d, of_x, of_y, mine)
+    sent = []
+
+    def go(ref, to, index, device):
+        copy = remote(ref, to, sem, index, device)
+        copy.start()
+        sent.append(copy)
+
+    for k, half in ((0, 0), (0, 1), (1, 0), (2, 1), (1, 1), (2, 0), (3, 0), (3, 1)):
+        go(src(half, order[k] + flip), near.at[k, half], 2 * k + half, dev_c)
+
+    def add(k, half):
+        landed(near.at[k, half], sem, 2 * k + half)
+        return src(half, order[k])[...].astype(F32) + near[k, half].astype(F32)
+
+    yield
+    part[0, 0] = add(0, 0).astype(BF16)
+    go(part.at[0, 0], diag.at[0], 8, dev_x)
+    part[0, 1] = add(0, 1).astype(BF16)
+    go(part.at[0, 1], diag.at[1], 9, dev_y)
+    part[1, 0] = add(1, 0).astype(BF16)
+    go(part.at[1, 0], from_x.at[0], 10, dev_x)
+    part[2, 1] = add(2, 1).astype(BF16)
+    go(part.at[2, 1], from_y.at[1], 11, dev_y)
+    yield
+    kept_x = add(1, 1)
+    landed(diag.at[1], sem, 9)
+    part[1, 1] = (kept_x + diag[1].astype(F32)).astype(BF16)
+    go(part.at[1, 1], from_x.at[1], 12, dev_x)
+    kept_y = add(2, 0)
+    landed(diag.at[0], sem, 8)
+    part[2, 0] = (kept_y + diag[0].astype(F32)).astype(BF16)
+    go(part.at[2, 0], from_y.at[0], 13, dev_y)
+    yield
+    own = [add(3, half) for half in range(2)]
+    for half, ix, iy in ((0, 10, 13), (1, 12, 11)):
+        landed(from_x.at[half], sem, ix)
+        landed(from_y.at[half], sem, iy)
+        total(half)[...] = own[half] + from_x[half].astype(F32) + from_y[half].astype(F32)
+    for copy in sent:
+        copy.wait_send()
+
+
+def scatter_scratch(r, n):
+    block = (2, r // 2, n)
+    return [
+        pltpu.VMEM((4,) + block, BF16),
+        pltpu.VMEM((3,) + block, BF16),
+        pltpu.VMEM(block, BF16),
+        pltpu.VMEM(block, BF16),
+        pltpu.VMEM(block, BF16),
+        sems(14),
+    ]
+
+
+def norm_parts(r):
+    centred = r - jnp.mean(r, axis=-1, keepdims=True)
+    scale = lax.rsqrt(jnp.mean(centred * centred, axis=-1, keepdims=True) + 1e-12)
+    return centred * scale, scale
+
+
+def norm_back(xh, scale, dh):
+    return (
+        dh
+        - jnp.mean(dh, axis=-1, keepdims=True)
+        - xh * jnp.mean(dh * xh, axis=-1, keepdims=True)
+    ) * scale
+
+
+def dot_nt(a, b):
+    return lax.dot_general(a, b, (((1,), (1,)), ((), ())), preferred_element_type=F32)
+
+
+def dot_tn(a, b):
+    return lax.dot_general(a, b, (((0,), (0,)), ((), ())), preferred_element_type=F32)
+
+
+def middle(branch, embedded, cotangent, up_one, up_cut, down_one, down_cut, up_bias, vectors, lag):
+    seqs, eight, r, d = branch.shape
+    half = r // 2
+    planes, four, e, fh = up_one.shape
+    f = 2 * fh
+    fcols = down_cut.shape[0]
+    dh_cols = d // 2
+    rows = 8 * r
+    q_rows = rows // 2
+
+    def run(ins, outs, own):
+        (x_ref, emb_ref, cot_ref, up1, up_src, down1, down_src, bias_ref, vec_ref) = ins
+        (out_ref, resid_ref, branch_out, down_sum, up_sum, sums_ref, bias_sum) = outs
+        it = iter(own)
+        up2, down2, up_sem, down_sem = (next(it) for _ in range(4))
+        first_g, grad_g, second, third, act, slope, inner_grad = (next(it) for _ in range(7))
+        first, xh_one, scale_one, grad_two, low, total = (next(it) for _ in range(6))
+        down_part, down_held, sum_sem = (next(it) for _ in range(3))
+        up_part, up_held, up_sum_sem = (next(it) for _ in range(3))
+        streams = []
+        for s in range(seqs):
+            scatters = [[next(it) for _ in range(6)] for _ in range(3)]
+            streams.append((scatters, [next(it) for _ in range(3)]))
+        o = place()[1]
+
+        weights = []
+        for k, p in enumerate(COLUMN):
+            for src, dst, sem in ((up_src, up2, up_sem), (down_src, down2, down_sem)):
+                copy = remote(src, dst.at[o], sem, k, peer(*p))
+                copy.start()
+                weights.append(copy)
+        up2[pl.ds(o, 1)] = up_src[...][None]
+        down2[pl.ds(o, 1)] = down_src[...][None]
+        sums_ref[...] = jnp.zeros_like(sums_ref)
+        bias_sum[...] = jnp.zeros_like(bias_sum)
+        yield
+
+        ups = [lambda: up1[...].reshape(d, fh), lambda: up2[...].reshape(d, fh)]
+        downs = [lambda: down1[...].reshape(f, dh_cols), lambda: down2[...].reshape(f, dh_cols)]
+        vec = lambda k: vec_ref[k : k + 1]
+
+        def piece(ref, s):
+            return lambda i, slot: ref.at[s, slot, pl.ds(i * half, half)]
+
+        def plain(ref, s):
+            return lambda i: ref.at[s, pl.ds(i * half, half)]
+
+        def quarter(ref, s, q):
+            return ref[s, 4 * q : 4 * q + 4].reshape(q_rows, d)
+
+        def note(k, value):
+            sums_ref[k : k + 1] += jnp.sum(value, axis=0, keepdims=True)
+
+        def stream(s):
+            scatters, gathers = streams[s]
+            at = lambda q: pl.ds(s * rows + q * q_rows, q_rows)
+            yield from scatter_steps(piece(x_ref, s), plain(total, s), *scatters[0])
+            xh, scale = norm_parts(emb_ref[s] + (total[s] + vec(0)))
+            xh_one[s] = xh
+            scale_one[s] = scale
+            value = xh * vec(4) + vec(1)
+            first[s] = value
+            low[s] = value.astype(BF16)
+            yield from gather_steps(plain(low, s), piece(first_g, s), gathers[0])
+            if s == 0:
+                for copy in weights:
+                    copy.wait()
+            for q in range(2):
+                rows_in = quarter(first_g, s, q)
+                for k in range(2):
+                    cols = slice(k * fh, (k + 1) * fh)
+                    inner = jnp.dot(rows_in, ups[k](), preferred_element_type=F32)
+                    inner = inner + bias_ref[:, cols]
+                    phi = 0.5 + 0.5 * lax.erf(inner * (0.5**0.5))
+                    act[at(q), cols] = (inner * phi).astype(BF16)
+                    bell = jnp.exp(inner * inner * -0.5) * (1.0 / math.sqrt(2.0 * math.pi))
+                    slope[at(q), cols] = phi + inner * bell
+                    yield
+                for k in range(2):
+                    part = jnp.dot(act[at(q)], downs[k](), preferred_element_type=F32)
+                    second[s, 4 * q : 4 * q + 4, :, k * dh_cols : (k + 1) * dh_cols] = part.astype(
+                        BF16
+                    ).reshape(4, r, dh_cols)
+                yield
+            yield from scatter_steps(piece(second, s), plain(total, s), *scatters[1])
+            xh, scale = norm_parts(first[s] + (total[s] + vec(2)))
+            out_ref[s] = (xh * vec(5) + vec(3)).astype(BF16)
+            cot = cot_ref[s].astype(F32)
+            note(5, cot * xh)
+            note(3, cot)
+            grad = norm_back(xh, scale, cot * vec(5))
+            grad_two[s] = grad
+            low[s] = grad.astype(BF16)
+            note(2, low[s].astype(F32))
+            yield from gather_steps(plain(low, s), piece(grad_g, s), gathers[1])
+            for q in range(2):
+                rows_in = quarter(grad_g, s, q)
+                back = dot_nt(rows_in[:, :dh_cols], downs[0]()) + dot_nt(
+                    rows_in[:, dh_cols:], downs[1]()
+                )
+                back = (back * slope[at(q)]).astype(BF16)
+                inner_grad[at(q)] = back
+                bias_sum[...] += jnp.sum(back.astype(F32), axis=0, keepdims=True)
+                yield
+                part = dot_nt(back[:, :fh], ups[0]()) + dot_nt(back[:, fh:], ups[1]())
+                third[s, 4 * q : 4 * q + 4] = part.astype(BF16).reshape(4, r, d)
+                yield
+            last = scatter_steps(piece(third, s), plain(total, s), *scatters[2])
+            next(last)
+            if s == seqs - 1:
+                all_grads = grad_g[...].reshape(seqs * rows, d)
+                for z in range(planes):
+                    cols = slice(z * fcols, (z + 1) * fcols)
+                    down_part[z] = dot_tn(act[:, cols], all_grads).astype(BF16)
+                    if z % 2:
+                        yield
+                send_sums(down_part, down_held, sum_sem)
+                for z in range(planes):
+                    cols = slice(z * 4 * e, (z + 1) * 4 * e)
+                    all_first = first_g[:, :, :, cols].reshape(seqs * rows, 4 * e)
+                    up_part[z] = dot_tn(all_first, inner_grad[...]).astype(BF16)
+                    if z % 2:
+                        yield
+                send_sums(up_part, up_held, up_sum_sem)
+            yield from last
+            grad = grad_two[s] + total[s]
+            note(4, grad * xh_one[s])
+            note(1, grad)
+            grad = norm_back(xh_one[s], scale_one[s], grad * vec(4))
+            resid_ref[s] = grad
+            low[s] = grad.astype(BF16)
+            note(0, low[s].astype(F32))
+            yield from gather_steps(plain(low, s), piece(branch_out, s), gathers[2])
+
+        def send_sums(part, held, sem):
+            for k, p in enumerate(COLUMN):
+                copy = remote(part.at[(o + k + 1) % 4], held.at[k], sem, k, peer(*p))
+                copy.start()
+                sums.append(copy)
+
+        sums = []
+        gens = [stream(s) for s in range(seqs)]
+        for _ in range(lag):
+            next(gens[0])
+        while gens:
+            for gen in list(gens):
+                try:
+                    next(gen)
+                except StopIteration:
+                    gens.remove(gen)
+        for copy in sums:
+            copy.wait()
+        for part, held, out in ((down_part, down_held, down_sum), (up_part, up_held, up_sum)):
+            value = part[o].astype(F32)
+            for k in range(3):
+                value += held[k].astype(F32)
+            out[...] = value.astype(BF16)
+
+    plane = (seqs, 8, r, d)
+    per_stream = []
+    for _ in range(seqs):
+        for _ in range(3):
+            per_stream += scatter_scratch(r, d)
+        per_stream += [sems(14)] * 3
+    return Part(
+        run,
+        [branch, embedded, cotangent, up_one, up_cut, down_one, down_cut, up_bias, vectors],
+        [
+            ((seqs, r, d), BF16),
+            ((seqs, r, d), F32),
+            (plane, BF16),
+            ((fcols, d), BF16),
+            ((4 * e, f), BF16),
+            ((8, d), F32),
+            ((1, f), F32),
+        ],
+        [
+            pltpu.VMEM(up_one.shape, BF16),
+            pltpu.VMEM(down_one.shape, BF16),
+            sems(3),
+            sems(3),
+            pltpu.VMEM(plane, BF16),
+            pltpu.VMEM(plane, BF16),
+            pltpu.VMEM(plane, BF16),
+            pltpu.VMEM(plane, BF16),
+            pltpu.VMEM((seqs * rows, f), BF16),
+            pltpu.VMEM((seqs * rows, f), F32),
+            pltpu.VMEM((seqs * rows, f), BF16),
+            pltpu.VMEM((seqs, r, d), F32),
+            pltpu.VMEM((seqs, r, d), F32),
+            pltpu.VMEM((seqs, r, 1), F32),
+            pltpu.VMEM((seqs, r, d), F32),
+            pltpu.VMEM((seqs, r, d), BF16),
+            pltpu.VMEM((seqs, r, d), F32),
+            pltpu.VMEM((planes, fcols, d), BF16),
+            pltpu.VMEM((3, fcols, d), BF16),
+            sems(3),
+            pltpu.VMEM((planes, 4 * e, f), BF16),
+            pltpu.VMEM((3, 4 * e, f), BF16),
+            sems(3),
+        ]
+        + per_stream,
+        (NEAR_X, NEAR_Y, NEAR_C) + COLUMN,
+    )
+
+
+def blk_gather_steps(src, spot_of, zsem, ysem, csem):
+    h, o, y, c = place()
+    at, seen = mirrored()
+    dev_y, dev_c = peer(*NEAR_Y), peer(*NEAR_C)
+    end, inner, other = (h, blk(seen(0), y, c)), (h, blk(seen(1), y, c)), (h, blk(seen(2), y, c))
+    sent = []
+
+    def spot(z, yy=y, cc=c):
+        return spot_of(z, yy, cc)
+
+    def go(ref, z, yy, sem, index, device):
+        copy = remote(ref, spot(z, yy), sem, index, device)
+        copy.start()
+        sent.append(copy)
+
+    def line(ref, z, index, device):
+        return remote(ref, spot(z), zsem, index, device)
+
+    @pl.when(at == 0)
+    def _():
+        line(src, o, 0, inner).start()
+
+    @pl.when(at == 1)
+    def _():
+        line(src, o, 1, end).start()
+        line(src, o, 2, other).start()
+
+    go(src, o, y, ysem, 0, dev_y)
+    go(src, o, y, csem, 0, dev_c)
+    spot(o)[...] = src[...]
+
+    def onward(j, z):
+        go(spot(z), z, y, ysem, j, dev_y)
+        go(spot(z), z, y, csem, j, dev_c)
+
+    first = seen(1 - at)
+    order = (o, first, seen(2), seen(3))
+
+    def from_y(j):
+        landed(spot(order[j], 1 - y), ysem, j)
+        go(spot(order[j], 1 - y), order[j], 1 - y, csem, 4 + j, dev_c)
+
+    yield
+
+    @pl.when(at == 0)
+    def _():
+        landed(spot(seen(1)), zsem, 1)
+
+    @pl.when(at == 1)
+    def _():
+        landed(spot(seen(0)), zsem, 0)
+        line(spot(seen(0)), seen(0), 3, other).start()
+
+    onward(1, first)
+
+    @pl.when(at == 1)
+    def _():
+        landed(spot(seen(2)), zsem, 2)
+        line(spot(seen(2)), seen(2), 4, end).start()
+
+    yield
+    from_y(0)
+
+    @pl.when(at == 0)
+    def _():
+        landed(spot(seen(2)), zsem, 4)
+
+    onward(2, seen(2))
+
+    @pl.when(at == 1)
+    def _():
+        landed(spot(seen(3)), zsem, 3)
+        line(spot(seen(3)), seen(3), 5, end).start()
+
+    yield
+    from_y(1)
+
+    @pl.when(at == 0)
+    def _():
+        landed(spot(seen(3)), zsem, 5)
+
+    onward(3, seen(3))
+    yield
+    from_y(2)
+    yield
+    from_y(3)
+    yield
+    for j, z in enumerate(order):
+        landed(spot(z, y, 1 - c), csem, j)
+        landed(spot(z, 1 - y, 1 - c), csem, 4 + j)
+
+    @pl.when(at == 0)
+    def _():
+        line(src, o, 0, inner).wait_send()
+
+    @pl.when(at == 1)
+    def _():
+        line(src, o, 1, end).wait_send()
+        line(src, o, 2, other).wait_send()
+        line(spot(seen(0)), seen(0), 3, other).wait_send()
+        line(spot(seen(2)), seen(2), 4, end).wait_send()
+        line(spot(seen(3)), seen(3), 5, end).wait_send()
+
+    for copy in sent:
+        copy.wait_send()
+
+
+ALL = tuple(
+    (dx, dz, dy, dc)
+    for dx in range(2)
+    for dz in range(4)
+    for dy in range(2)
+    for dc in range(2)
+    if dx or dz or dy or dc
+)
+
+
+def closing(partial, resid, ids, second, slots, chunks, lag):
+    seqs, eight, r, d = partial.shape
+    rows = seqs * r
+    w = d // chunks
+    blks = 16
+
+    def run(ins, outs, own):
+        (x_ref, resid_ref, ids_ref, second_ref), (grad_ref, pos_ref, type_ref) = ins, outs
+        it = iter(own)
+        low, gathered, pick, part, held, types, slabs = (next(it) for _ in range(7))
+        pair_sem, type_sem = next(it), next(it)
+        per_chunk = [[next(it) for _ in range(9)] for _ in range(chunks)]
+        h, o, y, c = place()
+
+        def chunk(q):
+            cols = pl.ds(q * w, w)
+            scatter, (zsem, ysem, csem) = per_chunk[q][:6], per_chunk[q][6:]
+            yield from scatter_steps(
+                lambda half, slot: x_ref.at[half, slot, :, cols],
+                lambda half: grad_ref.at[half, :, cols],
+                *scatter,
+            )
+            grad = grad_ref[:, :, cols] + resid_ref[:, :, cols]
+            grad_ref[:, :, cols] = grad
+            grad = grad.reshape(rows, w)
+            low[q] = grad.astype(BF16)
+            late = jnp.sum(grad * second_ref[...], axis=0, keepdims=True)
+            types[0:1, cols] = jnp.sum(grad * (1.0 - second_ref[...]), axis=0, keepdims=True)
+            types[1:2, cols] = late
+            yield from blk_gather_steps(
+                low.at[q], lambda z, yy, cc: gathered.at[q, blk(z, yy, cc)], zsem, ysem, csem
+            )
+            total = jnp.dot(
+                pick[...], gathered[q].reshape(blks * rows, w), preferred_element_type=F32
+            )
+            pos_ref[:, cols] = total
+            part[q] = total.astype(BF16)
+            copy = remote(part.at[q], held.at[q], pair_sem, q, peer(*NEAR_X))
+            copy.start()
+            pairs.append(copy)
+            yield
+
+        pairs = []
+        gens = [chunk(q) for q in range(chunks)]
+        next(gens[0])
+        yield
+        row = lax.broadcasted_iota(jnp.int32, (slots, 1), 0)
+        pick[...] = (ids_ref[...] == row).astype(F32).astype(BF16)
+        types[...] = jnp.zeros_like(types)
+        active, waiting = [gens[0]], gens[1:]
+        turn = 0
+        while active or waiting:
+            turn += 1
+            if waiting and turn % lag == 0:
+                active.append(waiting.pop(0))
+            for gen in list(active):
+                try:
+                    next(gen)
+                except StopIteration:
+                    active.remove(gen)
+            yield
+        copies = []
+        for k, p in enumerate(ALL):
+            to = peer(*p)
+            lanes = pl.ds(pl.multiple_of(to[1] // 2 * 128, 128), 128)
+            copy = remote(types.at[:, lanes], slabs.at[k], type_sem, k, to)
+            copy.start()
+            copies.append(copy)
+        yield
+        for q, copy in enumerate(pairs):
+            copy.wait()
+            cols = pl.ds(q * w, w)
+            pos_ref[:, cols] = pos_ref[:, cols] + held[q].astype(F32)
+        for copy in copies:
+            copy.wait()
+        mine = pl.ds(pl.multiple_of(blk(o, y, c) // 2 * 128, 128), 128)
+        type_ref[...] = types[:, mine] + jnp.sum(slabs[...], axis=0)
+
+    scratch = [
+        pltpu.VMEM((chunks, rows, w), BF16),
+        pltpu.VMEM((chunks, blks, rows, w), BF16),
+        pltpu.VMEM((slots, blks * rows), BF16),
+        pltpu.VMEM((chunks, slots, w), BF16),
+        pltpu.VMEM((chunks, slots, w), BF16),
+        pltpu.VMEM((8, d), F32),
+        pltpu.VMEM((31, 8, 128), F32),
+        sems(chunks),
+        sems(31),
+    ]
+    for _ in range(chunks):
+        scratch += scatter_scratch(2 * r, w) + [sems(6), sems(4), sems(8)]
+    return Part(
+        run,
+        [partial, resid, ids, second],
+        [((seqs, r, d), F32), ((slots, d), F32), ((8, 128), F32)],
+        scratch,
+        ALL,
     )
 
 
@@ -1303,7 +1911,10 @@
     )
 
 
-BIG = 56 << 20
+BIG = 60 << 20
+LAG = 3
+CHUNKS = 4
+CHUNK_LAG = 1
 
 
 def layer_in_planes(
@@ -1350,7 +1961,7 @@
     up_cut = lax.dynamic_slice_in_dim(up_cut, h, 1, 3).reshape(e, 4, 4, fcols)
     up_cut = up_cut.transpose(2, 0, 1, 3).reshape(4, e, 4 * fcols)
     down_cut = lax.dynamic_slice_in_dim(down_projection_weight, h * fcols, fcols, 0)
-    half_down, half_up = fcols // 2, 2 * fcols
+    half_down, half_up = width // 2, 2 * fcols
     (everyone,), (out_all,), (qkv_cut,), (up_cut,) = fused(
         "opening",
         0,
@@ -1405,92 +2016,35 @@
         3,
         [
             attend(projected.reshape(3, 2, e, plane_rows), scale),
-            line_gather(down_cut[:half_down]),
+            line_gather(down_cut[:, :half_down]),
         ],
         BIG,
     )
     attended = attended.reshape(2 * e, plane_rows)
     branch = jnp.einsum("fr,fd->rd", attended, out_own, preferred_element_type=F32).astype(BF16)
-    (branch,), (up_second,) = fused(
-        "scatter_branch",
+    vectors = jnp.concatenate([bias_float[2:6], gain_float, jnp.zeros((2, width), F32)])
+    (
+        (layer_out, grad_resid, plane_branch, got_down, up_total, norm_sums, grad_up_bias),
+    ) = fused(
+        "middle",
         4,
         [
-            plane_scatter(branch.reshape(seqs, 8, seg, width)),
-            line_gather(up_cut[:, :, half_up:]),
+            middle(
+                branch.reshape(seqs, 8, seg, width),
+                embedded.reshape(token_shape),
+                cotangent,
+                up_first,
+                up_cut[:, :, half_up:],
+                down_first,
+                down_cut[:, half_down:],
+                up_bias,
+                vectors,
+                LAG,
+            )
         ],
-    )
-    branch = branch.reshape(rows, width)
-    first, first_pull = jax.vjp(
-        norm_layer, embedded + (branch + bias_float[2]), gain_float[0], bias_float[3]
-    )
-
-    (first_low,), (down_second,) = fused(
-        "gather_first",
-        5,
-        [
-            plane_gather(first.astype(BF16).reshape(token_shape)),
-            line_gather(down_cut[half_down:]),
-        ],
-    )
-    first_low = first_low.reshape(plane_rows, width)
-    up_own = jnp.concatenate([up_first, up_second], axis=3).reshape(width, 4 * fcols)
-    down_own = jnp.concatenate([down_first, down_second], axis=1).reshape(4 * fcols, width)
-    inner = jnp.dot(first_low, up_own, preferred_element_type=F32) + up_bias
-    activated, gelu_pull = jax.vjp(gelu_exact, inner)
-    activated_low = activated.astype(BF16)
-    second = jnp.dot(activated_low, down_own, preferred_element_type=F32).astype(BF16)
-    ((second,),) = fused("scatter_second", 6, [plane_scatter(second.reshape(seqs, 8, seg, width))])
-    second = second.reshape(rows, width)
-    final, final_pull = jax.vjp(
-        norm_layer, first + (second + bias_float[4]), gain_float[1], bias_float[5]
-    )
-    layer_out = final.astype(BF16).reshape(token_shape)
-
-    grad_final, grad_gain_two, grad_shift_two = final_pull(
-        cotangent.reshape(rows, width).astype(F32)
-    )
-    grad_low = grad_final.astype(BF16)
-    grad_bias_second = jnp.sum(grad_low.astype(F32), axis=0)
-    ((plane_grad,),) = fused("gather_grad", 7, [plane_gather(grad_low.reshape(token_shape))])
-    plane_grad = plane_grad.reshape(plane_rows, width)
-    grad_down = jnp.einsum(
-        "rf,rd->fd", activated_low, plane_grad, preferred_element_type=F32
-    ).astype(BF16)
-    (grad_inner,) = gelu_pull(
-        jnp.einsum("rd,fd->rf", plane_grad, down_own, preferred_element_type=F32)
-    )
-    grad_inner_low = grad_inner.astype(BF16)
-    grad_up = jnp.einsum(
-        "rd,rf->df", first_low, grad_inner_low, preferred_element_type=F32
-    ).astype(BF16)
-    grad_up_bias = jnp.sum(grad_inner_low.astype(F32), axis=0)
-    grad_first = jnp.einsum(
-        "rf,df->rd", grad_inner_low, up_own, preferred_element_type=F32
-    ).astype(BF16)
-    grad_up = grad_up.reshape(4, 4, e, 4 * fcols)
-    grad_down = grad_down.reshape(4, fcols, width)
-    (grad_first,), (down_one,), (up_one,) = fused(
-        "scatter_first",
-        8,
-        [
-            plane_scatter(grad_first.reshape(seqs, 8, seg, width)),
-            line_sum(grad_down[:, :half_down]),
-            line_sum(grad_up[:, :, :, :half_up]),
-        ],
-    )
-    grad_first = grad_first.reshape(rows, width)
-    grad_resid, grad_gain_one, grad_shift_one = first_pull(grad_final + grad_first)
-    branch_low = grad_resid.astype(BF16)
-    grad_bias_branch = jnp.sum(branch_low.astype(F32), axis=0)
-    (plane_branch,), (down_two,), (up_two,) = fused(
-        "gather_branch",
-        9,
-        [
-            plane_gather(branch_low.reshape(token_shape)),
-            line_sum(grad_down[:, half_down:]),
-            line_sum(grad_up[:, :, :, half_up:]),
-        ],
-    )
+        BIG,
+    )
+    grad_resid = grad_resid.reshape(rows, width)
     plane_branch = plane_branch.reshape(plane_rows, width)
     grad_out = jnp.einsum(
         "fr,rd->fd", attended, plane_branch, preferred_element_type=F32
@@ -1498,18 +2052,18 @@
     grad_attended = jnp.einsum(
         "fd,rd->fr", out_own, plane_branch, preferred_element_type=F32
     ).astype(BF16)
-    (grad_qkv,), (out_total,), (got_up,), (got_down,) = fused(
+    (grad_qkv,), (got_up,), (got_down,), (got_out,) = fused(
         "attend_back",
-        10,
+        5,
         [
             attend_back(grad_attended.reshape(2, e, plane_rows), pair_qkv, pair_out, lse, scale),
-            out_grads(grad_out.reshape(2, e, width)),
             plane_spread(
-                jnp.concatenate([up_one, up_two], axis=2),
+                up_total.reshape(4, e, 4 * fcols),
                 ff,
                 lambda t: [(i * 4 + t % 4) * 2 + t // 4 for i in range(4)],
             ),
-            pair_copy(jnp.concatenate([down_one, down_two], axis=0)),
+            pair_copy(got_down),
+            out_grads(grad_out.reshape(2, e, width)).on(0),
         ],
         BIG,
     )
@@ -1519,40 +2073,17 @@
     ).astype(BF16)
     head_sums = jnp.sum(grad_qkv.astype(F32), axis=1).reshape(3, 2 * e)
     back = jnp.einsum("fr,kf->rk", grad_qkv, qkv_own, preferred_element_type=F32).astype(BF16)
-    (back,), (qkv_total,), (got_out,) = fused(
-        "scatter_back",
-        11,
-        [
-            plane_scatter(back.reshape(seqs, 8, seg, width)),
-            line_sum(grad_qkv_weight.reshape(4, 4, e, 6 * e)),
-            pair_copy(out_total.astype(BF16)),
-        ],
-    )
-    grad_embedded = grad_resid + back.reshape(rows, width)
-    grad_hidden = grad_embedded.reshape(token_shape)
-
-    second_mask = is_second.astype(F32)
-    type_one = jnp.sum(grad_embedded * second_mask, axis=0)
-    type_zero = jnp.sum(grad_embedded * (1.0 - second_mask), axis=0)
-
     def spread(part):
         whole = lax.dynamic_update_slice(
             jnp.zeros((8, 2 * e), F32), part.reshape(1, 2 * e), (h * 4 + g, 0)
         )
         return whole.reshape(width)
 
-    stacked = jnp.stack(
+    stacked = jnp.concatenate(
         [
-            spread(head_sums[0]),
-            spread(head_sums[2]),
-            grad_bias_branch,
-            grad_shift_one,
-            grad_bias_second,
-            grad_shift_two,
-            grad_gain_one,
-            grad_gain_two,
-            type_zero,
-            type_one,
+            spread(head_sums[0])[None],
+            spread(head_sums[2])[None],
+            norm_sums,
         ]
     )
     up_spread = lax.dynamic_update_slice(
@@ -1563,31 +2094,40 @@
     ).reshape(blks, 7, 2 * e)
     vector_pack = jnp.pad(vector_pack, ((0, 0), (0, 1), (0, 0)))
 
-    (all_grads,), (totals,), (got_qkv,) = fused(
+    flat_ids = all_ids.reshape(1, blks * rows) - b * slots
+    (grad_hidden, total_pos, type_slab), (totals,), (got_qkv,) = fused(
         "closing",
-        12,
+        6,
         [
-            blk_gather(grad_embedded.astype(BF16)),
+            closing(
+                back.reshape(seqs, 8, seg, width),
+                grad_resid.reshape(token_shape),
+                flat_ids,
+                is_second.astype(F32),
+                slots,
+                CHUNKS,
+                CHUNK_LAG,
+            ),
             small_scatter(vector_pack),
-            plane_spread(qkv_total, 3 * width, lambda t: [i * 8 + t for i in range(3)]),
+            sum_spread(
+                grad_qkv_weight.reshape(4, 4, e, 6 * e),
+                3 * width,
+                lambda t: [i * 8 + t for i in range(3)],
+            ).on(5),
         ],
+        BIG,
     )
     totals = totals[:7].reshape(14, e)
-    all_grads = all_grads.reshape(blks * rows, width)
-    flat_ids = all_ids.reshape(1, blks * rows) - b * slots
-    pick = (flat_ids == lax.broadcasted_iota(jnp.int32, (slots, 1), 0)).astype(BF16)
-    pos_part = jnp.dot(pick, all_grads, preferred_element_type=F32).astype(BF16)
-    ((total_pos,),) = fused("pos_sum", 13, [pair_sum(pos_part.reshape(8, slots // 8, width))])
-    total_pos = total_pos.reshape(slots, width)
+    total_types = lax.dynamic_slice_in_dim(type_slab[:2], b % 2 * e, e, 1)
     total_qkv = got_qkv.astype(F32)
     total_up = got_up.astype(F32)
     total_down = got_down.reshape(2 * fcols, width).astype(F32)
-    total_out = lax.dynamic_index_in_dim(got_out, o // 2, 0, False).astype(F32)
+    total_out = got_out.astype(F32)
     return (
         layer_out,
         grad_hidden,
         total_pos,
-        totals[8:10],
+        total_types,
         total_qkv,
         total_out,
         total_up,

time: 468 us -> 422 us (0.902)
  matrix products: 47.9 us -> 21.6 us
  other arithmetic: 24.7 us -> 10.8 us
  Pallas kernels: 376 us -> 370 us
    dot_general x7 -> x0, matrix products: 27 us -> none  [the longest x1 8.41 us: layer_in_planes(): inner = jnp.dot(first_low, up_own, preferred_element_type=F32) + up_bias]
    reduce_sum x12 -> x0, other arithmetic: 8.84 us -> none  [the longest x2 2.63 us: norm_layer(): average = jnp.mean(values_in, axis=-1, keepdims=True)]
    pallas_call x14 -> x7, Pallas kernels: 376 us -> 370 us  [fused(): pl.pallas_call(kernel, name=name, out_shape=[jax.ShapeDtypeStruct(s, d) f...]
    concatenate x4 -> x1, other arithmetic: 6.18 us -> 0.69 us  [layer_in_planes(): jnp.concatenate([bias_float[2:6], gain_float, jnp.zeros((2, width), F32)])]
where the time goes in v3:
time: 422 us
  Pallas kernels  370 us (88%)
  matrix products  21.6 us (5%)
  local copies, waits for them, and re-layouts  18.8 us (4%)
  other arithmetic  10.8 us (3%)
    pallas_call x7, Pallas kernels, fused(): pl.pallas_call(kernel, name=name, out_shape=[jax.ShapeDtypeStruct(s, d) f...  370 us

profile of v3, /device:TPU:0, one launch (start us, length us, event | category | flops | bytes accessed | tf_op | source)
XLA Modules:
  0.0 421.8 jit_solution(10320302605912700496)
XLA Ops:
  0.7 1.5 reshape.232
  2.3 0.5 constant_dynamic-slice_fusion.4
  2.8 0.1 copy.47
  3.0 0.8 reshape.234.refs_3_
  3.8 0.3 reshape.229
  4.1 0.1 copy.48
  4.2 0.8 reshape.231.refs_2_
  5.4 0.6 pad_maximum_fusion.1.refs_0_
  6.0 18.5 %opening.1 = (f32[16,8,128]{2,1,0:T(8,128)}, bf16[2,64,1024]{2,1,0:T(8,128)(2,1)}, bf16[4,64,384]{2,1,0:T(8,128)(2,1)}, bf16[4,64,512]{2,1,0:T(8,128)(2,1)}) custom-call(f32[8,128]{1,0:T(8,128)} %pad_maximum_fusion.1.refs_0_, bf16[64,1024]{1,0:T(8,128)(2,1)} %refs_1_.1, bf16[4,64,384]{2,1,0:T(8,128)(2,1)} %reshape.231.refs_2_, ...), custom_call_target="tpu_custom_call" | custom-call | tf_op jit(solution)/shard_map/opening/pallas_call | solution.py:104
  24.5 0.9 reshape.237
  25.6 0.9 convert_subtract_fusion
  26.4 3.9 fusion.1
  30.4 43.0 %rows.1 = (f32[128,1024]{1,0:T(8,128)}, bf16[4,4,64,384]{3,2,1,0:T(8,128)(2,1)}) custom-call(bf16[4,2,2,128,1024]{4,3,2,1,0:T(8,128)(2,1)} %bitcast.71, bf16[4,64,384]{2,1,0:T(8,128)(2,1)} %get-tuple-element.41.refs_1_), custom_call_target="tpu_custom_call" | custom-call | tf_op jit(solution)/shard_map/rows/pallas_call | solution.py:104
  73.7 2.0 fusion.7
  75.7 0.7 fusion.10
  76.5 15.4 %gather_tokens.1 = (bf16[2,8,64,1024]{3,2,1,0:T(8,128)(2,1)}, bf16[4,4,64,256]{3,2,1,0:T(8,128)(2,1)}) custom-call(bf16[2,64,1024]{2,1,0:T(8,128)(2,1)} %bitcast.80, bf16[4,64,256]{2,1,0:T(8,128)(2,1)} %get-tuple-element.78.refs_1_), custom_call_target="tpu_custom_call" | custom-call | tf_op jit(solution)/shard_map/gather_tokens/pallas_call | solution.py:104
  91.9 3.6 add_convert_fusion
  95.5 0.7 fusion.9
  96.2 40.9 %attend.1 = (bf16[2,64,1024]{2,1,0:T(8,128)(2,1)}, bf16[3,64,2048]{2,1,0:T(8,128)(2,1)}, f32[64,2048]{1,0:T(8,128)}, f32[1,2048]{1,0:T(1,128)}, bf16[4,128,512]{2,1,0:T(8,128)(2,1)}) custom-call(bf16[3,2,64,1024]{3,2,1,0:T(8,128)(2,1)} %bitcast.84, bf16[128,512]{1,0:T(8,128)(2,1)} %get-tuple-element.76.refs_1_), custom_call_target="tpu_custom_call" | custom-call | tf_op jit(solution)/shard_map/attend/pallas_call | solution.py:104
  137.1 3.0 bitcast_convert_fusion
  140.2 0.6 dynamic-slice_bitcast_fusion.refs_7_
  141.1 0.7 maximum_maximum_fusion.refs_8_
  141.8 126.3 %middle.1 = (bf16[2,64,1024]{2,1,0:T(8,128)(2,1)}, f32[2,64,1024]{2,1,0:T(8,128)}, bf16[2,8,64,1024]{3,2,1,0:T(8,128)(2,1)}, bf16[128,1024]{1,0:T(8,128)(2,1)}, ...) custom-call(bf16[2,8,64,1024]{3,2,1,0:T(8,128)(2,1)} %bitcast.70, f32[2,64,1024]{2,1,0:T(8,128)} %bitcast.73, ...), custom_call_target="tpu_custom_call" | custom-call | tf_op jit(solution)/shard_map/middle/pallas_call | solution.py:104
  268.1 2.9 convolution_convert_fusion.2
  271.0 1.5 convolution_convert_fusion.3
  272.6 46.3 %attend_back.1 = (bf16[3,2,64,1024]{3,2,1,0:T(8,128)(2,1)}, bf16[64,4096]{1,0:T(8,128)(2,1)}, bf16[2,128,1024]{2,1,0:T(8,128)(2,1)}, bf16[64,1024]{1,0:T(8,128)(2,1)}) custom-call(bf16[2,64,1024]{2,1,0:T(8,128)(2,1)} %bitcast.77, bf16[3,64,2048]{2,1,0:T(8,128)(2,1)} %get-tuple-element.52.refs_1_, f32[64,2048]{1,0:T(8,128)} %get-tuple-element.53.refs_2_, ...), custom_call_target="tpu_custom_call" | custom-call | tf_op jit(solution)/shard_map/attend_back/pallas_call | solution.py:104
  319.0 4.0 convolution_convert_fusion.1
  323.0 0.2 convert_reduce_fusion
  323.7 0.3 dynamic_update_slice.11
  324.2 0.6 pad.4.refs_4_
  324.9 2.6 convolution_convert_fusion
  327.5 1.5 fusion.26.refs_2_
  329.0 0.8 reshape.265.refs_3_
  329.7 79.0 %closing.1 = (f32[2,64,1024]{2,1,0:T(8,128)}, f32[512,1024]{1,0:T(8,128)}, f32[8,128]{1,0:T(8,128)}, f32[8,128]{1,0:T(8,128)}, bf16[64,3072]{1,0:T(8,128)(2,1)}) custom-call(bf16[2,8,64,1024]{3,2,1,0:T(8,128)(2,1)} %bitcast.72, f32[2,64,1024]{2,1,0:T(8,128)} %get-tuple-element.58.refs_1_, s32[1,2048]{1,0:T(1,128)} %fusion.26.refs_2_, ...), custom_call_target="tpu_custom_call" | custom-call | tf_op jit(solution)/shard_map/closing/pallas_call | solution.py:104
  408.8 2.0 convert_element_type.97
  410.8 0.7 slice.119
  411.5 0.6 constant_dynamic-slice_fusion.2
  412.2 0.7 slice.123
  412.8 0.7 slice.124
  413.5 0.7 slice_reduce_fusion.2
  414.2 0.6 slice.122
  414.8 1.2 slice_bitcast_fusion.1
  416.1 1.1 bitcast_convert_fusion.1
  417.2 1.0 convert_element_type.99
  418.2 0.7 convert_element_type.98
  419.0 0.7 copy.56
  419.7 0.8 copy.57
  420.5 1.3 copy.58
  (90 shorter events, 1.9 us)
Async XLA Ops:
  0.6 25.8 %copy-start = (bf16[512,1024]{1,0:T(8,128)(2,1)S(1)}, bf16[512,1024]{1,0:T(8,128)(2,1)}, u32[]{:S(2)}) copy-start(bf16[512,1024]{1,0:T(8,128)(2,1)} %param.17) | copy-start | bytes 3145732
  0.7 3.1 copy-start.9
  2.2 2.9 copy-start.23
  2.2 3.0 copy-start.17
  2.2 3.0 copy-start.20
  2.2 2.9 copy-start.21
  2.2 3.0 copy-start.18
  30.4 43.2 %copy-start.19 = (s32[2,64]{1,0:T(2,128)S(1)}, s32[2,64]{1,0:T(2,128)}, u32[]{:S(2)}) copy-start(s32[2,64]{1,0:T(2,128)} %param.15) | copy-start | bytes 1540
  30.4 43.3 %copy-start.12 = (bf16[2,64,1024]{2,1,0:T(8,128)(2,1)S(1)}, bf16[2,64,1024]{2,1,0:T(8,128)(2,1)}, u32[]{:S(2)}) copy-start(bf16[2,64,1024]{2,1,0:T(8,128)(2,1)} %param.13) | copy-start | bytes 786436
  30.4 45.4 %copy-start.11 = (bf16[4,64,512]{2,1,0:T(8,128)(2,1)S(1)}, bf16[4,64,512]{2,1,0:T(8,128)(2,1)}, u32[]{:S(2)}) copy-start(bf16[4,64,512]{2,1,0:T(8,128)(2,1)} %get-tuple-element.44) | copy-start | bytes 786436
  73.4 18.5 %copy-start.22 = (bf16[4,4,64,384]{3,2,1,0:T(8,128)(2,1)S(1)}, bf16[4,4,64,384]{3,2,1,0:T(8,128)(2,1)}, u32[]{:S(2)}) copy-start(bf16[4,4,64,384]{3,2,1,0:T(8,128)(2,1)} %get-tuple-element.42) | copy-start | bytes 2359300
  91.9 3.6 copy-start.14
  91.9 45.2 %copy-start.3 = (bf16[2,64,1024]{2,1,0:T(8,128)(2,1)S(1)}, bf16[2,64,1024]{2,1,0:T(8,128)(2,1)}, u32[]{:S(2)}) copy-start(bf16[2,64,1024]{2,1,0:T(8,128)(2,1)} %get-tuple-element.47) | copy-start | bytes 786436
  141.8 126.4 %copy-start.4 = (bf16[2,64,1024]{2,1,0:T(8,128)(2,1)S(1)}, bf16[2,64,1024]{2,1,0:T(8,128)(2,1)}, u32[]{:S(2)}) copy-start(bf16[2,64,1024]{2,1,0:T(8,128)(2,1)} %get-tuple-element.46) | copy-start | bytes 786436
  268.1 2.9 copy-start.1
  318.9 4.0 copy-start.5
  318.9 4.6 %copy-start.15 = (f32[8,1024]{1,0:T(8,128)S(1)}, f32[8,1024]{1,0:T(8,128)}, u32[]{:S(2)}) copy-start(f32[8,1024]{1,0:T(8,128)} %get-tuple-element.59) | copy-start | bytes 98308
  318.9 4.8 %copy-start.16 = (f32[1,512]{1,0:T(1,128)S(1)}, f32[1,512]{1,0:T(1,128)}, u32[]{:S(2)}) copy-start(f32[1,512]{1,0:T(1,128)} %get-tuple-element.60) | copy-start | bytes 6148
  329.7 86.3 %copy-start.7 = (bf16[2,128,1024]{2,1,0:T(8,128)(2,1)S(1)}, bf16[2,128,1024]{2,1,0:T(8,128)(2,1)}, u32[]{:S(2)}) copy-start(bf16[2,128,1024]{2,1,0:T(8,128)(2,1)} %get-tuple-element.67) | copy-start | bytes 1572868
  408.7 8.5 %copy-start.6 = (bf16[64,4096]{1,0:T(8,128)(2,1)S(1)}, bf16[64,4096]{1,0:T(8,128)(2,1)}, u32[]{:S(2)}) copy-start(bf16[64,4096]{1,0:T(8,128)(2,1)} %get-tuple-element.66) | copy-start | bytes 1572868
  408.8 9.5 %copy-start.13 = (bf16[64,1024]{1,0:T(8,128)(2,1)S(1)}, bf16[64,1024]{1,0:T(8,128)(2,1)}, u32[]{:S(2)}) copy-start(bf16[64,1024]{1,0:T(8,128)(2,1)} %get-tuple-element.65) | copy-start | bytes 393220
  408.8 10.2 %copy-start.10 = (bf16[2,64,1024]{2,1,0:T(8,128)(2,1)S(1)}, bf16[2,64,1024]{2,1,0:T(8,128)(2,1)}, u32[]{:S(2)}) copy-start(bf16[2,64,1024]{2,1,0:T(8,128)(2,1)} %get-tuple-element.96) | copy-start | bytes 786436
  410.8 8.9 %copy-start.8 = (f32[2,64,1024]{2,1,0:T(8,128)S(1)}, f32[2,64,1024]{2,1,0:T(8,128)}, u32[]{:S(2)}) copy-start(f32[2,64,1024]{2,1,0:T(8,128)} %get-tuple-element.97) | copy-start | bytes 1572868
  417.2 3.3 copy-start.2

commit v4 on v0

--- a/solution.py
+++ b/solution.py
@@ -1,13 +1,1521 @@
+import functools
 import math
+from types import SimpleNamespace
 
 import jax
 import jax.numpy as jnp
 from jax import lax
+from jax.experimental import pallas as pl
+from jax.experimental.pallas import tpu as pltpu
 from jax.sharding import PartitionSpec as P
 
 HEADS = 16
-
-
+MESH = pl.DeviceIdType.MESH
+F32 = jnp.float32
+BF16 = jnp.bfloat16
+VSPEC = pl.BlockSpec(memory_space=pltpu.VMEM)
+
+
+def place():
+    h = lax.axis_index("head")
+    b = lax.axis_index("blk")
+    return h, b // 4, (b // 2) % 2, b % 2
+
+
+def blk(o, y, c):
+    return (o * 2 + y) * 2 + c
+
+
+def peer(dx, dz, dy, dc):
+    h, o, y, c = place()
+    flip = lambda v, d: 1 - v if d else v
+    return flip(h, dx), blk((o + dz) % 4 if dz else o, flip(y, dy), flip(c, dc))
+
+
+def remote(src, dst, sems, index, device):
+    return pltpu.make_async_remote_copy(
+        src_ref=src,
+        dst_ref=dst,
+        send_sem=sems.at[0, index],
+        recv_sem=sems.at[1, index],
+        device_id=device,
+        device_id_type=MESH,
+    )
+
+
+def landed(ref, sems, index):
+    remote(ref, ref, sems, index, peer(1, 0, 0, 0)).wait_recv()
+
+
+def sems(count):
+    return pltpu.SemaphoreType.DMA((2, count))
+
+
+NEAR_X, NEAR_Y, NEAR_C = (1, 0, 0, 0), (0, 0, 1, 0), (0, 0, 0, 1)
+COLUMN = ((0, 1, 0, 0), (0, 2, 0, 0), (0, 3, 0, 0))
+PLANE = tuple(
+    (dx, 0, dy, dc) for dx in range(2) for dy in range(2) for dc in range(2) if dx or dy or dc
+)
+
+
+class Part:
+    def __init__(self, run, ins, outs, scratch, peers):
+        self.run, self.ins, self.outs, self.scratch, self.peers = run, ins, outs, scratch, peers
+        self.turns = ()
+
+    def on(self, *turns):
+        self.turns = turns
+        return self
+
+
+def fused(name, cid, parts, limit=None):
+    peers = sorted({p for part in parts for p in part.peers})
+    ins = [x for part in parts for x in part.ins]
+    outs = [s for part in parts for s in part.outs]
+    scratch = [s for part in parts for s in part.scratch]
+
+    def kernel(*refs):
+        in_refs, out_refs = refs[: len(ins)], refs[len(ins) : len(ins) + len(outs)]
+        own = refs[len(ins) + len(outs) :]
+        gens = []
+        i = j = k = 0
+        for part in parts:
+            gens.append(
+                part.run(
+                    in_refs[i : i + len(part.ins)],
+                    out_refs[j : j + len(part.outs)],
+                    own[k : k + len(part.scratch)],
+                )
+            )
+            i, j, k = i + len(part.ins), j + len(part.outs), k + len(part.scratch)
+        barrier = pltpu.get_barrier_semaphore()
+        for p in peers:
+            pl.semaphore_signal(barrier, inc=1, device_id=peer(*p), device_id_type=MESH)
+        pl.semaphore_wait(barrier, len(peers))
+        for gen in gens:
+            next(gen)
+        for turn, _ in enumerate(gens[0]):
+            for part, gen in zip(parts, gens):
+                if turn in part.turns:
+                    next(gen)
+        for gen in gens[1:]:
+            for _ in gen:
+                pass
+
+    got = pl.pallas_call(
+        kernel,
+        name=name,
+        out_shape=[jax.ShapeDtypeStruct(s, d) for s, d in outs],
+        in_specs=[VSPEC] * len(ins),
+        out_specs=[VSPEC] * len(outs),
+        scratch_shapes=scratch,
+        compiler_params=pltpu.CompilerParams(
+            collective_id=cid, has_side_effects=True, vmem_limit_bytes=limit
+        ),
+    )(*ins)
+    result = []
+    for part in parts:
+        result.append(got[: len(part.outs)])
+        got = got[len(part.outs) :]
+    return result
+
+
+def exchange(x, peers, out_lead, source, target):
+    peers = list(peers)
+
+    def coords(p):
+        h, o, y, c = place()
+        flip = lambda v, d: 1 - v if d else v
+        return flip(h, p[0]), (o + p[1]) % 4 if p[1] else o, flip(y, p[2]), flip(c, p[3])
+
+    def run(ins, outs, own):
+        (x_ref,), (out_ref,), (sem,) = ins, outs, own
+        me = place()
+        copies = []
+        for k, p in enumerate(peers):
+            copy = remote(
+                source(x_ref, coords(p)), target(out_ref, me), sem, k, peer(*p)
+            )
+            copy.start()
+            copies.append(copy)
+        yield
+        target(out_ref, me)[...] = source(x_ref, me)[...]
+        for copy in copies:
+            copy.wait()
+
+    return Part(run, [x], [(out_lead, x.dtype)], [sems(len(peers))], peers)
+
+
+def blk_exchange(x):
+    return exchange(
+        x,
+        [(0, 0, 1, 0), (0, 0, 0, 1), (0, 0, 1, 1)],
+        x.shape,
+        lambda r, d: r.at[d[2] * 2 + d[3]],
+        lambda r, s: r.at[s[2] * 2 + s[3]],
+    )
+
+
+def small_gather(x):
+    peers = [
+        (0, dz, dy, dc) for dz in range(4) for dy in range(2) for dc in range(2) if dz or dy or dc
+    ]
+    return exchange(x, peers, (16,) + x.shape, lambda r, d: r, lambda r, s: r.at[blk(*s[1:])])
+
+
+def place_copy(src, dst, send_sem, recv_sem, device):
+    return pltpu.make_async_remote_copy(
+        src_ref=src,
+        dst_ref=dst,
+        send_sem=send_sem,
+        recv_sem=recv_sem,
+        device_id=device,
+        device_id_type=MESH,
+    )
+
+
+BLK = tuple(
+    (0, dz, dy, dc) for dz in range(4) for dy in range(2) for dc in range(2) if dz or dy or dc
+)
+
+
+def out_weights(w):
+    r, n = w.shape
+
+    def run(ins, outs, own):
+        (w_ref,), (out_ref,), (send, recv) = ins, outs, own
+        h, o, y, c = place()
+        has = o // 2 == h
+        serves = (o % 2 == y) & (y == c)
+
+        def each(act):
+            for k in range(4):
+                device = (h, blk((o + k) % 4, o % 2, y))
+                copy = place_copy(w_ref, out_ref.at[c], send.at[k], recv.at[c], device)
+
+                @pl.when(has if k else has & jnp.logical_not(serves))
+                def _():
+                    act(copy)
+
+        each(lambda copy: copy.start())
+        yield
+
+        @pl.when(has & serves)
+        def _():
+            out_ref[pl.ds(c, 1)] = w_ref[...][None]
+
+        each(lambda copy: copy.wait_send())
+        for core in range(2):
+            from_self = (o == 2 * h + y) & (y == c) & (c == core)
+            ref = out_ref.at[core]
+
+            @pl.when(jnp.logical_not(from_self))
+            def _():
+                place_copy(ref, ref, send.at[0], recv.at[core], (h, blk(o, y, c))).wait_recv()
+
+    scratch = [pltpu.SemaphoreType.DMA((4,)), pltpu.SemaphoreType.DMA((2,))]
+    return Part(run, [w], [((2, r, n), BF16)], scratch, BLK)
+
+
+def mirrored():
+    o = place()[1]
+    far = o // 2
+    seen = lambda v: v * (1 - 2 * far) + 3 * far
+    return seen(o), seen
+
+
+def gather_steps(src, dst, sem):
+    h, o, y, c = place()
+    dev_x, dev_y, dev_c = peer(*NEAR_X), peer(*NEAR_Y), peer(*NEAR_C)
+    mine = h * 4 + y * 2 + c
+    of_x = (1 - h) * 4 + y * 2 + c
+    of_y = h * 4 + (1 - y) * 2 + c
+    of_d = (1 - h) * 4 + (1 - y) * 2 + c
+    flip = 1 - 2 * c
+    sent = []
+
+    def go(ref, slot, half, index, device):
+        copy = remote(ref, dst(half, slot), sem, index, device)
+        copy.start()
+        sent.append(copy)
+
+    go(src(0), mine, 0, 0, dev_x)
+    go(src(1), mine, 1, 1, dev_y)
+    go(src(1), mine, 1, 2, dev_x)
+    go(src(0), mine, 0, 3, dev_y)
+    go(src(0), mine, 0, 4, dev_c)
+    go(src(1), mine, 1, 5, dev_c)
+    for half in range(2):
+        dst(half, mine)[...] = src(half)[...]
+
+    def relay(slot, half, index, device, onward, to_core):
+        landed(dst(half, slot), sem, index)
+        if onward is not None:
+            go(dst(half, slot), slot, half, onward, device)
+        go(dst(half, slot), slot, half, to_core, dev_c)
+
+    yield
+    relay(of_x, 0, 0, dev_y, 6, 8)
+    relay(of_y, 1, 1, dev_x, 7, 9)
+    yield
+    relay(of_x, 1, 2, None, None, 10)
+    relay(of_y, 0, 3, None, None, 11)
+    yield
+    relay(of_d, 0, 6, None, None, 12)
+    relay(of_d, 1, 7, None, None, 13)
+    yield
+    for slot, half, index in (
+        (mine, 0, 4),
+        (mine, 1, 5),
+        (of_x, 0, 8),
+        (of_y, 1, 9),
+        (of_x, 1, 10),
+        (of_y, 0, 11),
+        (of_d, 0, 12),
+        (of_d, 1, 13),
+    ):
+        landed(dst(half, slot + flip), sem, index)
+    for copy in sent:
+        copy.wait_send()
+
+
+def scatter_steps(src, total, near, part, from_x, from_y, diag, sem):
+    h, o, y, c = place()
+    dev_x, dev_y, dev_c = peer(*NEAR_X), peer(*NEAR_Y), peer(*NEAR_C)
+    mine = h * 4 + y * 2 + c
+    of_x = (1 - h) * 4 + y * 2 + c
+    of_y = h * 4 + (1 - y) * 2 + c
+    of_d = (1 - h) * 4 + (1 - y) * 2 + c
+    flip = 1 - 2 * c
+    order = (of_d, of_x, of_y, mine)
+    sent = []
+
+    def go(ref, to, index, device):
+        copy = remote(ref, to, sem, index, device)
+        copy.start()
+        sent.append(copy)
+
+    for k, half in ((0, 0), (0, 1), (1, 0), (2, 1), (1, 1), (2, 0), (3, 0), (3, 1)):
+        go(src(half, order[k] + flip), near.at[k, half], 2 * k + half, dev_c)
+
+    def add(k, half):
+        landed(near.at[k, half], sem, 2 * k + half)
+        return src(half, order[k])[...].astype(F32) + near[k, half].astype(F32)
+
+    yield
+    part[0, 0] = add(0, 0).astype(BF16)
+    go(part.at[0, 0], diag.at[0], 8, dev_x)
+    part[0, 1] = add(0, 1).astype(BF16)
+    go(part.at[0, 1], diag.at[1], 9, dev_y)
+    part[1, 0] = add(1, 0).astype(BF16)
+    go(part.at[1, 0], from_x.at[0], 10, dev_x)
+    part[2, 1] = add(2, 1).astype(BF16)
+    go(part.at[2, 1], from_y.at[1], 11, dev_y)
+    yield
+    kept_x = add(1, 1)
+    landed(diag.at[1], sem, 9)
+    part[1, 1] = (kept_x + diag[1].astype(F32)).astype(BF16)
+    go(part.at[1, 1], from_x.at[1], 12, dev_x)
+    kept_y = add(2, 0)
+    landed(diag.at[0], sem, 8)
+    part[2, 0] = (kept_y + diag[0].astype(F32)).astype(BF16)
+    go(part.at[2, 0], from_y.at[0], 13, dev_y)
+    yield
+    own = [add(3, half) for half in range(2)]
+    for half, ix, iy in ((0, 10, 13), (1, 12, 11)):
+        landed(from_x.at[half], sem, ix)
+        landed(from_y.at[half], sem, iy)
+        total(half)[...] = own[half] + from_x[half].astype(F32) + from_y[half].astype(F32)
+    for copy in sent:
+        copy.wait_send()
+
+
+def scatter_scratch(r, n):
+    block = (2, r // 2, n)
+    return [
+        pltpu.VMEM((4,) + block, BF16),
+        pltpu.VMEM((3,) + block, BF16),
+        pltpu.VMEM(block, BF16),
+        pltpu.VMEM(block, BF16),
+        pltpu.VMEM(block, BF16),
+        sems(14),
+    ]
+
+
+def norm_parts(r):
+    centred = r - jnp.mean(r, axis=-1, keepdims=True)
+    scale = lax.rsqrt(jnp.mean(centred * centred, axis=-1, keepdims=True) + 1e-12)
+    return centred * scale, scale
+
+
+def norm_back(xh, scale, dh):
+    return (
+        dh
+        - jnp.mean(dh, axis=-1, keepdims=True)
+        - xh * jnp.mean(dh * xh, axis=-1, keepdims=True)
+    ) * scale
+
+
+def dot_nt(a, b):
+    return lax.dot_general(a, b, (((1,), (1,)), ((), ())), preferred_element_type=F32)
+
+
+def dot_tn(a, b):
+    return lax.dot_general(a, b, (((0,), (0,)), ((), ())), preferred_element_type=F32)
+
+
+def blk_gather_steps(src, spot_of, zsem, ysem, csem):
+    h, o, y, c = place()
+    at, seen = mirrored()
+    dev_y, dev_c = peer(*NEAR_Y), peer(*NEAR_C)
+    end, inner, other = (h, blk(seen(0), y, c)), (h, blk(seen(1), y, c)), (h, blk(seen(2), y, c))
+    sent = []
+
+    def spot(z, yy=y, cc=c):
+        return spot_of(z, yy, cc)
+
+    def go(ref, z, yy, sem, index, device):
+        copy = remote(ref, spot(z, yy), sem, index, device)
+        copy.start()
+        sent.append(copy)
+
+    def line(ref, z, index, device):
+        return remote(ref, spot(z), zsem, index, device)
+
+    @pl.when(at == 0)
+    def _():
+        line(src, o, 0, inner).start()
+
+    @pl.when(at == 1)
+    def _():
+        line(src, o, 1, end).start()
+        line(src, o, 2, other).start()
+
+    go(src, o, y, ysem, 0, dev_y)
+    go(src, o, y, csem, 0, dev_c)
+    spot(o)[...] = src[...]
+
+    def onward(j, z):
+        go(spot(z), z, y, ysem, j, dev_y)
+        go(spot(z), z, y, csem, j, dev_c)
+
+    first = seen(1 - at)
+    order = (o, first, seen(2), seen(3))
+
+    def from_y(j):
+        landed(spot(order[j], 1 - y), ysem, j)
+        go(spot(order[j], 1 - y), order[j], 1 - y, csem, 4 + j, dev_c)
+
+    yield
+
+    @pl.when(at == 0)
+    def _():
+        landed(spot(seen(1)), zsem, 1)
+
+    @pl.when(at == 1)
+    def _():
+        landed(spot(seen(0)), zsem, 0)
+        line(spot(seen(0)), seen(0), 3, other).start()
+
+    onward(1, first)
+
+    @pl.when(at == 1)
+    def _():
+        landed(spot(seen(2)), zsem, 2)
+        line(spot(seen(2)), seen(2), 4, end).start()
+
+    yield
+    from_y(0)
+
+    @pl.when(at == 0)
+    def _():
+        landed(spot(seen(2)), zsem, 4)
+
+    onward(2, seen(2))
+
+    @pl.when(at == 1)
+    def _():
+        landed(spot(seen(3)), zsem, 3)
+        line(spot(seen(3)), seen(3), 5, end).start()
+
+    yield
+    from_y(1)
+
+    @pl.when(at == 0)
+    def _():
+        landed(spot(seen(3)), zsem, 5)
+
+    onward(3, seen(3))
+    yield
+    from_y(2)
+    yield
+    from_y(3)
+    yield
+    for j, z in enumerate(order):
+        landed(spot(z, y, 1 - c), csem, j)
+        landed(spot(z, 1 - y, 1 - c), csem, 4 + j)
+
+    @pl.when(at == 0)
+    def _():
+        line(src, o, 0, inner).wait_send()
+
+    @pl.when(at == 1)
+    def _():
+        line(src, o, 1, end).wait_send()
+        line(src, o, 2, other).wait_send()
+        line(spot(seen(0)), seen(0), 3, other).wait_send()
+        line(spot(seen(2)), seen(2), 4, end).wait_send()
+        line(spot(seen(3)), seen(3), 5, end).wait_send()
+
+    for copy in sent:
+        copy.wait_send()
+
+
+ALL = tuple(
+    (dx, dz, dy, dc)
+    for dx in range(2)
+    for dz in range(4)
+    for dy in range(2)
+    for dc in range(2)
+    if dx or dz or dy or dc
+)
+
+
+def line_sum_steps(term_of, out, terms, ends, mids, last, sem):
+    h, o, y, c = place()
+    at, seen = mirrored()
+    end, inner, other = (h, blk(seen(0), y, c)), (h, blk(seen(1), y, c)), (h, blk(seen(2), y, c))
+    order = [seen(3), seen(2), seen(1 - at)]
+    plus = lambda a, b: a[...].astype(F32) + b[...].astype(F32)
+
+    @pl.when(at == 0)
+    def _():
+        for j in range(3):
+            remote(term_of(order[j]), ends.at[j], sem, j, inner).start()
+
+    for j in range(2):
+        yield
+
+        @pl.when(at == 1)
+        def _():
+            landed(ends.at[j], sem, j)
+            terms[j] = plus(term_of(order[j]), ends.at[j]).astype(BF16)
+            remote(terms.at[j], mids.at[j], sem, 3 + j, other).start()
+
+    yield
+
+    @pl.when(at == 1)
+    def _():
+        landed(mids.at[0], sem, 3)
+        terms[2] = plus(term_of(order[2]), mids.at[0]).astype(BF16)
+        remote(terms.at[2], last, sem, 5, end).start()
+
+    yield
+
+    @pl.when(at == 1)
+    def _():
+        landed(ends.at[2], sem, 2)
+        landed(mids.at[1], sem, 4)
+        out[...] = (plus(term_of(o), ends.at[2]) + mids[1].astype(F32)).astype(BF16)
+        for j in range(2):
+            remote(terms.at[j], mids.at[j], sem, 3 + j, other).wait_send()
+        remote(terms.at[2], last, sem, 5, end).wait_send()
+
+    @pl.when(at == 0)
+    def _():
+        landed(last, sem, 5)
+        out[...] = plus(term_of(o), last).astype(BF16)
+        for j in range(3):
+            remote(term_of(order[j]), ends.at[j], sem, j, inner).wait_send()
+
+
+def line_sum_scratch(block):
+    return [
+        pltpu.VMEM((3,) + block, BF16),
+        pltpu.VMEM((3,) + block, BF16),
+        pltpu.VMEM((2,) + block, BF16),
+        pltpu.VMEM(block, BF16),
+        sems(6),
+    ]
+
+
+def spread_steps(rows_of, out, spots, sem):
+    h, o, y, c = place()
+    t = h * 4 + y * 2 + c
+    columns = [
+        out.at[:, pl.ds(pl.multiple_of(lane * 128, 128), 128)] for lane in spots(t)
+    ]
+    pieces = len(columns)
+    copies = []
+    for k, p in enumerate(PLANE):
+        to = (1 - y if p[2] else y) * 2 + (1 - c if p[3] else c)
+        for i in range(pieces):
+            src = rows_of(to).at[:, pl.ds(i * 128, 128)]
+            copy = remote(src, columns[i], sem, k * pieces + i, peer(*p))
+            copy.start()
+            copies.append(copy)
+    for i in range(pieces):
+        columns[i][...] = rows_of(y * 2 + c)[:, i * 128 : (i + 1) * 128]
+    yield
+    for copy in copies:
+        copy.wait()
+
+
+def second_half(x, consts):
+    names = list(vars(x))
+    seqs, r, d = x.embedded.shape
+    planes, four, e, fh = x.up_one.shape
+    f = 2 * fh
+    fcols = x.down_cut.shape[0]
+    half, half_d = r // 2, d // 2
+    rows, q_rows = 8 * r, 4 * r
+    three, he, length = x.held.shape
+    n = length // 4
+    slots, chunks, lag, chunk_lag, scale = consts
+    own_rows, w, blks = seqs * r, d // chunks, 16
+    key_rows = 256
+    width_qkv = 3 * 2 * he
+
+    need = []
+
+    def scratch(shape, dtype):
+        need.append(pltpu.VMEM(shape, dtype))
+        return len(need) - 1
+
+    def many(specs):
+        start = len(need)
+        need.extend(specs)
+        return list(range(start, len(need)))
+
+    plane = (seqs, 8, r, d)
+    shapes = dict(
+        partial=(plane, BF16),
+        up_two=(x.up_one.shape, BF16),
+        down_two=(x.down_one.shape, BF16),
+        first_g=(plane, BF16),
+        grad_g=(plane, BF16),
+        branch_g=(plane, BF16),
+        act=((seqs * rows, f), BF16),
+        slope=((seqs * rows, f), F32),
+        inner_grad=((seqs * rows, f), BF16),
+        first=((seqs, r, d), F32),
+        xh_one=((seqs, r, d), F32),
+        scale_one=((seqs, r, 1), F32),
+        grad_two=((seqs, r, d), F32),
+        low=((seqs, r, d), BF16),
+        total=((seqs, r, d), F32),
+        resid=((seqs, r, d), F32),
+        down_part=((planes, fcols, d), BF16),
+        up_part=((planes, 4 * e, f), BF16),
+        up_total=((4 * e, f), BF16),
+        out_part=((2, he, d), BF16),
+        out_held=((4, he, d), BF16),
+        out_acc=((he, d), F32),
+        sums=((16, d), F32),
+        up_sums=((1, f), F32),
+        up_spots=((32, 128), F32),
+        go=((2, he, 2 * n), BF16),
+        gs=((he, length), BF16),
+        qs=((he, length), BF16),
+        q_rows=((length, he), BF16),
+        g_rows=((length, he), BF16),
+        dq=((he, length), F32),
+        delta=((1, length), F32),
+        pair_low=((three, he, length), BF16),
+        dqkv=((three, 2, he, 2 * n), BF16),
+        qkv_part=((planes, 4 * e, width_qkv), BF16),
+        qkv_total=((4 * e, width_qkv), BF16),
+        own=((chunks, own_rows, w), BF16),
+        gathered=((chunks, blks, own_rows, w), BF16),
+        pick=((slots, blks * own_rows), BF16),
+        pos_low=((chunks, slots, w), BF16),
+        pos_held=((chunks, slots, w), BF16),
+        pack=((blks, 24, 128), F32),
+        packs=((31, 24, 128), F32),
+    )
+    ids = {name: scratch(*spec) for name, spec in shapes.items()}
+    counts = dict(
+        up_sem=3,
+        down_sem=3,
+        ksem=3,
+        qsem=3,
+        down_pair=1,
+        up_spread=28,
+        qkv_spread=21,
+        out_pair=1,
+        pair_sem=chunks,
+        pack_sem=31,
+    )
+    sem_ids = {k: many([sems(v)])[0] for k, v in counts.items()}
+    for k, v in dict(go_send=4, go_recv=4, out_send=2, out_recv=4).items():
+        sem_ids[k] = many([pltpu.SemaphoreType.DMA((v,))])[0]
+    stream_ids = [
+        ([many(scatter_scratch(r, d)) for _ in range(3)], [many([sems(14)])[0] for _ in range(3)])
+        for _ in range(seqs)
+    ]
+    chunk_ids = [
+        (many(scatter_scratch(2 * r, w)), many([sems(6), sems(4), sems(8)])) for _ in range(chunks)
+    ]
+    down_line = many(line_sum_scratch((fcols, d)))
+    up_line = many(line_sum_scratch((4 * e, f)))
+    qkv_line = many(line_sum_scratch((4 * e, width_qkv)))
+
+    def run(ins, outs, own):
+        src = SimpleNamespace(**dict(zip(names, ins)))
+        out_ref, grad_ref, pos_ref, got_down, got_up, got_qkv, got_out, totals = outs
+        m = SimpleNamespace(**{k: own[v] for k, v in ids.items()})
+        sem = SimpleNamespace(**{k: own[v] for k, v in sem_ids.items()})
+        pick_refs = lambda some: [own[i] for i in some]
+        h, o, y, c = place()
+        g = y * 2 + c
+        t = h * 4 + g
+        tail = []
+
+        up_more = src.up_cut.at[:, :, pl.ds(fh, fh)]
+        down_more = src.down_cut.at[:, pl.ds(half_d, half_d)]
+        weights = []
+        for k, p in enumerate(COLUMN):
+            for ref, dst, s in (
+                (up_more, m.up_two, sem.up_sem),
+                (down_more, m.down_two, sem.down_sem),
+            ):
+                copy = remote(ref, dst.at[o], s, k, peer(*p))
+                copy.start()
+                weights.append(copy)
+        m.up_two[pl.ds(o, 1)] = up_more[...][None]
+        m.down_two[pl.ds(o, 1)] = down_more[...][None]
+        for ref in (m.sums, m.up_sums, m.up_spots, m.dq):
+            ref[...] = jnp.zeros_like(ref)
+        yield
+
+        ups = [lambda k=k: src.up_one[...].reshape(d, fh) if k == 0 else m.up_two[...].reshape(d, fh) for k in range(2)]
+        downs = [lambda k=k: src.down_one[...].reshape(f, half_d) if k == 0 else m.down_two[...].reshape(f, half_d) for k in range(2)]
+        vec = lambda k: src.vectors[k + 2 : k + 3]
+        partial, low, total = m.partial, m.low, m.total
+
+        def piece(ref, s):
+            return lambda i, slot: ref.at[s, slot, pl.ds(i * half, half)]
+
+        def plain(ref, s):
+            return lambda i: ref.at[s, pl.ds(i * half, half)]
+
+        def quarter(ref, s, q):
+            return ref[s, 4 * q : 4 * q + 4].reshape(q_rows, d)
+
+        def note(k, value):
+            m.sums[k : k + 1] += jnp.sum(value, axis=0, keepdims=True)
+
+        def step(*some):
+            for gen in some:
+                next(gen, None)
+
+        def down_sums():
+            yield from line_sum_steps(
+                lambda z: m.down_part.at[z], got_down.at[h], *pick_refs(down_line)
+            )
+            copy = remote(got_down.at[h], got_down.at[h], sem.down_pair, 0, peer(*NEAR_X))
+            copy.start()
+            yield
+            copy.wait_send()
+            landed(got_down.at[1 - h], sem.down_pair, 0)
+
+        def up_sums():
+            yield from line_sum_steps(lambda z: m.up_part.at[z], m.up_total, *pick_refs(up_line))
+            yield from spread_steps(
+                lambda k: m.up_total.at[pl.ds(k * e, e)],
+                got_up,
+                lambda k: [(i * 4 + k % 4) * 2 + k // 4 for i in range(4)],
+                sem.up_spread,
+            )
+
+        def qkv_sums():
+            yield from line_sum_steps(
+                lambda z: m.qkv_part.at[z], m.qkv_total, *pick_refs(qkv_line)
+            )
+            yield from spread_steps(
+                lambda k: m.qkv_total.at[pl.ds(k * e, e)],
+                got_qkv,
+                lambda k: [i * 8 + k for i in range(3)],
+                sem.qkv_spread,
+            )
+
+        def out_sums():
+            has = o // 2 == h
+            held, acc, send, recv = m.out_held, m.out_acc, sem.out_send, sem.out_recv
+
+            def each(act):
+                for j in range(2):
+                    device = (h, blk(2 * h + y, c, j))
+                    copy = place_copy(m.out_part.at[j], held.at[o], send.at[j], recv.at[o], device)
+
+                    @pl.when(jnp.logical_not((o == 2 * h + y) & (y == c) & (c == j)))
+                    def _():
+                        act(copy)
+
+            each(lambda copy: copy.start())
+            yield
+            acc[...] = jnp.zeros_like(acc)
+            for z in range(4):
+                mine = (z == o) & (o % 2 == y) & (y == c)
+
+                @pl.when(has & mine)
+                def _():
+                    acc[...] += m.out_part[c].astype(F32)
+
+                @pl.when(has & jnp.logical_not(mine))
+                def _():
+                    ref = held.at[z]
+                    place_copy(ref, ref, send.at[0], recv.at[z], (h, blk(o, y, c))).wait_recv()
+                    acc[...] += held[z].astype(F32)
+
+            pair = remote(got_out, got_out, sem.out_pair, 0, peer(*NEAR_X))
+
+            @pl.when(has)
+            def _():
+                got_out[...] = acc[...].astype(BF16)
+                pair.start()
+
+            yield
+            each(lambda copy: copy.wait_send())
+
+            @pl.when(has)
+            def _():
+                pair.wait_send()
+
+            @pl.when(jnp.logical_not(has))
+            def _():
+                landed(got_out, sem.out_pair, 0)
+
+        def go_copy(s, j):
+            z = 2 * s + j
+            return place_copy(
+                m.go.at[j, :, pl.ds(s * n, n)],
+                m.gs.at[:, pl.ds(pl.multiple_of(o * n, n), n)],
+                sem.go_send.at[z],
+                sem.go_recv.at[o],
+                (h, z * 4 + g),
+            )
+
+        def stream(s):
+            scatters = [pick_refs(i) for i in stream_ids[s][0]]
+            gathers = pick_refs(stream_ids[s][1])
+            at = lambda q: pl.ds(s * rows + q * q_rows, q_rows)
+            branch = dot_tn(
+                src.attended[:, :, s * n : (s + 1) * n].reshape(2 * he, n), src.out_own[...]
+            )
+            partial[s] = branch.astype(BF16).reshape(8, r, d)
+            yield from scatter_steps(piece(partial, s), plain(total, s), *scatters[0])
+            xh, scale_r = norm_parts(src.embedded[s] + (total[s] + vec(0)))
+            m.xh_one[s] = xh
+            m.scale_one[s] = scale_r
+            value = xh * vec(4) + vec(1)
+            m.first[s] = value
+            low[s] = value.astype(BF16)
+            yield from gather_steps(plain(low, s), piece(m.first_g, s), gathers[0])
+            if s == 0:
+                for copy in weights:
+                    copy.wait()
+            for q in range(2):
+                rows_in = quarter(m.first_g, s, q)
+                for k in range(2):
+                    cols = slice(k * fh, (k + 1) * fh)
+                    inner = jnp.dot(rows_in, ups[k](), preferred_element_type=F32)
+                    inner = inner + src.up_bias[:, cols]
+                    phi = 0.5 + 0.5 * lax.erf(inner * (0.5**0.5))
+                    m.act[at(q), cols] = (inner * phi).astype(BF16)
+                    bell = jnp.exp(inner * inner * -0.5) * (1.0 / math.sqrt(2.0 * math.pi))
+                    m.slope[at(q), cols] = phi + inner * bell
+                    yield
+                for k in range(2):
+                    part = jnp.dot(m.act[at(q)], downs[k](), preferred_element_type=F32)
+                    partial[s, 4 * q : 4 * q + 4, :, k * half_d : (k + 1) * half_d] = part.astype(
+                        BF16
+                    ).reshape(4, r, half_d)
+                yield
+            yield from scatter_steps(piece(partial, s), plain(total, s), *scatters[1])
+            xh, scale_r = norm_parts(m.first[s] + (total[s] + vec(2)))
+            out_ref[s] = (xh * vec(5) + vec(3)).astype(BF16)
+            cot = src.cotangent[s].astype(F32)
+            note(5, cot * xh)
+            note(3, cot)
+            grad = norm_back(xh, scale_r, cot * vec(5))
+            m.grad_two[s] = grad
+            low[s] = grad.astype(BF16)
+            note(2, low[s].astype(F32))
+            yield from gather_steps(plain(low, s), piece(m.grad_g, s), gathers[1])
+            for q in range(2):
+                rows_in = quarter(m.grad_g, s, q)
+                back = dot_nt(rows_in[:, :half_d], downs[0]()) + dot_nt(
+                    rows_in[:, half_d:], downs[1]()
+                )
+                back = (back * m.slope[at(q)]).astype(BF16)
+                m.inner_grad[at(q)] = back
+                m.up_sums[...] += jnp.sum(back.astype(F32), axis=0, keepdims=True)
+                yield
+                part = dot_nt(back[:, :fh], ups[0]()) + dot_nt(back[:, fh:], ups[1]())
+                partial[s, 4 * q : 4 * q + 4] = part.astype(BF16).reshape(4, r, d)
+                yield
+            last = scatter_steps(piece(partial, s), plain(total, s), *scatters[2])
+            next(last)
+            if s == seqs - 1:
+                all_grads = m.grad_g[...].reshape(seqs * rows, d)
+                for z in range(planes):
+                    cols = slice(z * fcols, (z + 1) * fcols)
+                    m.down_part[z] = dot_tn(m.act[:, cols], all_grads).astype(BF16)
+                step(down)
+                yield
+                for z in range(planes):
+                    cols = slice(z * 4 * e, (z + 1) * 4 * e)
+                    all_first = m.first_g[:, :, :, cols].reshape(seqs * rows, 4 * e)
+                    m.up_part[z] = dot_tn(all_first, m.inner_grad[...]).astype(BF16)
+                yield
+            yield from last
+            grad = m.grad_two[s] + total[s]
+            note(4, grad * m.xh_one[s])
+            note(1, grad)
+            grad = norm_back(m.xh_one[s], m.scale_one[s], grad * vec(4))
+            m.resid[s] = grad
+            low[s] = grad.astype(BF16)
+            note(0, low[s].astype(F32))
+            for k, _ in enumerate(gather_steps(plain(low, s), piece(m.branch_g, s), gathers[2])):
+                yield
+                if s == seqs - 1 and k in EARLY:
+                    step(down)
+            go = dot_nt(src.out_own[...], m.branch_g[s].reshape(rows, d))
+            m.go[:, :, s * n : (s + 1) * n] = go.astype(BF16).reshape(2, he, n)
+            for j in range(2):
+
+                @pl.when(o != 2 * s + j)
+                def _():
+                    go_copy(s, j).start()
+
+                @pl.when(o == 2 * s + j)
+                def _():
+                    m.gs[:, pl.ds(pl.multiple_of(o * n, n), n)] = m.go[
+                        j, :, s * n : (s + 1) * n
+                    ]
+
+            yield
+
+        down, up, out, qkv = down_sums(), up_sums(), out_sums(), qkv_sums()
+        gens = [stream(s) for s in range(seqs)]
+        for _ in range(lag):
+            next(gens[0])
+        while gens:
+            for gen in list(gens):
+                try:
+                    next(gen)
+                except StopIteration:
+                    gens.remove(gen)
+
+        step(up)
+        grad_out = jnp.dot(
+            src.attended[...].reshape(2 * he, 2 * n),
+            m.branch_g[...].reshape(seqs * rows, d),
+            preferred_element_type=F32,
+        )
+        m.out_part[...] = grad_out.astype(BF16).reshape(2, he, d)
+        held = src.held
+        gs, qs, q_t, g_t, dq, delta, pair_low = (
+            m.gs, m.qs, m.q_rows, m.g_rows, m.dq, m.delta, m.pair_low
+        )
+        q32 = held[0].astype(F32) * scale
+        qs[...] = q32.astype(BF16)
+        q_t[...] = q32.T.astype(BF16)
+        row = lax.broadcasted_iota(jnp.int32, (slots, 1), 0)
+        m.pick[...] = (src.ids[...] == row).astype(F32).astype(BF16)
+        for z in range(4):
+
+            @pl.when(z != o)
+            def _():
+                ref = gs.at[:, pl.ds(z * n, n)]
+                place_copy(
+                    ref, ref, sem.go_send.at[0], sem.go_recv.at[z], peer(*NEAR_X)
+                ).wait_recv()
+
+        g32 = gs[...].astype(F32)
+        g_t[...] = g32.T.astype(BF16)
+        delta[...] = jnp.sum(g32 * src.pair_out[...], axis=0, keepdims=True)
+        mine = pl.ds(pl.multiple_of((o // 2) * n, n), n)
+        dqkv = m.dqkv
+
+        def back(part, which, i, z):
+            return remote(
+                pair_low.at[part, :, pl.ds(pl.multiple_of(z * n, n), n)],
+                dqkv.at[part, o % 2, :, mine],
+                which,
+                i,
+                (h, z * 4 + g),
+            )
+
+        late = pl.ds(1, 2)
+        for i in range(4):
+            z = (o + 1 + i) % 4
+
+            @pl.loop(0, n // key_rows)
+            def _(step):
+                at = pl.ds(pl.multiple_of(z * n + step * key_rows, key_rows), key_rows)
+                k_cols = held[1, :, at]
+                k_rows = k_cols.astype(F32).T.astype(BF16)
+                v_rows = held[2, :, at].astype(F32).T.astype(BF16)
+                s = jnp.dot(k_rows, qs[...], preferred_element_type=F32)
+                p = jnp.exp(s - src.lse[...])
+                dv = jnp.dot(p.astype(BF16), g_t[...], preferred_element_type=F32)
+                dp = jnp.dot(v_rows, gs[...], preferred_element_type=F32)
+                ds = (p * (dp - delta[...])).astype(BF16)
+                dk = jnp.dot(ds, q_t[...], preferred_element_type=F32)
+                dq[...] += jnp.dot(k_cols, ds, preferred_element_type=F32)
+                pair_low[1, :, at] = dk.T.astype(BF16)
+                pair_low[2, :, at] = dv.T.astype(BF16)
+
+            if i < 3:
+                back(late, sem.ksem, i, z).start()
+            if i == 0:
+                step(*[down] * (3 - len(EARLY)))
+            if i == 2:
+                step(up)
+        pair_low[0] = (dq[...] * scale).astype(BF16)
+        for i in range(3):
+            back(pl.ds(0, 1), sem.qsem, i, (o + 1 + i) % 4).start()
+        dqkv[:, o % 2, :, mine] = pair_low[:, :, pl.ds(pl.multiple_of(o * n, n), n)]
+        step(down, up)
+        for i in range(3):
+            z = (o + 3 - i) % 4
+            there = pl.ds(pl.multiple_of((z // 2) * n, n), n)
+            landed(dqkv.at[late, z % 2, :, there], sem.ksem, i)
+            landed(dqkv.at[pl.ds(0, 1), z % 2, :, there], sem.qsem, i)
+
+        all_dqkv = lambda: dqkv[...].reshape(width_qkv, 2 * n)
+
+        def back_chunk(q):
+            part = lax.dot_general(
+                all_dqkv(),
+                src.qkv_own[q * w : (q + 1) * w],
+                (((0,), (1,)), ((), ())),
+                preferred_element_type=F32,
+            )
+            partial[:, :, :, q * w : (q + 1) * w] = part.astype(BF16).reshape(seqs, 8, r, w)
+
+        def chunk(q):
+            cols = pl.ds(q * w, w)
+            scatter, (zsem, ysem, csem) = pick_refs(chunk_ids[q][0]), pick_refs(chunk_ids[q][1])
+            back_chunk(q)
+            yield from scatter_steps(
+                lambda i, slot: partial.at[i, slot, :, cols],
+                lambda i: grad_ref.at[i, :, cols],
+                *scatter,
+            )
+            grad = grad_ref[:, :, cols] + m.resid[:, :, cols]
+            grad_ref[:, :, cols] = grad
+            grad = grad.reshape(own_rows, w)
+            m.own[q] = grad.astype(BF16)
+            second = src.second[...]
+            m.sums[6:7, cols] = jnp.sum(grad * (1.0 - second), axis=0, keepdims=True)
+            m.sums[7:8, cols] = jnp.sum(grad * second, axis=0, keepdims=True)
+            yield from blk_gather_steps(
+                m.own.at[q],
+                lambda z, yy, cc: m.gathered.at[q, blk(z, yy, cc)],
+                zsem,
+                ysem,
+                csem,
+            )
+            found = jnp.dot(
+                m.pick[...],
+                m.gathered[q].reshape(blks * own_rows, w),
+                preferred_element_type=F32,
+            )
+            pos_ref[:, cols] = found
+            m.pos_low[q] = found.astype(BF16)
+            copy = remote(
+                m.pos_low.at[q], m.pos_held.at[q], sem.pair_sem, q, peer(*NEAR_X)
+            )
+            copy.start()
+            pairs.append(copy)
+            yield
+
+        pairs = []
+        active, waiting = [], [chunk(q) for q in range(chunks)]
+        turn = 0
+        while active or waiting:
+            if waiting and turn % chunk_lag == 0:
+                active.append(waiting.pop(0))
+            for gen in list(active):
+                try:
+                    next(gen)
+                except StopIteration:
+                    active.remove(gen)
+            if turn == 0:
+                low_all = src.plane_low[...].reshape(seqs * rows, d)
+                for z in range(planes):
+                    cols = slice(z * 4 * e, (z + 1) * 4 * e)
+                    part = lax.dot_general(
+                        low_all[:, cols],
+                        all_dqkv(),
+                        (((0,), (1,)), ((), ())),
+                        preferred_element_type=F32,
+                    )
+                    m.qkv_part[z] = part.astype(BF16)
+                step(qkv)
+                ones = jnp.ones((8, 2 * n), BF16)
+                heads = dot_nt(ones, all_dqkv())
+                own_lanes = pl.ds(pl.multiple_of(t * 128, 128), 128)
+                m.sums[8:9, own_lanes] = heads[0:1, 0:128]
+                m.sums[9:10, own_lanes] = heads[0:1, 256:384]
+                for i in range(4):
+                    m.up_spots[pl.ds((i * 4 + g) * 2 + h, 1)] = m.up_sums[
+                        :, i * 128 : (i + 1) * 128
+                    ]
+            for when, gen in zip(TURNS, (up, qkv, out)):
+                if turn in when:
+                    step(gen)
+            turn += 1
+        for b in range(blks):
+            m.pack[b, 0:16] = m.sums[:, b // 2 * 128 : (b // 2 + 1) * 128]
+            m.pack[b, 16:18] = m.up_spots[2 * b : 2 * b + 2]
+            m.pack[b, 18:24] = jnp.zeros((6, 128), F32)
+        copies = []
+        for k, p in enumerate(ALL):
+            to = peer(*p)
+            copy = remote(m.pack.at[to[1]], m.packs.at[k], sem.pack_sem, k, to)
+            copy.start()
+            copies.append(copy)
+        for gen in (down, up, out, qkv):
+            for _ in gen:
+                pass
+        for q, copy in enumerate(pairs):
+            copy.wait()
+            cols = pl.ds(q * w, w)
+            pos_ref[:, cols] = pos_ref[:, cols] + m.pos_held[q].astype(F32)
+        for copy in copies:
+            copy.wait()
+        totals[...] = m.pack[blk(o, y, c)] + jnp.sum(m.packs[...], axis=0)
+        for i in range(3):
+            back(late, sem.ksem, i, (o + 1 + i) % 4).wait_send()
+            back(pl.ds(0, 1), sem.qsem, i, (o + 1 + i) % 4).wait_send()
+        for s in range(seqs):
+            for j in range(2):
+
+                @pl.when(o != 2 * s + j)
+                def _():
+                    go_copy(s, j).wait_send()
+
+    return Part(
+        run,
+        list(vars(x).values()),
+        [
+            ((seqs, r, d), BF16),
+            ((seqs, r, d), F32),
+            ((slots, d), F32),
+            ((2, fcols, d), BF16),
+            ((e, 8 * f), BF16),
+            ((e, 3 * d), BF16),
+            ((he, d), BF16),
+            ((24, 128), F32),
+        ],
+        need,
+        ALL,
+    )
+
+
+def rows_steps(own_of, near, part, from_y, term, ends, mids, last, csem, ysem, zsem, out):
+    h, o, y, c = place()
+    at, seen = mirrored()
+    dev_y = peer(*NEAR_Y)
+    order = [seen(3), seen(2), seen(1 - at), o]
+    end, inner, other = (h, blk(seen(0), y, c)), (h, blk(seen(1), y, c)), (h, blk(seen(2), y, c))
+    sent = []
+    for j, z in enumerate(order):
+        landed(near.at[0, j], csem, j)
+        part[j] = own_of(z, 1 - y)[...] + near[0, j]
+        copy = remote(part.at[j], from_y.at[j], ysem, j, dev_y)
+        copy.start()
+        sent.append(copy)
+    for j, z in enumerate(order):
+        yield
+        landed(near.at[1, j], csem, 4 + j)
+        landed(from_y.at[j], ysem, j)
+        term[j] = own_of(z, y)[...] + near[1, j] + from_y[j]
+        if j < 3:
+
+            @pl.when(at == 0)
+            def _():
+                remote(term.at[j], ends.at[j], zsem, j, inner).start()
+
+        if j < 2:
+
+            @pl.when(at == 1)
+            def _():
+                landed(ends.at[j], zsem, j)
+                term[j] += ends[j]
+                remote(term.at[j], mids.at[j], zsem, 3 + j, other).start()
+
+    yield
+
+    @pl.when(at == 1)
+    def _():
+        landed(mids.at[0], zsem, 3)
+        term[2] += mids[0]
+        remote(term.at[2], last, zsem, 5, end).start()
+
+    yield
+
+    @pl.when(at == 1)
+    def _():
+        landed(ends.at[2], zsem, 2)
+        landed(mids.at[1], zsem, 4)
+        out[...] = (term[3] + ends[2] + mids[1]).astype(F32)
+        for j in range(2):
+            remote(term.at[j], mids.at[j], zsem, 3 + j, other).wait_send()
+        remote(term.at[2], last, zsem, 5, end).wait_send()
+
+    @pl.when(at == 0)
+    def _():
+        landed(last, zsem, 5)
+        out[...] = (term[3] + last[...]).astype(F32)
+        for j in range(3):
+            remote(term.at[j], ends.at[j], zsem, j, inner).wait_send()
+
+    for copy in sent:
+        copy.wait_send()
+
+
+def first_half(x, scale, lag):
+    names = list(vars(x))
+    seqs, r, d = x.hidden.shape
+    slots = x.table.shape[0]
+    four, e, wq = x.qkv_cut.shape
+    f = x.up_cut.shape[2]
+    fcols = x.down_cut.shape[0]
+    he = wq // 6
+    n = 8 * r
+    length = 4 * n
+    half, fh, half_d = r // 2, f // 2, d // 2
+    blks = 16
+    cols = 256
+    small = small_gather(x.packed)
+    outw = out_weights(x.out_weight)
+    trade_qkv, trade_up = blk_exchange(x.qkv_cut), blk_exchange(x.up_cut)
+    need = []
+
+    def many(specs):
+        start = len(need)
+        need.extend(specs)
+        return list(range(start, len(need)))
+
+    block = (r, d)
+    shapes = dict(
+        everyone=((blks,) + x.packed.shape, F32),
+        found=((4, 2, 2, seqs, r, d), BF16),
+        rows=((seqs, r, d), F32),
+        low=((seqs, r, d), BF16),
+        qkv_in=(x.qkv_cut.shape, BF16),
+        projected=((3, 2, he, 2 * n), BF16),
+        keys=((length, he), BF16),
+        pair_low=((he, length), BF16),
+    )
+    ids = {k: many([pltpu.VMEM(*v)])[0] for k, v in shapes.items()}
+    counts = dict(qkv_sem=3, up_sem=3, down_sem=3, back_sem=3)
+    sem_ids = {k: many([sems(v)])[0] for k, v in counts.items()}
+    for k in ("send", "recv"):
+        sem_ids[k] = many([pltpu.SemaphoreType.DMA((4,))])[0]
+    small_ids, outw_ids = many(small.scratch), many(outw.scratch)
+    trade_ids = many(trade_qkv.scratch), many(trade_up.scratch)
+    row_ids = [
+        many(
+            [
+                pltpu.VMEM((2, 4) + block, BF16),
+                pltpu.VMEM((4,) + block, BF16),
+                pltpu.VMEM((4,) + block, BF16),
+                pltpu.VMEM((4,) + block, BF16),
+                pltpu.VMEM((3,) + block, BF16),
+                pltpu.VMEM((2,) + block, BF16),
+                pltpu.VMEM(block, BF16),
+                sems(8),
+                sems(4),
+                sems(6),
+            ]
+        )
+        for _ in range(seqs)
+    ]
+    gather_ids = [many([sems(14)])[0] for _ in range(seqs)]
+
+    def run(ins, outs, own):
+        src = SimpleNamespace(**dict(zip(names, ins)))
+        attended, held, o_ref, lse_ref, emb_ref, plane_ref, qkv_ref = outs[:7]
+        outw_ref, up_one, up_in, down_one, vec_ref, bias_ref, ids_ref = outs[7:]
+        m = SimpleNamespace(**{k: own[v] for k, v in ids.items()})
+        sem = SimpleNamespace(**{k: own[v] for k, v in sem_ids.items()})
+        pick_refs = lambda some: [own[i] for i in some]
+        h, o, y, c = place()
+        g = y * 2 + c
+        t = h * 4 + g
+        gather_small = small.run((src.packed,), (m.everyone,), pick_refs(small_ids))
+        trades = [
+            trade_qkv.run((src.qkv_cut,), (m.qkv_in,), pick_refs(trade_ids[0])),
+            trade_up.run((src.up_cut,), (up_in,), pick_refs(trade_ids[1])),
+        ]
+        weights = outw.run((src.out_weight,), (outw_ref,), pick_refs(outw_ids))
+        next(gather_small)
+        next(trades[0])
+        yield
+        next(trades[1])
+        bulk = []
+
+        def line(ref, dst, s):
+            for k, p in enumerate(COLUMN):
+                copy = remote(ref, dst.at[o], s, k, peer(*p))
+                copy.start()
+                bulk.append(copy)
+            dst[pl.ds(o, 1)] = ref[...][None]
+
+        for _ in gather_small:
+            pass
+
+        at, seen = mirrored()
+        order = [seen(3), seen(2), seen(1 - at), o]
+        b = blk(o, y, c)
+        row = lax.broadcasted_iota(jnp.int32, (slots, 1), 0).astype(F32)
+        base = (b * slots).astype(F32)
+        streams = [pick_refs(i) for i in row_ids]
+        core = []
+        for i, yy in enumerate((1 - y, y)):
+            for j, z in enumerate(order):
+                hot = jnp.concatenate(
+                    [
+                        (m.everyone[blk(z, yy, cc), 7:8] - base == row).astype(F32).astype(BF16)
+                        for cc in range(2)
+                    ],
+                    axis=1,
+                )
+                rows_of = dot_tn(hot, src.table[...]).astype(BF16)
+                m.found[z, yy] = rows_of.reshape(2, seqs, r, d)
+                for s in range(seqs):
+                    near, csem = streams[s][0], streams[s][7]
+                    copy = remote(
+                        m.found.at[z, yy, 1 - c, s],
+                        near.at[i, j],
+                        csem,
+                        i * 4 + j,
+                        peer(*NEAR_C),
+                    )
+                    copy.start()
+                    core.append(copy)
+            if i == 0:
+                for gen in trades:
+                    for _ in gen:
+                        pass
+                line(m.qkv_in, qkv_ref, sem.qkv_sem)
+
+        lane = lax.broadcasted_iota(jnp.int32, (1, 128), 1)
+        for k in range(5):
+            for i in range(blks // 2):
+                one, two = m.everyone[2 * i, k : k + 1], m.everyone[2 * i + 1, k : k + 1]
+                lanes = slice(i * 128, (i + 1) * 128)
+                vec_ref[2 * k : 2 * k + 1, lanes] = jnp.where(
+                    lane < 64, one, pltpu.roll(two, 64, 1)
+                )
+                vec_ref[2 * k + 1 : 2 * k + 2, lanes] = jnp.where(
+                    lane < 64, pltpu.roll(one, 64, 1), two
+                )
+        for i in range(blks):
+            ids_ref[:, i * 128 : (i + 1) * 128] = (m.everyone[i, 7:8] - base).astype(jnp.int32)
+        for i in range(4):
+            bias_ref[:, i * 128 : (i + 1) * 128] = m.everyone[i * 4 + g, pl.ds(5 + h, 1)]
+        eye = lax.broadcasted_iota(jnp.int32, (128, 128), 0) == lax.broadcasted_iota(
+            jnp.int32, (128, 128), 1
+        )
+
+        def column(k):
+            lanes = vec_ref[k : k + 1, pl.ds(pl.multiple_of(t * 128, 128), 128)]
+            return jnp.sum(jnp.where(eye, lanes, 0.0), axis=1, keepdims=True)
+
+        def send_pair(s, j):
+            z = 2 * s + j
+            return place_copy(
+                m.projected.at[:, j, :, pl.ds(s * n, n)],
+                held.at[:, :, pl.ds(pl.multiple_of(o * n, n), n)],
+                sem.send.at[z],
+                sem.recv.at[o],
+                (h, z * 4 + g),
+            )
+
+        def stream(s):
+            yield from rows_steps(
+                lambda z, yy: m.found.at[z, yy, c, s], *streams[s], m.rows.at[s]
+            )
+            second = src.second[s * r : (s + 1) * r]
+            typed = vec_ref[8:9] * (1.0 - second) + vec_ref[9:10] * second
+            value = src.hidden[s].astype(F32) + m.rows[s] + typed
+            emb_ref[s] = value
+            m.low[s] = value.astype(BF16)
+            yield from gather_steps(
+                lambda i: m.low.at[s, pl.ds(i * half, half)],
+                lambda i, slot: plane_ref.at[s, slot, pl.ds(i * half, half)],
+                own[gather_ids[s]],
+            )
+            if s == 0:
+                for copy in bulk:
+                    copy.wait()
+                bulk.clear()
+                line(up_in.at[:, :, pl.ds(0, fh)], up_one, sem.up_sem)
+            part = lax.dot_general(
+                qkv_ref[...].reshape(d, wq),
+                plane_ref[s].reshape(n, d),
+                (((0,), (1,)), ((), ())),
+                preferred_element_type=F32,
+            )
+            here = slice(s * n, (s + 1) * n)
+            third = wq // 3
+            m.projected[0, :, :, here] = (part[:third] + column(0)).astype(BF16).reshape(2, he, n)
+            m.projected[1, :, :, here] = part[third : 2 * third].astype(BF16).reshape(2, he, n)
+            m.projected[2, :, :, here] = (
+                (part[2 * third :] + column(1)).astype(BF16).reshape(2, he, n)
+            )
+            for j in range(2):
+
+                @pl.when(o != 2 * s + j)
+                def _():
+                    send_pair(s, j).start()
+
+                @pl.when(o == 2 * s + j)
+                def _():
+                    held[:, :, pl.ds(pl.multiple_of(o * n, n), n)] = m.projected[:, j, :, here]
+
+            yield
+
+        gens = [stream(s) for s in range(seqs)]
+        for _ in range(lag):
+            next(gens[0])
+        while gens:
+            for gen in list(gens):
+                try:
+                    next(gen)
+                except StopIteration:
+                    gens.remove(gen)
+        next(weights)
+        for z in range(4):
+
+            @pl.when(z != o)
+            def _():
+                ref = held.at[:, :, pl.ds(z * n, n)]
+                place_copy(ref, ref, sem.send.at[0], sem.recv.at[z], peer(*NEAR_X)).wait_recv()
+
+        line(src.down_cut.at[:, pl.ds(0, half_d)], down_one, sem.down_sem)
+        m.keys[...] = held[1].astype(F32).T.astype(BF16)
+        mine = pl.ds(pl.multiple_of((o // 2) * n, n), n)
+
+        def back(i, z):
+            return remote(
+                m.pair_low.at[:, pl.ds(pl.multiple_of(z * n, n), n)],
+                attended.at[o % 2, :, mine],
+                sem.back_sem,
+                i,
+                (h, z * 4 + g),
+            )
+
+        @pl.loop(0, 4 * (n // cols))
+        def _(step):
+            i = step // (n // cols)
+            z = (o + 1 + i) % 4
+            here = pl.ds(pl.multiple_of(z * n + step % (n // cols) * cols, cols), cols)
+            q = (held[0, :, here].astype(F32) * scale).astype(BF16)
+            s = jnp.dot(m.keys[...], q, preferred_element_type=F32)
+            peak = jnp.max(s, axis=0, keepdims=True)
+            p = jnp.exp(s - peak)
+            total = jnp.sum(p, axis=0, keepdims=True)
+            out = jnp.dot(held[2], p.astype(BF16), preferred_element_type=F32) / total
+            o_ref[:, here] = out
+            m.pair_low[:, here] = out.astype(BF16)
+            lse_ref[:, here] = peak + jnp.log(total)
+
+            @pl.when((step % (n // cols) == n // cols - 1) & (i < 3))
+            def _():
+                back(i, z).start()
+
+        attended[o % 2, :, mine] = m.pair_low[:, pl.ds(pl.multiple_of(o * n, n), n)]
+        for i in range(3):
+            back(i, (o + 1 + i) % 4).wait_send()
+            z = (o + 3 - i) % 4
+            landed(attended.at[z % 2, :, pl.ds(pl.multiple_of((z // 2) * n, n), n)], sem.back_sem, i)
+        for _ in weights:
+            pass
+        for copy in bulk:
+            copy.wait()
+        for copy in core:
+            copy.wait_send()
+        for s in range(seqs):
+            for j in range(2):
+
+                @pl.when(o != 2 * s + j)
+                def _():
+                    send_pair(s, j).wait_send()
+
+    return Part(
+        run,
+        list(vars(x).values()),
+        [
+            ((2, he, 2 * n), BF16),
+            ((3, he, length), BF16),
+            ((he, length), F32),
+            ((1, length), F32),
+            ((seqs, r, d), F32),
+            ((seqs, 8, r, d), BF16),
+            ((4,) + x.qkv_cut.shape, BF16),
+            ((2,) + x.out_weight.shape, BF16),
+            ((4, four, e, fh), BF16),
+            (x.up_cut.shape, BF16),
+            ((4, fcols, half_d), BF16),
+            ((10, d), F32),
+            ((1, f), F32),
+            ((1, blks * seqs * r), jnp.int32),
+        ],
+        need,
+        ALL,
+    )
+
+
+def finish_kernel(odd, layer, hid, pos, down, up, qkv, out, totals, *outs):
+    o_layer, o_hid, o_pos, o_types, o_qkv, o_out, o_up, o_down, o_upb, o_gains, o_bias = outs
+    o_layer[...] = layer[...]
+    o_hid[...] = hid[...]
+    o_pos[...] = pos[...]
+    o_qkv[...] = qkv[...].astype(F32)
+    o_out[...] = out[...].astype(F32)
+    o_up[...] = up[...].astype(F32)
+    o_down[...] = down[...].astype(F32)
+    t = totals[...]
+    mine = jnp.where(odd[0] == 1, t[:, 64:], t[:, :64])
+    o_types[...] = mine[6:8]
+    o_gains[...] = mine[4:6]
+    o_bias[0:1] = mine[8:9]
+    o_bias[1:2] = mine[9:10]
+    o_bias[2:6] = mine[0:4]
+    o_upb[...] = t[16:18]
+
+
+def finish(odd, layer, hid, pos, down, up, qkv, out, totals):
+    like = lambda a, dtype=F32: jax.ShapeDtypeStruct(a.shape, dtype)
+    e = out.shape[0]
+    return pl.pallas_call(
+        finish_kernel,
+        name="finish",
+        out_shape=[
+            like(layer, BF16),
+            like(hid),
+            like(pos),
+            jax.ShapeDtypeStruct((2, e), F32),
+            like(qkv),
+            like(out),
+            like(up),
+            like(down),
+            jax.ShapeDtypeStruct((2, 128), F32),
+            jax.ShapeDtypeStruct((2, e), F32),
+            jax.ShapeDtypeStruct((6, e), F32),
+        ],
+        in_specs=[pl.BlockSpec(memory_space=pltpu.SMEM)] + [VSPEC] * 8,
+        out_specs=[VSPEC] * 11,
+        compiler_params=pltpu.CompilerParams(vmem_limit_bytes=48 << 20),
+    )(odd, layer, hid, pos, down, up, qkv, out, totals)
 def norm_layer(values_in, gain_row, offset_row):
     average = jnp.mean(values_in, axis=-1, keepdims=True)
     centred = values_in - average
@@ -153,7 +1661,7 @@
     return fold_queries
 
 
-def on_device(
+def layer_in_blocks(
     hidden,
     pos_ids,
     type_ids,
@@ -450,6 +1958,136 @@
     )
 
 
+BIG = 56 << 20
+WHOLE = 67043328
+LAG = 3
+CHUNKS = 4
+CHUNK_LAG = 1
+EARLY = (1, 3)
+TURNS = ((1, 3), (2, 4, 6, 8), (6, 12))
+
+
+def layer_in_planes(
+    hidden,
+    pos_ids,
+    type_ids,
+    cotangent,
+    pos_table,
+    type_table,
+    query_key_value_weight,
+    attention_output_weight,
+    up_projection_weight,
+    down_projection_weight,
+    up_projection_bias,
+    norm_gains,
+    biases,
+):
+    seqs, seg, width = hidden.shape
+    blks = lax.axis_size("blk")
+    h = lax.axis_index("head")
+    b = lax.axis_index("blk")
+    o, g = b // 4, b % 4
+    rows = seqs * seg
+    e = width // HEADS
+    ff = up_projection_weight.shape[1]
+    scale = 1.0 / math.sqrt(e)
+    slots = pos_table.shape[0]
+    fcols = ff // blks // 2
+    plane_rows = 8 * rows
+
+    small = jnp.concatenate(
+        [
+            biases.astype(F32),
+            norm_gains.astype(F32),
+            type_table.astype(F32),
+            up_projection_bias.astype(F32).reshape(4, e),
+        ]
+    ).reshape(7, 2 * e)
+    packed = jnp.concatenate([small, pos_ids.astype(F32).reshape(1, rows)])
+    qkv_cut = query_key_value_weight.reshape(e, 3, 2, 4, 2 * e)
+    qkv_cut = lax.dynamic_slice_in_dim(qkv_cut, h, 1, 2).reshape(e, 3, 4, 2 * e)
+    qkv_cut = qkv_cut.transpose(2, 0, 1, 3).reshape(4, e, 6 * e)
+    up_cut = up_projection_weight.reshape(e, 4, 4, 2, fcols)
+    up_cut = lax.dynamic_slice_in_dim(up_cut, h, 1, 3).reshape(e, 4, 4, fcols)
+    up_cut = up_cut.transpose(2, 0, 1, 3).reshape(4, e, 4 * fcols)
+    down_cut = lax.dynamic_slice_in_dim(down_projection_weight, h * fcols, fcols, 0)
+    is_second = (type_ids.reshape(rows, 1) == 1).astype(F32)
+    begin = SimpleNamespace(
+        packed=packed,
+        out_weight=attention_output_weight,
+        qkv_cut=qkv_cut,
+        up_cut=up_cut,
+        down_cut=down_cut,
+        table=pos_table,
+        hidden=hidden,
+        second=is_second,
+    )
+    (
+        (
+            attended,
+            held,
+            pair_out,
+            lse,
+            embedded,
+            plane_low,
+            qkv_own,
+            out_own,
+            up_one,
+            up_cut,
+            down_one,
+            vectors,
+            up_bias,
+            pos_all,
+        ),
+    ) = fused("first_half", 0, [first_half(begin, scale, LAG)], WHOLE)
+    parts = SimpleNamespace(
+        attended=attended,
+        out_own=out_own.reshape(2 * e, width),
+        embedded=embedded,
+        cotangent=cotangent,
+        up_one=up_one,
+        up_cut=up_cut,
+        down_one=down_one,
+        down_cut=down_cut,
+        up_bias=up_bias,
+        vectors=vectors,
+        held=held,
+        pair_out=pair_out,
+        lse=lse,
+        qkv_own=qkv_own.reshape(width, 6 * e),
+        plane_low=plane_low,
+        ids=pos_all,
+        second=is_second,
+    )
+    sizes = (slots, CHUNKS, LAG, CHUNK_LAG, scale)
+    ((layer_out, grad_hidden, pos, down, up, qkv, out, totals),) = fused(
+        "second_half", 4, [second_half(parts, sizes)], WHOLE
+    )
+    outs = finish(
+        (b % 2).reshape(1),
+        layer_out,
+        grad_hidden,
+        pos,
+        down.reshape(2 * fcols, width),
+        up,
+        qkv,
+        out,
+        totals,
+    )
+    return (*outs[:8], outs[8].reshape(4 * e), *outs[9:])
+
+
+def planes_fit(hidden, head_axis, blk_axis):
+    seqs, seg, width = hidden.shape
+    return head_axis == 2 and blk_axis == HEADS and seqs == 2 and seqs * seg == 2 * width // HEADS
+
+
+def on_device(hidden, *rest):
+    if planes_fit(hidden, lax.axis_size("head"), lax.axis_size("blk")):
+        return layer_in_planes(hidden, *rest)
+    return layer_in_blocks(hidden, *rest)
+
+
 def solution(mesh):
     in_specs = (
         P(None, ("head", "blk"), None),

time: 1850 us -> 383 us (0.21)
  waiting for transfers between devices: 1300 us -> 0 us
  Pallas kernels: 0 us -> 357 us
  blocking collectives: 212 us -> 0 us
  matrix products: 155 us -> 0 us
  local copies, waits for them, and re-layouts: 115 us -> 15.7 us
  other arithmetic: 26 us -> 2.74 us
  starting transfers between devices: 19.4 us -> 0 us
    reduce_scatter x5 -> x0, waiting for transfers between devices: 720 us -> none  [the longest x1 334 us: on_device(): lax.psum_scatter(buffer[:length], 'blk', scatter_dimension=0, tiled=True)]
    pallas_call x0 -> x3, Pallas kernels: none -> 357 us  [the longest x2 354 us: fused(): pl.pallas_call(kernel, name=name, out_shape=[jax.ShapeDtypeStruct(s, d) f...]
    all_gather x9 -> x0, waiting for transfers between devices: 322 us -> none  [the longest x1 105 us: on_device(): portion = lax.all_gather(pos_table, 'blk', axis=0, tiled=True)]
    dot_general x41 -> x0, matrix products: 155 us -> none  [the longest x12 26.1 us: block_scores(): jnp.einsum('sqhe,skhe->shqk', query_heads, key_block, preferred_element_t...]
    psum x1 -> x0, waiting for transfers between devices: 126 us -> none  [on_device(): lax.psum((shard_qkv, shard_out, shard_up, shard_down, shard_up_bias, shar...]
    all_gather x6 -> x0, blocking collectives: 120 us -> none  [the longest x1 23.7 us: fetch_weights(): lax.all_gather(type_table, 'blk', axis=1, tiled=True)]
    unnamed x21 -> x0, waiting for transfers between devices: 118 us -> none
    unnamed x1 -> x0, blocking collectives: 59.7 us -> none
  transfers between devices with their start and end apart: 23 -> 0, of which waited for: 15 -> 0; matrix products, arithmetic and copies ran while one was open for 15% -> 0% of each run, Pallas kernels for 0% -> 0%
where the time goes in v4:
time: 383 us; the launch traced here: 377 us
  Pallas kernels  357 us (93%)
  local copies, waits for them, and re-layouts  15.7 us (4%)
    pallas_call x2, Pallas kernels, fused(): pl.pallas_call(kernel, name=name, out_shape=[jax.ShapeDtypeStruct(s, d) f...  354 us
    unnamed x18, local copies, waits for them, and re-layouts  8.27 us

profile of v4, /device:TPU:0, one launch (start us, length us, event | category | flops | bytes accessed | tf_op | source)
XLA Modules:
  0.0 376.6 jit_solution(5414849033183312592)
XLA Ops:
  0.6 0.0 copy-start.8
  0.7 0.7 convert_element_type.12
  1.4 0.1 reshape.93
  1.5 0.7 compare_convert_fusion
  2.2 0.7 reshape.90
  2.9 0.7 maximum_convert_fusion
  3.6 0.1 reshape.105
  3.7 0.6 pad_maximum_fusion.refs_0_
  4.3 0.8 reshape.107.refs_7_.refs_16_
  5.1 1.7 constant_dynamic-slice_fusion.refs_4_.refs_7_
  6.7 1.3 reshape.94
  8.0 0.1 constant_dynamic-slice_fusion.2
  8.1 0.1 copy.35
  8.2 0.8 reshape.96.refs_2_
  9.0 0.0 copy-done.8
  9.1 0.4 reshape.97
  9.4 0.5 constant_dynamic-slice_fusion.1
  10.0 0.1 copy.34
  10.1 0.8 reshape.99.refs_3_
  10.9 119.4 %first_half.1 = (bf16[2,64,1024]{2,1,0:T(8,128)(2,1)}, bf16[3,64,2048]{2,1,0:T(8,128)(2,1)}, f32[64,2048]{1,0:T(8,128)}, f32[1,2048]{1,0:T(1,128)}, f32[2,64,102...) custom-call(f32[8,128]{1,0:T(8,128)} %pad_maximum_fusion.refs_0_, ...), custom_call_target="tpu_custom_call" | custom-call | tf_op jit(solution)/shard_map/first_half/pallas_call | solution.py:105
  130.3 234.8 %second_half.1 = (bf16[2,64,1024]{2,1,0:T(8,128)(2,1)}, f32[2,64,1024]{2,1,0:T(8,128)}, f32[512,1024]{1,0:T(8,128)}, bf16[2,128,1024]{2,1,0:T(8,128)(2,1)}, bf16...) custom-call(bf16[2,64,1024]{2,1,0:T(8,128)(2,1)} %get-tuple-element.44.refs_0_, ...), custom_call_target="tpu_custom_call" | custom-call | tf_op jit(solution)/shard_map/second_half/pallas_call | solution.py:105
  365.2 0.0 copy-start
  365.2 1.6 copy-done
  366.8 0.0 copy-start.1
  366.8 1.0 copy-done.1
  367.8 0.0 copy-start.2
  367.8 1.0 copy-done.2
  368.9 0.0 copy-start.3
  368.9 1.0 copy-done.3
  369.9 0.0 copy-start.4
  369.9 1.0 copy-done.4
  370.9 0.0 copy-start.5
  370.9 0.9 copy-done.5
  371.9 0.0 copy-start.6
  371.9 0.9 copy-done.6
  372.8 0.0 copy-start.7
  372.8 0.7 copy-done.7
  373.5 2.7 finish.1
Async XLA Ops:
  0.6 8.4 %copy-start.8 = (bf16[64,4096]{1,0:T(8,128)(2,1)S(1)}, bf16[64,4096]{1,0:T(8,128)(2,1)}, u32[]{:S(2)}) copy-start(bf16[64,4096]{1,0:T(8,128)(2,1)} %param.21) | copy-start | bytes 1572868
  365.2 1.6 copy-start
  366.8 1.0 copy-start.1
  367.8 1.0 copy-start.2
  368.9 1.0 copy-start.3
  369.9 1.0 copy-start.4
  370.9 0.9 copy-start.5
  371.9 0.9 copy-start.6
  372.8 0.7 copy-start.7

commit v5 on v4

--- a/solution.py
+++ b/solution.py
@@ -144,16 +144,6 @@
             copy.wait()
 
     return Part(run, [x], [(out_lead, x.dtype)], [sems(len(peers))], peers)
-
-
-def blk_exchange(x):
-    return exchange(
-        x,
-        [(0, 0, 1, 0), (0, 0, 0, 1), (0, 0, 1, 1)],
-        x.shape,
-        lambda r, d: r.at[d[2] * 2 + d[3]],
-        lambda r, s: r.at[s[2] * 2 + s[3]],
-    )
 
 
 def small_gather(x):
@@ -566,7 +556,7 @@
     seqs, r, d = x.embedded.shape
     planes, four, e, fh = x.up_one.shape
     f = 2 * fh
-    fcols = x.down_cut.shape[0]
+    fcols = x.down_weight.shape[0] // 2
     half, half_d = r // 2, d // 2
     rows, q_rows = 8 * r, 4 * r
     three, he, length = x.held.shape
@@ -672,7 +662,8 @@
         tail = []
 
         up_more = src.up_cut.at[:, :, pl.ds(fh, fh)]
-        down_more = src.down_cut.at[:, pl.ds(half_d, half_d)]
+        down_rows = pl.ds(pl.multiple_of(h * fcols, fcols), fcols)
+        down_more = src.down_weight.at[down_rows, pl.ds(half_d, half_d)]
         weights = []
         for k, p in enumerate(COLUMN):
             for ref, dst, s in (
@@ -858,16 +849,21 @@
             last = scatter_steps(piece(partial, s), plain(total, s), *scatters[2])
             next(last)
             if s == seqs - 1:
-                all_grads = m.grad_g[...].reshape(seqs * rows, d)
-                for z in range(planes):
-                    cols = slice(z * fcols, (z + 1) * fcols)
+                @pl.loop(0, planes)
+                def _(z):
+                    cols = pl.ds(pl.multiple_of(z * fcols, fcols), fcols)
+                    all_grads = m.grad_g[...].reshape(seqs * rows, d)
                     m.down_part[z] = dot_tn(m.act[:, cols], all_grads).astype(BF16)
+
                 step(down)
                 yield
-                for z in range(planes):
-                    cols = slice(z * 4 * e, (z + 1) * 4 * e)
+
+                @pl.loop(0, planes)
+                def _(z):
+                    cols = pl.ds(pl.multiple_of(z * 4 * e, 4 * e), 4 * e)
                     all_first = m.first_g[:, :, :, cols].reshape(seqs * rows, 4 * e)
                     m.up_part[z] = dot_tn(all_first, m.inner_grad[...]).astype(BF16)
+
                 yield
             yield from last
             grad = m.grad_two[s] + total[s]
@@ -922,8 +918,13 @@
         q32 = held[0].astype(F32) * scale
         qs[...] = q32.astype(BF16)
         q_t[...] = q32.T.astype(BF16)
-        row = lax.broadcasted_iota(jnp.int32, (slots, 1), 0)
-        m.pick[...] = (src.ids[...] == row).astype(F32).astype(BF16)
+
+        @pl.loop(0, slots // 64)
+        def _(k):
+            row = lax.broadcasted_iota(jnp.int32, (64, 1), 0) + k * 64
+            some = pl.ds(pl.multiple_of(k * 64, 64), 64)
+            m.pick[some] = (src.ids[...] == row).astype(F32).astype(BF16)
+
         for z in range(4):
 
             @pl.when(z != o)
@@ -1019,13 +1020,18 @@
                 ysem,
                 csem,
             )
-            found = jnp.dot(
-                m.pick[...],
-                m.gathered[q].reshape(blks * own_rows, w),
-                preferred_element_type=F32,
-            )
-            pos_ref[:, cols] = found
-            m.pos_low[q] = found.astype(BF16)
+
+            @pl.loop(0, slots // 128)
+            def _(k):
+                some = pl.ds(pl.multiple_of(k * 128, 128), 128)
+                found = jnp.dot(
+                    m.pick[some],
+                    m.gathered[q].reshape(blks * own_rows, w),
+                    preferred_element_type=F32,
+                )
+                pos_ref[some, cols] = found
+                m.pos_low[q, some] = found.astype(BF16)
+
             copy = remote(
                 m.pos_low.at[q], m.pos_held.at[q], sem.pair_sem, q, peer(*NEAR_X)
             )
@@ -1045,16 +1051,17 @@
                 except StopIteration:
                     active.remove(gen)
             if turn == 0:
-                low_all = src.plane_low[...].reshape(seqs * rows, d)
-                for z in range(planes):
-                    cols = slice(z * 4 * e, (z + 1) * 4 * e)
+                @pl.loop(0, planes)
+                def _(z):
+                    cols = pl.ds(pl.multiple_of(z * 4 * e, 4 * e), 4 * e)
                     part = lax.dot_general(
-                        low_all[:, cols],
+                        src.plane_low[:, :, :, cols].reshape(seqs * rows, 4 * e),
                         all_dqkv(),
                         (((0,), (1,)), ((), ())),
                         preferred_element_type=F32,
                     )
                     m.qkv_part[z] = part.astype(BF16)
+
                 step(qkv)
                 ones = jnp.ones((8, 2 * n), BF16)
                 heads = dot_nt(ones, all_dqkv())
@@ -1183,18 +1190,17 @@
     names = list(vars(x))
     seqs, r, d = x.hidden.shape
     slots = x.table.shape[0]
-    four, e, wq = x.qkv_cut.shape
-    f = x.up_cut.shape[2]
-    fcols = x.down_cut.shape[0]
+    e = x.qkv_weight.shape[0]
+    four, wq, f = 4, x.qkv_weight.shape[1] // 8, x.up_weight.shape[1] // 8
+    fcols = x.down_weight.shape[0] // 2
     he = wq // 6
     n = 8 * r
     length = 4 * n
     half, fh, half_d = r // 2, f // 2, d // 2
     blks = 16
     cols = 256
-    small = small_gather(x.packed)
+    small = small_gather(jax.ShapeDtypeStruct((8, 128), F32))
     outw = out_weights(x.out_weight)
-    trade_qkv, trade_up = blk_exchange(x.qkv_cut), blk_exchange(x.up_cut)
     need = []
 
     def many(specs):
@@ -1204,22 +1210,22 @@
 
     block = (r, d)
     shapes = dict(
-        everyone=((blks,) + x.packed.shape, F32),
+        packed=((8, 128), F32),
+        everyone=((blks, 8, 128), F32),
         found=((4, 2, 2, seqs, r, d), BF16),
         rows=((seqs, r, d), F32),
         low=((seqs, r, d), BF16),
-        qkv_in=(x.qkv_cut.shape, BF16),
+        qkv_in=((four, e, wq), BF16),
         projected=((3, 2, he, 2 * n), BF16),
         keys=((length, he), BF16),
         pair_low=((he, length), BF16),
     )
     ids = {k: many([pltpu.VMEM(*v)])[0] for k, v in shapes.items()}
-    counts = dict(qkv_sem=3, up_sem=3, down_sem=3, back_sem=3)
+    counts = dict(qkv_sem=3, up_sem=3, down_sem=3, back_sem=3, qkv_trade=9, up_trade=12)
     sem_ids = {k: many([sems(v)])[0] for k, v in counts.items()}
     for k in ("send", "recv"):
         sem_ids[k] = many([pltpu.SemaphoreType.DMA((4,))])[0]
     small_ids, outw_ids = many(small.scratch), many(outw.scratch)
-    trade_ids = many(trade_qkv.scratch), many(trade_up.scratch)
     row_ids = [
         many(
             [
@@ -1242,23 +1248,49 @@
     def run(ins, outs, own):
         src = SimpleNamespace(**dict(zip(names, ins)))
         attended, held, o_ref, lse_ref, emb_ref, plane_ref, qkv_ref = outs[:7]
-        outw_ref, up_one, up_in, down_one, vec_ref, bias_ref, ids_ref = outs[7:]
+        outw_ref, up_one, up_in, down_one, vec_ref, bias_ref, ids_ref, second_ref = outs[7:]
         m = SimpleNamespace(**{k: own[v] for k, v in ids.items()})
         sem = SimpleNamespace(**{k: own[v] for k, v in sem_ids.items()})
         pick_refs = lambda some: [own[i] for i in some]
         h, o, y, c = place()
         g = y * 2 + c
         t = h * 4 + g
-        gather_small = small.run((src.packed,), (m.everyone,), pick_refs(small_ids))
-        trades = [
-            trade_qkv.run((src.qkv_cut,), (m.qkv_in,), pick_refs(trade_ids[0])),
-            trade_up.run((src.up_cut,), (up_in,), pick_refs(trade_ids[1])),
-        ]
+        side = lambda a: jnp.concatenate([a[0:1], a[1:2]], axis=1).astype(F32)
+        for k in range(3):
+            m.packed[k : k + 1] = side(src.biases[2 * k : 2 * k + 2])
+        m.packed[3:4] = side(src.gains[...])
+        m.packed[4:5] = side(src.types[...])
+        m.packed[5:7] = src.up_bias[...].astype(F32)
+        m.packed[7:8] = side(src.pos_ids[...])
+        gather_small = small.run((m.packed,), (m.everyone,), pick_refs(small_ids))
+        trades = []
+
+        def trade(ref, dst, s, lanes_of):
+            count = len(lanes_of(0))
+            for k, p in enumerate(((0, 0, 1, 0), (0, 0, 0, 1), (0, 0, 1, 1))):
+                to = (1 - y if p[2] else y) * 2 + (1 - c if p[3] else c)
+                for i, lane in enumerate(lanes_of(to)):
+                    copy = remote(
+                        ref.at[:, pl.ds(pl.multiple_of(lane * 128, 128), 128)],
+                        dst.at[g, :, pl.ds(i * 128, 128)],
+                        s,
+                        k * count + i,
+                        peer(*p),
+                    )
+                    copy.start()
+                    trades.append(copy)
+            for i, lane in enumerate(lanes_of(g)):
+                dst[g, :, i * 128 : (i + 1) * 128] = ref[
+                    :, pl.ds(pl.multiple_of(lane * 128, 128), 128)
+                ]
+
         weights = outw.run((src.out_weight,), (outw_ref,), pick_refs(outw_ids))
+        qkv_lanes = lambda k: [i * 8 + h * 4 + k for i in range(3)]
+        up_lanes = lambda k: [(i * 4 + k) * 2 + h for i in range(4)]
+        trade(src.qkv_weight, m.qkv_in, sem.qkv_trade, qkv_lanes)
         next(gather_small)
-        next(trades[0])
         yield
-        next(trades[1])
+        trade(src.up_weight, up_in, sem.up_trade, up_lanes)
         bulk = []
 
         def line(ref, dst, s):
@@ -1301,9 +1333,8 @@
                     copy.start()
                     core.append(copy)
             if i == 0:
-                for gen in trades:
-                    for _ in gen:
-                        pass
+                for copy in trades:
+                    copy.wait()
                 line(m.qkv_in, qkv_ref, sem.qkv_sem)
 
         lane = lax.broadcasted_iota(jnp.int32, (1, 128), 1)
@@ -1325,9 +1356,13 @@
             jnp.int32, (128, 128), 1
         )
 
+        def upright(lanes):
+            return jnp.sum(jnp.where(eye, lanes, 0.0), axis=1, keepdims=True)
+
         def column(k):
-            lanes = vec_ref[k : k + 1, pl.ds(pl.multiple_of(t * 128, 128), 128)]
-            return jnp.sum(jnp.where(eye, lanes, 0.0), axis=1, keepdims=True)
+            return upright(vec_ref[k : k + 1, pl.ds(pl.multiple_of(t * 128, 128), 128)])
+
+        second_ref[...] = upright(side(src.type_ids[...]))
 
         def send_pair(s, j):
             z = 2 * s + j
@@ -1343,7 +1378,7 @@
             yield from rows_steps(
                 lambda z, yy: m.found.at[z, yy, c, s], *streams[s], m.rows.at[s]
             )
-            second = src.second[s * r : (s + 1) * r]
+            second = second_ref[s * r : (s + 1) * r]
             typed = vec_ref[8:9] * (1.0 - second) + vec_ref[9:10] * second
             value = src.hidden[s].astype(F32) + m.rows[s] + typed
             emb_ref[s] = value
@@ -1400,7 +1435,8 @@
                 ref = held.at[:, :, pl.ds(z * n, n)]
                 place_copy(ref, ref, sem.send.at[0], sem.recv.at[z], peer(*NEAR_X)).wait_recv()
 
-        line(src.down_cut.at[:, pl.ds(0, half_d)], down_one, sem.down_sem)
+        down_rows = pl.ds(pl.multiple_of(h * fcols, fcols), fcols)
+        line(src.down_weight.at[down_rows, pl.ds(0, half_d)], down_one, sem.down_sem)
         m.keys[...] = held[1].astype(F32).T.astype(BF16)
         mine = pl.ds(pl.multiple_of((o // 2) * n, n), n)
 
@@ -1460,14 +1496,15 @@
             ((1, length), F32),
             ((seqs, r, d), F32),
             ((seqs, 8, r, d), BF16),
-            ((4,) + x.qkv_cut.shape, BF16),
+            ((4, four, e, wq), BF16),
             ((2,) + x.out_weight.shape, BF16),
             ((4, four, e, fh), BF16),
-            (x.up_cut.shape, BF16),
+            ((four, e, f), BF16),
             ((4, fcols, half_d), BF16),
             ((10, d), F32),
             ((1, f), F32),
             ((1, blks * seqs * r), jnp.int32),
+            ((seqs * r, 1), F32),
         ],
         need,
         ALL,
@@ -1493,29 +1530,36 @@
     o_upb[...] = t[16:18]
 
 
-def finish(odd, layer, hid, pos, down, up, qkv, out, totals):
-    like = lambda a, dtype=F32: jax.ShapeDtypeStruct(a.shape, dtype)
+def finish(odd, layer, hid, pos, down, up, qkv, out, totals, steps=4):
     e = out.shape[0]
+    large = [(layer, BF16), (hid, F32), (pos, F32), (qkv, F32), (out, F32), (up, F32), (down, F32)]
+
+    def cut(a):
+        return pl.BlockSpec((a.shape[0] // steps, a.shape[1]), lambda i: (i, 0))
+
+    def whole(*shape):
+        return pl.BlockSpec(shape, lambda i: (0, 0))
+
+    like = {id(a): jax.ShapeDtypeStruct(a.shape, dtype) for a, dtype in large}
+    full = lambda *shape: jax.ShapeDtypeStruct(shape, F32)
     return pl.pallas_call(
         finish_kernel,
         name="finish",
-        out_shape=[
-            like(layer, BF16),
-            like(hid),
-            like(pos),
-            jax.ShapeDtypeStruct((2, e), F32),
-            like(qkv),
-            like(out),
-            like(up),
-            like(down),
-            jax.ShapeDtypeStruct((2, 128), F32),
-            jax.ShapeDtypeStruct((2, e), F32),
-            jax.ShapeDtypeStruct((6, e), F32),
-        ],
-        in_specs=[pl.BlockSpec(memory_space=pltpu.SMEM)] + [VSPEC] * 8,
-        out_specs=[VSPEC] * 11,
-        compiler_params=pltpu.CompilerParams(vmem_limit_bytes=48 << 20),
+        grid=(steps,),
+        out_shape=[like[id(a)] for a in (layer, hid, pos)]
+        + [full(2, e)]
+        + [like[id(a)] for a in (qkv, out, up, down)]
+        + [full(2, 128), full(2, e), full(6, e)],
+        in_specs=[pl.BlockSpec(memory_space=pltpu.SMEM)]
+        + [cut(a) for a in (layer, hid, pos, down, up, qkv, out)]
+        + [whole(24, 128)],
+        out_specs=[cut(a) for a in (layer, hid, pos)]
+        + [whole(2, e)]
+        + [cut(a) for a in (qkv, out, up, down)]
+        + [whole(2, 128), whole(2, e), whole(6, e)],
     )(odd, layer, hid, pos, down, up, qkv, out, totals)
+
+
 def norm_layer(values_in, gain_row, offset_row):
     average = jnp.mean(values_in, axis=-1, keepdims=True)
     centred = values_in - average
@@ -1960,7 +2004,7 @@
 
 BIG = 56 << 20
 WHOLE = 67043328
-LAG = 3
+LAG = 1
 CHUNKS = 4
 CHUNK_LAG = 1
 EARLY = (1, 3)
@@ -1983,44 +2027,27 @@
     biases,
 ):
     seqs, seg, width = hidden.shape
-    blks = lax.axis_size("blk")
-    h = lax.axis_index("head")
     b = lax.axis_index("blk")
-    o, g = b // 4, b % 4
     rows = seqs * seg
     e = width // HEADS
-    ff = up_projection_weight.shape[1]
     scale = 1.0 / math.sqrt(e)
     slots = pos_table.shape[0]
-    fcols = ff // blks // 2
-    plane_rows = 8 * rows
-
-    small = jnp.concatenate(
-        [
-            biases.astype(F32),
-            norm_gains.astype(F32),
-            type_table.astype(F32),
-            up_projection_bias.astype(F32).reshape(4, e),
-        ]
-    ).reshape(7, 2 * e)
-    packed = jnp.concatenate([small, pos_ids.astype(F32).reshape(1, rows)])
-    qkv_cut = query_key_value_weight.reshape(e, 3, 2, 4, 2 * e)
-    qkv_cut = lax.dynamic_slice_in_dim(qkv_cut, h, 1, 2).reshape(e, 3, 4, 2 * e)
-    qkv_cut = qkv_cut.transpose(2, 0, 1, 3).reshape(4, e, 6 * e)
-    up_cut = up_projection_weight.reshape(e, 4, 4, 2, fcols)
-    up_cut = lax.dynamic_slice_in_dim(up_cut, h, 1, 3).reshape(e, 4, 4, fcols)
-    up_cut = up_cut.transpose(2, 0, 1, 3).reshape(4, e, 4 * fcols)
-    down_cut = lax.dynamic_slice_in_dim(down_projection_weight, h * fcols, fcols, 0)
-    is_second = (type_ids.reshape(rows, 1) == 1).astype(F32)
+    fcols = down_projection_weight.shape[0] // 2
+
+    token_shape = (seqs, seg, width)
     begin = SimpleNamespace(
-        packed=packed,
+        biases=biases,
+        gains=norm_gains,
+        types=type_table,
+        up_bias=up_projection_bias.reshape(2, 2 * e),
+        pos_ids=pos_ids,
+        type_ids=type_ids,
+        qkv_weight=query_key_value_weight,
         out_weight=attention_output_weight,
-        qkv_cut=qkv_cut,
-        up_cut=up_cut,
-        down_cut=down_cut,
+        up_weight=up_projection_weight,
+        down_weight=down_projection_weight,
         table=pos_table,
         hidden=hidden,
-        second=is_second,
     )
     (
         (
@@ -2038,6 +2065,7 @@
             vectors,
             up_bias,
             pos_all,
+            is_second,
         ),
     ) = fused("first_half", 0, [first_half(begin, scale, LAG)], WHOLE)
     parts = SimpleNamespace(
@@ -2048,7 +2076,7 @@
         up_one=up_one,
         up_cut=up_cut,
         down_one=down_one,
-        down_cut=down_cut,
+        down_weight=down_projection_weight,
         up_bias=up_bias,
         vectors=vectors,
         held=held,
@@ -2065,8 +2093,8 @@
     )
     outs = finish(
         (b % 2).reshape(1),
-        layer_out,
-        grad_hidden,
+        layer_out.reshape(rows, width),
+        grad_hidden.reshape(rows, width),
         pos,
         down.reshape(2 * fcols, width),
         up,
@@ -2074,7 +2102,13 @@
         out,
         totals,
     )
-    return (*outs[:8], outs[8].reshape(4 * e), *outs[9:])
+    return (
+        outs[0].reshape(token_shape),
+        outs[1].reshape(token_shape),
+        *outs[2:8],
+        outs[8].reshape(4 * e),
+        *outs[9:],
+    )
 
 
 def planes_fit(hidden, head_axis, blk_axis):

time: 383 us -> 353 us (0.922); the launches traced: 377 us -> 352 us
  local copies, waits for them, and re-layouts: 15.7 us -> 0 us
  Pallas kernels: 357 us -> 351 us
    unnamed x18 -> x0, local copies, waits for them, and re-layouts: 8.27 us -> none
    pallas_call x2, Pallas kernels: 354 us -> 346 us  [fused(): pl.pallas_call(kernel, name=name, out_shape=[jax.ShapeDtypeStruct(s, d) f...]
    reshape x7 -> x0, local copies, waits for them, and re-layouts: 4.17 us -> none  [the longest x1 1.26 us: layer_in_planes(): qkv_cut = query_key_value_weight.reshape(e, 3, 2, 4, 2 * e)]
where the time goes in v5:
time: 353 us; the launch traced here: 352 us
  Pallas kernels  351 us (99%)
    pallas_call x2, Pallas kernels, fused(): pl.pallas_call(kernel, name=name, out_shape=[jax.ShapeDtypeStruct(s, d) f...  346 us

profile of v5, /device:TPU:0, one launch (start us, length us, event | category | flops | bytes accessed | tf_op | source)
XLA Modules:
  0.0 352.3 jit_solution(2989747014874594027)
XLA Ops:
  0.6 115.2 %first_half.1 = (bf16[2,64,1024]{2,1,0:T(8,128)(2,1)}, bf16[3,64,2048]{2,1,0:T(8,128)(2,1)}, f32[64,2048]{1,0:T(8,128)}, f32[1,2048]{1,0:T(1,128)}, f32[2,64,102...) custom-call(bf16[6,64]{1,0:T(8,128)(2,1)} %refs_0_.1, ...), custom_call_target="tpu_custom_call" | custom-call | tf_op jit(solution)/shard_map/first_half/pallas_call | solution.py:105
  115.9 231.0 %second_half.1 = (bf16[2,64,1024]{2,1,0:T(8,128)(2,1)}, f32[2,64,1024]{2,1,0:T(8,128)}, f32[512,1024]{1,0:T(8,128)}, bf16[2,128,1024]{2,1,0:T(8,128)(2,1)}, bf16...) custom-call(bf16[2,64,1024]{2,1,0:T(8,128)(2,1)} %get-tuple-element.45.refs_0_, ...), custom_call_target="tpu_custom_call" | custom-call | tf_op jit(solution)/shard_map/second_half/pallas_call | solution.py:105
  346.9 5.2 %finish.1 = (bf16[128,1024]{1,0:T(8,128)(2,1)}, f32[128,1024]{1,0:T(8,128)}, f32[512,1024]{1,0:T(8,128)}, f32[2,64]{1,0:T(2,128)}, f32[64,3072]{1,0:T(8,128)}, /...) custom-call(s32[1]{0:T(128)} %bitcast.odd, ...), custom_call_target="tpu_custom_call" | custom-call | tf_op jit(solution)/shard_map/finish/pallas_call | solution.py:1545

commit v6 on v5

--- a/solution.py
+++ b/solution.py
@@ -471,6 +471,48 @@
 )
 
 
+def line_gather_steps(src, spot, sem):
+    h, o, y, c = place()
+    at, seen = mirrored()
+    end, inner, other = (h, blk(seen(0), y, c)), (h, blk(seen(1), y, c)), (h, blk(seen(2), y, c))
+
+    def line(ref, z, index, device):
+        return remote(ref, spot(z), sem, index, device)
+
+    @pl.when(at == 0)
+    def _():
+        line(src, o, 0, inner).start()
+
+    @pl.when(at == 1)
+    def _():
+        line(src, o, 2, other).start()
+        line(src, o, 1, end).start()
+
+    spot(o)[...] = src[...]
+    for k, (z, to, device) in enumerate(((0, 3, other), (2, 4, end), (3, 5, end))):
+        yield
+
+        @pl.when(at == 1)
+        def _():
+            landed(spot(seen(z)), sem, (0, 2, 3)[k])
+            line(spot(seen(z)), seen(z), to, device).start()
+
+    yield
+
+    @pl.when(at == 0)
+    def _():
+        for z, index in ((1, 1), (2, 4), (3, 5)):
+            landed(spot(seen(z)), sem, index)
+        line(src, o, 0, inner).wait_send()
+
+    @pl.when(at == 1)
+    def _():
+        line(src, o, 1, end).wait_send()
+        line(src, o, 2, other).wait_send()
+        for z, to, device in ((0, 3, other), (2, 4, end), (3, 5, end)):
+            line(spot(seen(z)), seen(z), to, device).wait_send()
+
+
 def line_sum_steps(term_of, out, terms, ends, mids, last, sem):
     h, o, y, c = place()
     at, seen = mirrored()
@@ -557,11 +599,11 @@
     planes, four, e, fh = x.up_one.shape
     f = 2 * fh
     fcols = x.down_weight.shape[0] // 2
-    half, half_d = r // 2, d // 2
+    half_d = d // 2
     rows, q_rows = 8 * r, 4 * r
     three, he, length = x.held.shape
     n = length // 4
-    slots, chunks, lag, chunk_lag, scale = consts
+    slots, chunks, chunk_lag, scale = consts
     own_rows, w, blks = seqs * r, d // chunks, 16
     key_rows = 256
     width_qkv = 3 * 2 * he
@@ -581,7 +623,7 @@
     shapes = dict(
         partial=(plane, BF16),
         up_two=(x.up_one.shape, BF16),
-        down_two=(x.down_one.shape, BF16),
+        down_all=((planes, fcols, d), BF16),
         first_g=(plane, BF16),
         grad_g=(plane, BF16),
         branch_g=(plane, BF16),
@@ -625,8 +667,8 @@
     )
     ids = {name: scratch(*spec) for name, spec in shapes.items()}
     counts = dict(
-        up_sem=3,
-        down_sem=3,
+        up_sem=6,
+        down_sem=6,
         ksem=3,
         qsem=3,
         down_pair=1,
@@ -640,8 +682,7 @@
     for k, v in dict(go_send=4, go_recv=4, out_send=2, out_recv=4).items():
         sem_ids[k] = many([pltpu.SemaphoreType.DMA((v,))])[0]
     stream_ids = [
-        ([many(scatter_scratch(r, d)) for _ in range(3)], [many([sems(14)])[0] for _ in range(3)])
-        for _ in range(seqs)
+        ([many(scatter_scratch(2 * r, d)) for _ in range(3)], [many([sems(14)])[0] for _ in range(3)])
     ]
     chunk_ids = [
         (many(scatter_scratch(2 * r, w)), many([sems(6), sems(4), sems(8)])) for _ in range(chunks)
@@ -663,32 +704,30 @@
 
         up_more = src.up_cut.at[:, :, pl.ds(fh, fh)]
         down_rows = pl.ds(pl.multiple_of(h * fcols, fcols), fcols)
-        down_more = src.down_weight.at[down_rows, pl.ds(half_d, half_d)]
-        weights = []
-        for k, p in enumerate(COLUMN):
-            for ref, dst, s in (
-                (up_more, m.up_two, sem.up_sem),
-                (down_more, m.down_two, sem.down_sem),
-            ):
-                copy = remote(ref, dst.at[o], s, k, peer(*p))
-                copy.start()
-                weights.append(copy)
-        m.up_two[pl.ds(o, 1)] = up_more[...][None]
-        m.down_two[pl.ds(o, 1)] = down_more[...][None]
+        down_more = src.down_weight.at[down_rows]
+        up_line_in = line_gather_steps(up_more, lambda z: m.up_two.at[z], sem.up_sem)
+        down_line_in = line_gather_steps(down_more, lambda z: m.down_all.at[z], sem.down_sem)
+        next(up_line_in)
+        next(down_line_in)
         for ref in (m.sums, m.up_sums, m.up_spots, m.dq):
             ref[...] = jnp.zeros_like(ref)
         yield
 
         ups = [lambda k=k: src.up_one[...].reshape(d, fh) if k == 0 else m.up_two[...].reshape(d, fh) for k in range(2)]
-        downs = [lambda k=k: src.down_one[...].reshape(f, half_d) if k == 0 else m.down_two[...].reshape(f, half_d) for k in range(2)]
+        downs = [
+            lambda k=k: m.down_all[:, :, k * half_d : (k + 1) * half_d].reshape(f, half_d)
+            for k in range(2)
+        ]
         vec = lambda k: src.vectors[k + 2 : k + 3]
         partial, low, total = m.partial, m.low, m.total
 
-        def piece(ref, s):
-            return lambda i, slot: ref.at[s, slot, pl.ds(i * half, half)]
-
-        def plain(ref, s):
-            return lambda i: ref.at[s, pl.ds(i * half, half)]
+        both = range(seqs)
+
+        def piece(ref):
+            return lambda i, slot: ref.at[i, slot]
+
+        def plain(ref):
+            return lambda i: ref.at[i]
 
         def quarter(ref, s, q):
             return ref[s, 4 * q : 4 * q + 4].reshape(q_rows, d)
@@ -787,123 +826,126 @@
                 (h, z * 4 + g),
             )
 
-        def stream(s):
-            scatters = [pick_refs(i) for i in stream_ids[s][0]]
-            gathers = pick_refs(stream_ids[s][1])
-            at = lambda q: pl.ds(s * rows + q * q_rows, q_rows)
-            branch = dot_tn(
-                src.attended[:, :, s * n : (s + 1) * n].reshape(2 * he, n), src.out_own[...]
-            )
-            partial[s] = branch.astype(BF16).reshape(8, r, d)
-            yield from scatter_steps(piece(partial, s), plain(total, s), *scatters[0])
-            xh, scale_r = norm_parts(src.embedded[s] + (total[s] + vec(0)))
-            m.xh_one[s] = xh
-            m.scale_one[s] = scale_r
-            value = xh * vec(4) + vec(1)
-            m.first[s] = value
-            low[s] = value.astype(BF16)
-            yield from gather_steps(plain(low, s), piece(m.first_g, s), gathers[0])
-            if s == 0:
-                for copy in weights:
-                    copy.wait()
-            for q in range(2):
-                rows_in = quarter(m.first_g, s, q)
+        def stream():
+            scatters = [pick_refs(i) for i in stream_ids[0][0]]
+            gathers = pick_refs(stream_ids[0][1])
+            at = lambda s, q: pl.ds(s * rows + q * q_rows, q_rows)
+            for s in both:
+                branch = dot_tn(
+                    src.attended[:, :, s * n : (s + 1) * n].reshape(2 * he, n), src.out_own[...]
+                )
+                partial[s] = branch.astype(BF16).reshape(8, r, d)
+            for k, _ in enumerate(scatter_steps(piece(partial), plain(total), *scatters[0])):
+                if k > 0:
+                    step(up_line_in)
+                yield
+            for s in both:
+                xh, scale_r = norm_parts(src.embedded[s] + (total[s] + vec(0)))
+                m.xh_one[s] = xh
+                m.scale_one[s] = scale_r
+                value = xh * vec(4) + vec(1)
+                m.first[s] = value
+                low[s] = value.astype(BF16)
+            step(up_line_in, down_line_in)
+            for k, _ in enumerate(gather_steps(plain(low), piece(m.first_g), gathers[0])):
+                if k in (1, 3):
+                    step(down_line_in)
+                yield
+            for _ in up_line_in:
+                pass
+            for s in both:
+                for q in range(2):
+                    rows_in = quarter(m.first_g, s, q)
+                    for k in range(2):
+                        cols = slice(k * fh, (k + 1) * fh)
+                        inner = jnp.dot(rows_in, ups[k](), preferred_element_type=F32)
+                        inner = inner + src.up_bias[:, cols]
+                        phi = 0.5 + 0.5 * lax.erf(inner * (0.5**0.5))
+                        m.act[at(s, q), cols] = (inner * phi).astype(BF16)
+                        bell = jnp.exp(inner * inner * -0.5) * (1.0 / math.sqrt(2.0 * math.pi))
+                        m.slope[at(s, q), cols] = phi + inner * bell
+            for _ in down_line_in:
+                pass
+            for s in both:
                 for k in range(2):
-                    cols = slice(k * fh, (k + 1) * fh)
-                    inner = jnp.dot(rows_in, ups[k](), preferred_element_type=F32)
-                    inner = inner + src.up_bias[:, cols]
-                    phi = 0.5 + 0.5 * lax.erf(inner * (0.5**0.5))
-                    m.act[at(q), cols] = (inner * phi).astype(BF16)
-                    bell = jnp.exp(inner * inner * -0.5) * (1.0 / math.sqrt(2.0 * math.pi))
-                    m.slope[at(q), cols] = phi + inner * bell
-                    yield
-                for k in range(2):
-                    part = jnp.dot(m.act[at(q)], downs[k](), preferred_element_type=F32)
-                    partial[s, 4 * q : 4 * q + 4, :, k * half_d : (k + 1) * half_d] = part.astype(
-                        BF16
-                    ).reshape(4, r, half_d)
+                    part = jnp.dot(
+                        m.act[s * rows : (s + 1) * rows], downs[k](), preferred_element_type=F32
+                    )
+                    partial[s, :, :, k * half_d : (k + 1) * half_d] = part.astype(BF16).reshape(
+                        8, r, half_d
+                    )
+            yield from scatter_steps(piece(partial), plain(total), *scatters[1])
+            for s in both:
+                xh, scale_r = norm_parts(m.first[s] + (total[s] + vec(2)))
+                out_ref[s] = (xh * vec(5) + vec(3)).astype(BF16)
+                cot = src.cotangent[s].astype(F32)
+                note(5, cot * xh)
+                note(3, cot)
+                grad = norm_back(xh, scale_r, cot * vec(5))
+                m.grad_two[s] = grad
+                low[s] = grad.astype(BF16)
+                note(2, low[s].astype(F32))
+            yield from gather_steps(plain(low), piece(m.grad_g), gathers[1])
+            for s in both:
+                for q in range(2):
+                    rows_in = quarter(m.grad_g, s, q)
+                    back = dot_nt(rows_in[:, :half_d], downs[0]()) + dot_nt(
+                        rows_in[:, half_d:], downs[1]()
+                    )
+                    back = (back * m.slope[at(s, q)]).astype(BF16)
+                    m.inner_grad[at(s, q)] = back
+                    m.up_sums[...] += jnp.sum(back.astype(F32), axis=0, keepdims=True)
+                    part = dot_nt(back[:, :fh], ups[0]()) + dot_nt(back[:, fh:], ups[1]())
+                    partial[s, 4 * q : 4 * q + 4] = part.astype(BF16).reshape(4, r, d)
+            last = scatter_steps(piece(partial), plain(total), *scatters[2])
+            next(last)
+
+            @pl.loop(0, planes)
+            def _(z):
+                cols = pl.ds(pl.multiple_of(z * fcols, fcols), fcols)
+                all_grads = m.grad_g[...].reshape(seqs * rows, d)
+                m.down_part[z] = dot_tn(m.act[:, cols], all_grads).astype(BF16)
+
+            step(down)
+            next(last)
+
+            @pl.loop(0, planes)
+            def _(z):
+                cols = pl.ds(pl.multiple_of(z * 4 * e, 4 * e), 4 * e)
+                all_first = m.first_g[:, :, :, cols].reshape(seqs * rows, 4 * e)
+                m.up_part[z] = dot_tn(all_first, m.inner_grad[...]).astype(BF16)
+
+            yield from last
+            for s in both:
+                grad = m.grad_two[s] + total[s]
+                note(4, grad * m.xh_one[s])
+                note(1, grad)
+                grad = norm_back(m.xh_one[s], m.scale_one[s], grad * vec(4))
+                m.resid[s] = grad
+                low[s] = grad.astype(BF16)
+                note(0, low[s].astype(F32))
+            for k, _ in enumerate(gather_steps(plain(low), piece(m.branch_g), gathers[2])):
                 yield
-            yield from scatter_steps(piece(partial, s), plain(total, s), *scatters[1])
-            xh, scale_r = norm_parts(m.first[s] + (total[s] + vec(2)))
-            out_ref[s] = (xh * vec(5) + vec(3)).astype(BF16)
-            cot = src.cotangent[s].astype(F32)
-            note(5, cot * xh)
-            note(3, cot)
-            grad = norm_back(xh, scale_r, cot * vec(5))
-            m.grad_two[s] = grad
-            low[s] = grad.astype(BF16)
-            note(2, low[s].astype(F32))
-            yield from gather_steps(plain(low, s), piece(m.grad_g, s), gathers[1])
-            for q in range(2):
-                rows_in = quarter(m.grad_g, s, q)
-                back = dot_nt(rows_in[:, :half_d], downs[0]()) + dot_nt(
-                    rows_in[:, half_d:], downs[1]()
-                )
-                back = (back * m.slope[at(q)]).astype(BF16)
-                m.inner_grad[at(q)] = back
-                m.up_sums[...] += jnp.sum(back.astype(F32), axis=0, keepdims=True)
-                yield
-                part = dot_nt(back[:, :fh], ups[0]()) + dot_nt(back[:, fh:], ups[1]())
-                partial[s, 4 * q : 4 * q + 4] = part.astype(BF16).reshape(4, r, d)
-                yield
-            last = scatter_steps(piece(partial, s), plain(total, s), *scatters[2])
-            next(last)
-            if s == seqs - 1:
-                @pl.loop(0, planes)
-                def _(z):
-                    cols = pl.ds(pl.multiple_of(z * fcols, fcols), fcols)
-                    all_grads = m.grad_g[...].reshape(seqs * rows, d)
-                    m.down_part[z] = dot_tn(m.act[:, cols], all_grads).astype(BF16)
-
-                step(down)
-                yield
-
-                @pl.loop(0, planes)
-                def _(z):
-                    cols = pl.ds(pl.multiple_of(z * 4 * e, 4 * e), 4 * e)
-                    all_first = m.first_g[:, :, :, cols].reshape(seqs * rows, 4 * e)
-                    m.up_part[z] = dot_tn(all_first, m.inner_grad[...]).astype(BF16)
-
-                yield
-            yield from last
-            grad = m.grad_two[s] + total[s]
-            note(4, grad * m.xh_one[s])
-            note(1, grad)
-            grad = norm_back(m.xh_one[s], m.scale_one[s], grad * vec(4))
-            m.resid[s] = grad
-            low[s] = grad.astype(BF16)
-            note(0, low[s].astype(F32))
-            for k, _ in enumerate(gather_steps(plain(low, s), piece(m.branch_g, s), gathers[2])):
-                yield
-                if s == seqs - 1 and k in EARLY:
+                if k in EARLY:
                     step(down)
-            go = dot_nt(src.out_own[...], m.branch_g[s].reshape(rows, d))
-            m.go[:, :, s * n : (s + 1) * n] = go.astype(BF16).reshape(2, he, n)
-            for j in range(2):
-
-                @pl.when(o != 2 * s + j)
-                def _():
-                    go_copy(s, j).start()
-
-                @pl.when(o == 2 * s + j)
-                def _():
-                    m.gs[:, pl.ds(pl.multiple_of(o * n, n), n)] = m.go[
-                        j, :, s * n : (s + 1) * n
-                    ]
-
-            yield
+            for s in both:
+                go = dot_nt(src.out_own[...], m.branch_g[s].reshape(rows, d))
+                m.go[:, :, s * n : (s + 1) * n] = go.astype(BF16).reshape(2, he, n)
+                for j in range(2):
+
+                    @pl.when(o != 2 * s + j)
+                    def _():
+                        go_copy(s, j).start()
+
+                    @pl.when(o == 2 * s + j)
+                    def _():
+                        m.gs[:, pl.ds(pl.multiple_of(o * n, n), n)] = m.go[
+                            j, :, s * n : (s + 1) * n
+                        ]
 
         down, up, out, qkv = down_sums(), up_sums(), out_sums(), qkv_sums()
-        gens = [stream(s) for s in range(seqs)]
-        for _ in range(lag):
-            next(gens[0])
-        while gens:
-            for gen in list(gens):
-                try:
-                    next(gen)
-                except StopIteration:
-                    gens.remove(gen)
-
+        for _ in stream():
+            pass
         step(up)
         grad_out = jnp.dot(
             src.attended[...].reshape(2 * he, 2 * n),
@@ -1192,11 +1234,10 @@
     slots = x.table.shape[0]
     e = x.qkv_weight.shape[0]
     four, wq, f = 4, x.qkv_weight.shape[1] // 8, x.up_weight.shape[1] // 8
-    fcols = x.down_weight.shape[0] // 2
     he = wq // 6
     n = 8 * r
     length = 4 * n
-    half, fh, half_d = r // 2, f // 2, d // 2
+    half, fh = r // 2, f // 2
     blks = 16
     cols = 256
     small = small_gather(jax.ShapeDtypeStruct((8, 128), F32))
@@ -1221,7 +1262,7 @@
         pair_low=((he, length), BF16),
     )
     ids = {k: many([pltpu.VMEM(*v)])[0] for k, v in shapes.items()}
-    counts = dict(qkv_sem=3, up_sem=3, down_sem=3, back_sem=3, qkv_trade=9, up_trade=12)
+    counts = dict(qkv_sem=3, up_sem=3, back_sem=3, qkv_trade=9, up_trade=12)
     sem_ids = {k: many([sems(v)])[0] for k, v in counts.items()}
     for k in ("send", "recv"):
         sem_ids[k] = many([pltpu.SemaphoreType.DMA((4,))])[0]
@@ -1248,7 +1289,7 @@
     def run(ins, outs, own):
         src = SimpleNamespace(**dict(zip(names, ins)))
         attended, held, o_ref, lse_ref, emb_ref, plane_ref, qkv_ref = outs[:7]
-        outw_ref, up_one, up_in, down_one, vec_ref, bias_ref, ids_ref, second_ref = outs[7:]
+        outw_ref, up_one, up_in, vec_ref, bias_ref, ids_ref, second_ref = outs[7:]
         m = SimpleNamespace(**{k: own[v] for k, v in ids.items()})
         sem = SimpleNamespace(**{k: own[v] for k, v in sem_ids.items()})
         pick_refs = lambda some: [own[i] for i in some]
@@ -1290,6 +1331,7 @@
         trade(src.qkv_weight, m.qkv_in, sem.qkv_trade, qkv_lanes)
         next(gather_small)
         yield
+        next(weights)
         trade(src.up_weight, up_in, sem.up_trade, up_lanes)
         bulk = []
 
@@ -1378,6 +1420,8 @@
             yield from rows_steps(
                 lambda z, yy: m.found.at[z, yy, c, s], *streams[s], m.rows.at[s]
             )
+            if s == seqs - 1:
+                line(up_in.at[:, :, pl.ds(0, fh)], up_one, sem.up_sem)
             second = second_ref[s * r : (s + 1) * r]
             typed = vec_ref[8:9] * (1.0 - second) + vec_ref[9:10] * second
             value = src.hidden[s].astype(F32) + m.rows[s] + typed
@@ -1389,10 +1433,9 @@
                 own[gather_ids[s]],
             )
             if s == 0:
-                for copy in bulk:
+                for copy in bulk[:3]:
                     copy.wait()
-                bulk.clear()
-                line(up_in.at[:, :, pl.ds(0, fh)], up_one, sem.up_sem)
+                del bulk[:3]
             part = lax.dot_general(
                 qkv_ref[...].reshape(d, wq),
                 plane_ref[s].reshape(n, d),
@@ -1427,7 +1470,6 @@
                     next(gen)
                 except StopIteration:
                     gens.remove(gen)
-        next(weights)
         for z in range(4):
 
             @pl.when(z != o)
@@ -1435,8 +1477,6 @@
                 ref = held.at[:, :, pl.ds(z * n, n)]
                 place_copy(ref, ref, sem.send.at[0], sem.recv.at[z], peer(*NEAR_X)).wait_recv()
 
-        down_rows = pl.ds(pl.multiple_of(h * fcols, fcols), fcols)
-        line(src.down_weight.at[down_rows, pl.ds(0, half_d)], down_one, sem.down_sem)
         m.keys[...] = held[1].astype(F32).T.astype(BF16)
         mine = pl.ds(pl.multiple_of((o // 2) * n, n), n)
 
@@ -1500,7 +1540,6 @@
             ((2,) + x.out_weight.shape, BF16),
             ((4, four, e, fh), BF16),
             ((four, e, f), BF16),
-            ((4, fcols, half_d), BF16),
             ((10, d), F32),
             ((1, f), F32),
             ((1, blks * seqs * r), jnp.int32),
@@ -2045,7 +2084,6 @@
         qkv_weight=query_key_value_weight,
         out_weight=attention_output_weight,
         up_weight=up_projection_weight,
-        down_weight=down_projection_weight,
         table=pos_table,
         hidden=hidden,
     )
@@ -2061,7 +2099,6 @@
             out_own,
             up_one,
             up_cut,
-            down_one,
             vectors,
             up_bias,
             pos_all,
@@ -2075,7 +2112,6 @@
         cotangent=cotangent,
         up_one=up_one,
         up_cut=up_cut,
-        down_one=down_one,
         down_weight=down_projection_weight,
         up_bias=up_bias,
         vectors=vectors,
@@ -2087,7 +2123,7 @@
         ids=pos_all,
         second=is_second,
     )
-    sizes = (slots, CHUNKS, LAG, CHUNK_LAG, scale)
+    sizes = (slots, CHUNKS, CHUNK_LAG, scale)
     ((layer_out, grad_hidden, pos, down, up, qkv, out, totals),) = fused(
         "second_half", 4, [second_half(parts, sizes)], WHOLE
     )

time: 353 us -> 338 us (0.958)
  Pallas kernels: 351 us -> 336 us
    pallas_call x2, Pallas kernels: 346 us -> 331 us  [fused(): pl.pallas_call(kernel, name=name, out_shape=[jax.ShapeDtypeStruct(s, d) f...]
where the time goes in v6:
time: 338 us; the launch traced here: 337 us
  Pallas kernels  336 us (99%)
    pallas_call x2, Pallas kernels, fused(): pl.pallas_call(kernel, name=name, out_shape=[jax.ShapeDtypeStruct(s, d) f...  331 us

profile of v6, /device:TPU:0, one launch (start us, length us, event | category | flops | bytes accessed | tf_op | source)
XLA Modules:
  0.0 337.3 jit_solution(14735871997770196662)
XLA Ops:
  0.6 103.4 %first_half.1 = (bf16[2,64,1024]{2,1,0:T(8,128)(2,1)}, bf16[3,64,2048]{2,1,0:T(8,128)(2,1)}, f32[64,2048]{1,0:T(8,128)}, f32[1,2048]{1,0:T(1,128)}, f32[2,64,102...) custom-call(bf16[6,64]{1,0:T(8,128)(2,1)} %refs_0_.1, ...), custom_call_target="tpu_custom_call" | custom-call | tf_op jit(solution)/shard_map/first_half/pallas_call | solution.py:105
  104.0 227.9 %second_half.1 = (bf16[2,64,1024]{2,1,0:T(8,128)(2,1)}, f32[2,64,1024]{2,1,0:T(8,128)}, f32[512,1024]{1,0:T(8,128)}, bf16[2,128,1024]{2,1,0:T(8,128)(2,1)}, bf16...) custom-call(bf16[2,64,1024]{2,1,0:T(8,128)(2,1)} %get-tuple-element.44.refs_0_, ...), custom_call_target="tpu_custom_call" | custom-call | tf_op jit(solution)/shard_map/second_half/pallas_call | solution.py:105
  331.9 5.2 %finish.1 = (bf16[128,1024]{1,0:T(8,128)(2,1)}, f32[128,1024]{1,0:T(8,128)}, f32[512,1024]{1,0:T(8,128)}, f32[2,64]{1,0:T(2,128)}, f32[64,3072]{1,0:T(8,128)}, /...) custom-call(s32[1]{0:T(128)} %bitcast.odd, ...), custom_call_target="tpu_custom_call" | custom-call | tf_op jit(solution)/shard_map/finish/pallas_call | solution.py:1584

commit v7 on v6

--- a/solution.py
+++ b/solution.py
@@ -1262,7 +1262,7 @@
         pair_low=((he, length), BF16),
     )
     ids = {k: many([pltpu.VMEM(*v)])[0] for k, v in shapes.items()}
-    counts = dict(qkv_sem=3, up_sem=3, back_sem=3, qkv_trade=9, up_trade=12)
+    counts = dict(qkv_sem=6, up_sem=6, back_sem=3, qkv_trade=9, up_trade=12)
     sem_ids = {k: many([sems(v)])[0] for k, v in counts.items()}
     for k in ("send", "recv"):
         sem_ids[k] = many([pltpu.SemaphoreType.DMA((4,))])[0]
@@ -1333,14 +1333,9 @@
         yield
         next(weights)
         trade(src.up_weight, up_in, sem.up_trade, up_lanes)
-        bulk = []
-
-        def line(ref, dst, s):
-            for k, p in enumerate(COLUMN):
-                copy = remote(ref, dst.at[o], s, k, peer(*p))
-                copy.start()
-                bulk.append(copy)
-            dst[pl.ds(o, 1)] = ref[...][None]
+        qkv_line = line_gather_steps(m.qkv_in, lambda z: qkv_ref.at[z], sem.qkv_sem)
+        up_first = up_in.at[:, :, pl.ds(0, fh)]
+        up_line = line_gather_steps(up_first, lambda z: up_one.at[z], sem.up_sem)
 
         for _ in gather_small:
             pass
@@ -1377,7 +1372,7 @@
             if i == 0:
                 for copy in trades:
                     copy.wait()
-                line(m.qkv_in, qkv_ref, sem.qkv_sem)
+                next(qkv_line)
 
         lane = lax.broadcasted_iota(jnp.int32, (1, 128), 1)
         for k in range(5):
@@ -1421,7 +1416,7 @@
                 lambda z, yy: m.found.at[z, yy, c, s], *streams[s], m.rows.at[s]
             )
             if s == seqs - 1:
-                line(up_in.at[:, :, pl.ds(0, fh)], up_one, sem.up_sem)
+                next(up_line)
             second = second_ref[s * r : (s + 1) * r]
             typed = vec_ref[8:9] * (1.0 - second) + vec_ref[9:10] * second
             value = src.hidden[s].astype(F32) + m.rows[s] + typed
@@ -1433,9 +1428,8 @@
                 own[gather_ids[s]],
             )
             if s == 0:
-                for copy in bulk[:3]:
-                    copy.wait()
-                del bulk[:3]
+                for _ in qkv_line:
+                    pass
             part = lax.dot_general(
                 qkv_ref[...].reshape(d, wq),
                 plane_ref[s].reshape(n, d),
@@ -1464,12 +1458,19 @@
         gens = [stream(s) for s in range(seqs)]
         for _ in range(lag):
             next(gens[0])
+        turn = 0
         while gens:
             for gen in list(gens):
                 try:
                     next(gen)
                 except StopIteration:
                     gens.remove(gen)
+            if turn in QKV_TURNS:
+                next(qkv_line, None)
+            if turn in UP_TURNS:
+                next(up_line, None)
+            turn += 1
+
         for z in range(4):
 
             @pl.when(z != o)
@@ -1515,8 +1516,8 @@
             landed(attended.at[z % 2, :, pl.ds(pl.multiple_of((z // 2) * n, n), n)], sem.back_sem, i)
         for _ in weights:
             pass
-        for copy in bulk:
-            copy.wait()
+        for _ in up_line:
+            pass
         for copy in core:
             copy.wait_send()
         for s in range(seqs):
@@ -2046,8 +2047,10 @@
 LAG = 1
 CHUNKS = 4
 CHUNK_LAG = 1
+QKV_TURNS = (1, 3, 5)
+UP_TURNS = (8, 9, 10)
 EARLY = (1, 3)
-TURNS = ((1, 3), (2, 4, 6, 8), (6, 12))
+TURNS = ((1, 3), (3, 5, 8, 11), (10, 14))
 
 
 def layer_in_planes(

time: 338 us -> 318 us (0.941)
  Pallas kernels: 336 us -> 317 us
    pallas_call x2, Pallas kernels: 331 us -> 312 us  [fused(): pl.pallas_call(kernel, name=name, out_shape=[jax.ShapeDtypeStruct(s, d) f...]
where the time goes in v7:
time: 318 us
  Pallas kernels  317 us (100%)
    pallas_call x2, Pallas kernels, fused(): pl.pallas_call(kernel, name=name, out_shape=[jax.ShapeDtypeStruct(s, d) f...  312 us

profile of v7, /device:TPU:0, one launch (start us, length us, event | category | flops | bytes accessed | tf_op | source)
XLA Modules:
  0.0 317.6 jit_solution(16225477097829823166)
XLA Ops:
  0.6 101.1 %first_half.1 = (bf16[2,64,1024]{2,1,0:T(8,128)(2,1)}, bf16[3,64,2048]{2,1,0:T(8,128)(2,1)}, f32[64,2048]{1,0:T(8,128)}, f32[1,2048]{1,0:T(1,128)}, f32[2,64,102...) custom-call(bf16[6,64]{1,0:T(8,128)(2,1)} %refs_0_.1, ...), custom_call_target="tpu_custom_call" | custom-call | tf_op jit(solution)/shard_map/first_half/pallas_call | solution.py:105
  101.7 210.4 %second_half.1 = (bf16[2,64,1024]{2,1,0:T(8,128)(2,1)}, f32[2,64,1024]{2,1,0:T(8,128)}, f32[512,1024]{1,0:T(8,128)}, bf16[2,128,1024]{2,1,0:T(8,128)(2,1)}, bf16...) custom-call(bf16[2,64,1024]{2,1,0:T(8,128)(2,1)} %get-tuple-element.44.refs_0_, ...), custom_call_target="tpu_custom_call" | custom-call | tf_op jit(solution)/shard_map/second_half/pallas_call | solution.py:105
  312.2 5.2 %finish.1 = (bf16[128,1024]{1,0:T(8,128)(2,1)}, f32[128,1024]{1,0:T(8,128)}, f32[512,1024]{1,0:T(8,128)}, f32[2,64]{1,0:T(2,128)}, f32[64,3072]{1,0:T(8,128)}, /...) custom-call(s32[1]{0:T(128)} %bitcast.odd, ...), custom_call_target="tpu_custom_call" | custom-call | tf_op jit(solution)/shard_map/finish/pallas_call | solution.py:1585

commit v8 on v7

--- a/solution.py
+++ b/solution.py
@@ -1239,7 +1239,7 @@
     length = 4 * n
     half, fh = r // 2, f // 2
     blks = 16
-    cols = 256
+    cols = 512
     small = small_gather(jax.ShapeDtypeStruct((8, 128), F32))
     outw = out_weights(x.out_weight)
     need = []

time: 318 us -> 317 us (level)
  no operation moved by 1% of the time
where the time goes in v8:
time: 317 us
  Pallas kernels  316 us (100%)
    pallas_call x2, Pallas kernels, fused(): pl.pallas_call(kernel, name=name, out_shape=[jax.ShapeDtypeStruct(s, d) f...  311 us

profile of v8, /device:TPU:0, one launch (start us, length us, event | category | flops | bytes accessed | tf_op | source)
XLA Modules:
  0.0 317.0 jit_solution(12977954549125102987)
XLA Ops:
  0.6 101.3 %first_half.1 = (bf16[2,64,1024]{2,1,0:T(8,128)(2,1)}, bf16[3,64,2048]{2,1,0:T(8,128)(2,1)}, f32[64,2048]{1,0:T(8,128)}, f32[1,2048]{1,0:T(1,128)}, f32[2,64,102...) custom-call(bf16[6,64]{1,0:T(8,128)(2,1)} %refs_0_.1, ...), custom_call_target="tpu_custom_call" | custom-call | tf_op jit(solution)/shard_map/first_half/pallas_call | solution.py:105
  102.0 209.6 %second_half.1 = (bf16[2,64,1024]{2,1,0:T(8,128)(2,1)}, f32[2,64,1024]{2,1,0:T(8,128)}, f32[512,1024]{1,0:T(8,128)}, bf16[2,128,1024]{2,1,0:T(8,128)(2,1)}, bf16...) custom-call(bf16[2,64,1024]{2,1,0:T(8,128)(2,1)} %get-tuple-element.44.refs_0_, ...), custom_call_target="tpu_custom_call" | custom-call | tf_op jit(solution)/shard_map/second_half/pallas_call | solution.py:105
  311.6 5.2 %finish.1 = (bf16[128,1024]{1,0:T(8,128)(2,1)}, f32[128,1024]{1,0:T(8,128)}, f32[512,1024]{1,0:T(8,128)}, f32[2,64]{1,0:T(2,128)}, f32[64,3072]{1,0:T(8,128)}, /...) custom-call(s32[1]{0:T(128)} %bitcast.odd, ...), custom_call_target="tpu_custom_call" | custom-call | tf_op jit(solution)/shard_map/finish/pallas_call | solution.py:1585
